TPU v7x, 32 devices: a whole 2x2x4 slice. The times are simulated.
32 devices in a mesh: row: 8 (over z, y), col: 4 (over x, core).
Axes of the slice: x: 2, y: 2, z: 4, core: 2. Of those that a mesh axis runs over, the one named last changes fastest.
Arguments:
- right_side: float32 [3, 64, 512], P(None, 'row', 'col'), may hold values from -6 to 6
- viscosity: float32 [64, 512], P('row', 'col'), may hold values from 0.1 to 3
- free_mask: int32 [3, 64, 512], P(None, 'row', 'col'), may hold values 0 or 1
- coarse_basis: float32 [64, 3, 64, 512], P(None, None, 'row', 'col'), may hold values from -6 to 6
- gram_inverse: float32 [64, 64], P('col'), may hold values from -3 to 6, as said below
Outputs:
- solution: float32 [3, 64, 512], P(None, 'row', 'col')
- residual: float32 [3, 64, 512], P(None, 'row', 'col')
Inputs may be any that keep to these rules, and one draw needn't show every extreme that they name: `free_mask`: 1 marks a free velocity unknown, 0 one whose value is prescribed. `gram_inverse`: symmetric positive definite.
All inputs are finite; a program needn't handle non-finite values. No bound on the sum of `free_mask` on one device may be relied on, other than what follows from the above.
Results may differ from a plain program's by a relative error of at most 0.0003.
Values sent between devices are 32-bit elements; how exact they have to be, the bound alone decides.
No kernel may reach another device: no remote copies, remote signals or barrier semaphores. Data moves between devices by JAX's collectives and lax.ppermute only.
A program may use at most 64 MiB of HBM per device.

v0:
```python
import math

import jax
import jax.numpy as jnp
from jax import lax
from jax.sharding import PartitionSpec as P

ITERS = 2


def padded_2(shard, sides, width):
    for axis, dim in sides:
        count, length = (lax.axis_size(axis), shard.shape[dim])
        up = [(i, (i + 1) % count) for i in range(count - 1)]
        down = [(j, i) for i, j in up]
        last = lax.slice_in_dim(shard, length - width, length, axis=dim)
        leading = lax.slice_in_dim(shard, 0, width, axis=dim)
        before = lax.ppermute(last, axis, up)
        after = lax.ppermute(leading, axis, down)
        shard = jnp.concatenate([before, shard, after], axis=dim)
    return shard


def on_device(right_side, viscosity, free_mask, coarse_basis, gram_inverse):
    high = lax.Precision.HIGHEST
    components, patch_rows, patch_cols = right_side.shape
    columns = coarse_basis.shape[0]
    unknowns = (
        components * patch_rows * patch_cols * lax.axis_size("row") * lax.axis_size("col") * columns
    )
    coarse_scale = 1.0 / (32.0 * math.sqrt(float(unknowns)))
    viscosity_pad = padded_2(viscosity, (("row", 0), ("col", 1)), 1)
    face_north = 0.5 * (viscosity + viscosity_pad[2:, 1:-1])
    face_south = 0.5 * (viscosity + viscosity_pad[:-2, 1:-1])
    face_east = 0.5 * (viscosity + viscosity_pad[1:-1, 2:])
    face_west = 0.5 * (viscosity + viscosity_pad[1:-1, :-2])
    diagonal = 1.0 + face_north + face_south + face_east + face_west
    unfixed = free_mask.astype(jnp.float32)
    jacobi = unfixed / diagonal + (1.0 - unfixed)
    basis_rows = coarse_basis.reshape(columns, -1)

    def solve_coarse(coarse_dot):
        coeff_part = jnp.dot(gram_inverse, coarse_dot, precision=high) * coarse_scale
        return lax.all_gather(coeff_part, "col", axis=0, tiled=True)

    def precondition(residual, coarse_dot, weighted_sq):
        coeffs = solve_coarse(coarse_dot)
        smoothed = jacobi * residual + jnp.dot(coeffs, basis_rows, precision=high).reshape(
            residual.shape
        )
        return (smoothed, weighted_sq + jnp.dot(coarse_dot, coeffs, precision=high))

    solution = jnp.zeros_like(right_side)
    residual = right_side
    coarse_dot, weighted_sq = lax.psum(
        (
            jnp.dot(basis_rows, residual.reshape(-1), precision=high),
            jnp.sum(jacobi * residual * residual),
        ),
        ("row", "col"),
    )
    direction, energy = precondition(residual, coarse_dot, weighted_sq)
    for iteration in range(ITERS):
        masked = unfixed * direction
        padded = padded_2(masked, (("row", 1), ("col", 2)), 1)
        stencil = diagonal * masked - (
            face_north * padded[:, 2:, 1:-1]
            + face_south * padded[:, :-2, 1:-1]
            + face_east * padded[:, 1:-1, 2:]
            + face_west * padded[:, 1:-1, :-2]
        )
        applied = unfixed * stencil + (1.0 - unfixed) * direction
        if iteration + 1 < ITERS:
            curve_sum, image_coarse, cross_term, image_sq = lax.psum(
                (
                    jnp.sum(direction * applied),
                    jnp.dot(basis_rows, applied.reshape(-1), precision=high),
                    jnp.sum(jacobi * residual * applied),
                    jnp.sum(jacobi * applied * applied),
                ),
                ("row", "col"),
            )
            step_len = energy / curve_sum
            solution = step_len * direction
            residual = residual - step_len * applied
            coarse_dot = coarse_dot - step_len * image_coarse
            weighted_sq = weighted_sq - 2.0 * step_len * cross_term + step_len * step_len * image_sq
            smoothed, energy_new = precondition(residual, coarse_dot, weighted_sq)
            direction = smoothed + energy_new / energy * direction
            energy = energy_new
        else:
            curve_sum = lax.psum(jnp.sum(direction * applied), ("row", "col"))
            step_len = energy / curve_sum
            solution = solution + step_len * direction
            residual = residual - step_len * applied
    return (solution, residual)


def solution(mesh):
    in_specs = (
        P(None, "row", "col"),
        P("row", "col"),
        P(None, "row", "col"),
        P(None, None, "row", "col"),
        P("col", None),
    )
    out_specs = (P(None, "row", "col"), P(None, "row", "col"))
    return jax.shard_map(
        on_device, mesh=mesh, in_specs=in_specs, out_specs=out_specs, check_vma=False
    )
```

profile of v0, /device:TPU:0, one launch (start us, length us, event | category | flops | bytes accessed | tf_op | source)
XLA Modules:
  0.0 198.3 jit_solution(4688476039508117926)
XLA Ops:
  0.6 0.8 fusion.55
  1.4 1.3 collective-permute-start
  2.7 5.5 %collective-permute-start.1 = (f32[1,128]{1,0:T(1,128)S(1)}, f32[1,128]{1,0:T(1,128)S(1)}, u32[]{:S(2)}, u32[]{:S(2)}) collective-permute-start(f32[1,128]{1,0:T(1,128)S(1)} %get-tuple-element.33), channel_id=1, source_target_pairs={{0,4},{4,8},{8,12},{12,16},{16,20},{20,24},{24,28},{1,5},{5,9},{9,... | collective-permute-start | bytes 1544 | tf_op jit(solution)/shard_map/ppermute | solution.py:18
  8.2 1.3 copy.32
  9.7 1.0 copy-done.1
  10.7 0.7 convolution_bitcast_fusion.3
  11.4 41.9 %psum.50 = f32[64]{0:T(128)S(1)} all-reduce(f32[64]{0:T(128)S(1)} %convolution_bitcast_fusion.3), channel_id=1, replica_groups=mesh['row'=8,'col'=4] {'row','col'}, use_global_device_ids=true, to_apply=%region_2.0 | all-reduce | flops 64 | bytes 512 | tf_op jit(solution)/shard_map/psum | solution.py:55
  53.4 0.7 copy-done.5
  55.5 5.8 %all-reduce = f32[64]{0:T(128)S(1)} all-reduce(f32[64]{0:T(128)S(1)} %dynamic-update-slice), channel_id=1, replica_groups=mesh['row'=8,'col'=4] {'col'}, use_global_device_ids=true, to_apply=%add | all-reduce | flops 64 | bytes 512
  62.1 1.3 collective-permute-start.2
  63.4 3.0 %collective-permute-start.3 = (f32[10,1]{1,0:T(8,128)S(1)}, f32[10,1]{1,0:T(8,128)S(1)}, u32[]{:S(2)}, u32[]{:S(2)}) collective-permute-start(f32[10,1]{1,0:T(8,128)S(1)} %get-tuple-element.31), channel_id=1, source_target_pairs={{0,1},{1,2},{2,3},{4,5},{5,6},{6,7},{8,9},{9,10},{10,11},{12,13},{... | collective-permute-start | bytes 128 | tf_op jit(solution)/shard_map/ppermute | solution.py:18
  66.5 0.8 collective-permute-done.3
  67.4 1.3 collective-permute-start.4
  68.7 4.8 %collective-permute-start.5 = (f32[3,1,128]{2,1,0:T(1,128)S(1)}, f32[3,1,128]{2,1,0:T(1,128)S(1)}, u32[]{:S(2)}, u32[]{:S(2)}) collective-permute-start(f32[3,1,128]{2,1,0:T(1,128)S(1)} %get-tuple-element.29), channel_id=1, source_target_pairs={{0,4},{4,8},{8,12},{12,16},{16,20},{20,24},{24,28},{1,5},{5,9},{9,... | collective-permute-start | bytes 4616 | tf_op jit(solution)/shard_map/ppermute | solution.py:18
  73.5 1.3 collective-permute-done.5
  74.9 2.3 %collective-permute-start.7 = (f32[3,10,1]{2,1,0:T(8,128)S(1)}, f32[3,10,1]{2,1,0:T(8,128)S(1)}, u32[]{:S(2)}, u32[]{:S(2)}) collective-permute-start(f32[3,10,1]{2,1,0:T(8,128)S(1)} %get-tuple-element.26), channel_id=1, source_target_pairs={{0,1},{1,2},{2,3},{4,5},{5,6},{6,7},{8,9},{9,10},{10,11},{12,13},{... | collective-permute-start | bytes 368 | tf_op jit(solution)/shard_map/ppermute | solution.py:18
  77.2 1.3 collective-permute-start.6
  78.5 0.7 multiply_reduce_fusion.5
  79.1 4.0 %collective-permute-done.6 = f32[3,10,1]{2,1,0:T(8,128)S(1)} collective-permute-done((f32[3,10,1]{2,1,0:T(8,128)S(1)}, f32[3,10,1]{2,1,0:T(8,128)S(1)}, u32[]{:S(2)}, u32[]{:S(2)}) %collective-permute-start.6) | collective-permute-done | bytes 152 | tf_op jit(solution)/shard_map/ppermute | solution.py:19
  83.2 0.7 fusion.8
  83.9 0.7 convolution_bitcast_fusion.1
  84.6 42.6 %all-reduce.2 = (f32[64]{0:T(128)S(1)}, f32[]{:T(128)}, f32[]{:T(128)}, f32[]{:T(128)}, f32[]{:T(128)}) all-reduce(f32[64]{0:T(128)S(1)} %convolution_bitcast_fusion.1, f32[]{:T(128)} %get-tuple-element.4, f32[]{:T(128)} %get-tuple-element.5, f32[]{:T(128)} %get-tuple-element.3, ...), channel_id=1, replica_groups=mesh['row'=8,'col'=4] {'row','col'}, use_global_device_ids=true, to_apply=%region_9.0 | all-reduce | flops 68 | bytes 544 | tf_op jit(solution)/shard_map/psum | solution.py:74
  129.5 7.6 %all-reduce.1 = f32[64]{0:T(128)S(1)} all-reduce(f32[64]{0:T(128)S(1)} %dynamic-update-slice.1), channel_id=1, replica_groups=mesh['row'=8,'col'=4] {'col'}, use_global_device_ids=true, to_apply=%add.1 | all-reduce | flops 64 | bytes 512
  140.8 1.3 collective-permute-start.8
  142.1 4.5 %collective-permute-start.9 = (f32[3,1,128]{2,1,0:T(1,128)S(1)}, f32[3,1,128]{2,1,0:T(1,128)S(1)}, u32[]{:S(2)}, u32[]{:S(2)}) collective-permute-start(f32[3,1,128]{2,1,0:T(1,128)S(1)} %get-tuple-element.27), channel_id=1, source_target_pairs={{0,4},{4,8},{8,12},{12,16},{16,20},{20,24},{24,28},{1,5},{5,9},{9,... | collective-permute-start | bytes 4616 | tf_op jit(solution)/shard_map/ppermute | solution.py:18
  146.7 1.3 collective-permute-done.9
  148.0 1.3 collective-permute-start.11
  149.3 1.3 collective-permute-start.10
  150.6 2.6 %collective-permute-done.10 = f32[3,10,1]{2,1,0:T(8,128)S(1)} collective-permute-done((f32[3,10,1]{2,1,0:T(8,128)S(1)}, f32[3,10,1]{2,1,0:T(8,128)S(1)}, u32[]{:S(2)}, u32[]{:S(2)}) %collective-permute-start.10) | collective-permute-done | bytes 152 | tf_op jit(solution)/shard_map/ppermute | solution.py:19
  153.3 0.7 multiply_reduce_fusion
  154.0 43.0 %psum.55 = f32[]{:T(128)} all-reduce(f32[]{:T(128)} %get-tuple-element.11), channel_id=1, replica_groups=mesh['row'=8,'col'=4] {'row','col'}, use_global_device_ids=true, to_apply=%region_11.0 | all-reduce | flops 1 | bytes 8 | tf_op jit(solution)/shard_map/psum | solution.py:92
  197.7 0.6 multiply_subtract_fusion
  (39 shorter events, 3.7 us)
Async XLA Ops:
  0.6 52.6 %copy-start = (f32[16,64]{1,0:T(8,128)S(1)}, f32[16,64]{1,0:T(8,128)}, u32[]{:S(2)}) copy-start(f32[16,64]{1,0:T(8,128)} %param.9) | copy-start | bytes 12292
  1.4 60.5 %collective-permute-start = (f32[1,128]{1,0:T(1,128)S(1)}, f32[1,128]{1,0:T(1,128)S(1)}, u32[]{:S(2)}, u32[]{:S(2)}) collective-permute-start(f32[1,128]{1,0:T(1,128)S(1)} %get-tuple-element.34), channel_id=1, source_target_pairs={{4,0},{8,4},{12,8},{16,12},{20,16},{24,20},{28,24},{5,1},{9,5},{13... | collective-permute-start | bytes 1544 | tf_op jit(solution)/shard_map/ppermute | solution.py:19
  2.7 59.2 %collective-permute-start.1 = (f32[1,128]{1,0:T(1,128)S(1)}, f32[1,128]{1,0:T(1,128)S(1)}, u32[]{:S(2)}, u32[]{:S(2)}) collective-permute-start(f32[1,128]{1,0:T(1,128)S(1)} %get-tuple-element.33), channel_id=1, source_target_pairs={{0,4},{4,8},{8,12},{12,16},{16,20},{20,24},{24,28},{1,5},{5,9},{9,... | collective-permute-start | bytes 1544 | tf_op jit(solution)/shard_map/ppermute | solution.py:18
  9.5 1.1 copy-start.1
  9.5 1.1 copy-start.2
  53.4 0.7 copy-start.5
  61.3 0.7 copy-start.4
  62.0 5.3 %copy-start.3 = (s32[3,8,128]{2,1,0:T(8,128)S(1)}, s32[3,8,128]{2,1,0:T(8,128)}, u32[]{:S(2)}) copy-start(s32[3,8,128]{2,1,0:T(8,128)} %param.7) | copy-start | bytes 36868
  62.1 4.3 %collective-permute-start.2 = (f32[10,1]{1,0:T(8,128)S(1)}, f32[10,1]{1,0:T(8,128)S(1)}, u32[]{:S(2)}, u32[]{:S(2)}) collective-permute-start(f32[10,1]{1,0:T(8,128)S(1)} %get-tuple-element.32), channel_id=1, source_target_pairs={{1,0},{2,1},{3,2},{5,4},{6,5},{7,6},{9,8},{10,9},{11,10},{13,12},{... | collective-permute-start | bytes 128 | tf_op jit(solution)/shard_map/ppermute | solution.py:19
  63.4 3.8 %collective-permute-start.3 = (f32[10,1]{1,0:T(8,128)S(1)}, f32[10,1]{1,0:T(8,128)S(1)}, u32[]{:S(2)}, u32[]{:S(2)}) collective-permute-start(f32[10,1]{1,0:T(8,128)S(1)} %get-tuple-element.31), channel_id=1, source_target_pairs={{0,1},{1,2},{2,3},{4,5},{5,6},{6,7},{8,9},{9,10},{10,11},{12,13},{... | collective-permute-start | bytes 128 | tf_op jit(solution)/shard_map/ppermute | solution.py:18
  67.4 6.1 %collective-permute-start.4 = (f32[3,1,128]{2,1,0:T(1,128)S(1)}, f32[3,1,128]{2,1,0:T(1,128)S(1)}, u32[]{:S(2)}, u32[]{:S(2)}) collective-permute-start(f32[3,1,128]{2,1,0:T(1,128)S(1)} %get-tuple-element.30), channel_id=1, source_target_pairs={{4,0},{8,4},{12,8},{16,12},{20,16},{24,20},{28,24},{5,1},{9,5},{13... | collective-permute-start | bytes 4616 | tf_op jit(solution)/shard_map/ppermute | solution.py:19
  68.7 6.1 %collective-permute-start.5 = (f32[3,1,128]{2,1,0:T(1,128)S(1)}, f32[3,1,128]{2,1,0:T(1,128)S(1)}, u32[]{:S(2)}, u32[]{:S(2)}) collective-permute-start(f32[3,1,128]{2,1,0:T(1,128)S(1)} %get-tuple-element.29), channel_id=1, source_target_pairs={{0,4},{4,8},{8,12},{12,16},{16,20},{20,24},{24,28},{1,5},{5,9},{9,... | collective-permute-start | bytes 4616 | tf_op jit(solution)/shard_map/ppermute | solution.py:18
  74.9 4.3 %collective-permute-start.7 = (f32[3,10,1]{2,1,0:T(8,128)S(1)}, f32[3,10,1]{2,1,0:T(8,128)S(1)}, u32[]{:S(2)}, u32[]{:S(2)}) collective-permute-start(f32[3,10,1]{2,1,0:T(8,128)S(1)} %get-tuple-element.26), channel_id=1, source_target_pairs={{0,1},{1,2},{2,3},{4,5},{5,6},{6,7},{8,9},{9,10},{10,11},{12,13},{... | collective-permute-start | bytes 368 | tf_op jit(solution)/shard_map/ppermute | solution.py:18
  77.2 6.0 %collective-permute-start.6 = (f32[3,10,1]{2,1,0:T(8,128)S(1)}, f32[3,10,1]{2,1,0:T(8,128)S(1)}, u32[]{:S(2)}, u32[]{:S(2)}) collective-permute-start(f32[3,10,1]{2,1,0:T(8,128)S(1)} %get-tuple-element.25), channel_id=1, source_target_pairs={{1,0},{2,1},{3,2},{5,4},{6,5},{7,6},{9,8},{10,9},{11,10},{13,12},{... | collective-permute-start | bytes 368 | tf_op jit(solution)/shard_map/ppermute | solution.py:19
  140.8 5.9 %collective-permute-start.8 = (f32[3,1,128]{2,1,0:T(1,128)S(1)}, f32[3,1,128]{2,1,0:T(1,128)S(1)}, u32[]{:S(2)}, u32[]{:S(2)}) collective-permute-start(f32[3,1,128]{2,1,0:T(1,128)S(1)} %get-tuple-element.28), channel_id=1, source_target_pairs={{4,0},{8,4},{12,8},{16,12},{20,16},{24,20},{28,24},{5,1},{9,5},{13... | collective-permute-start | bytes 4616 | tf_op jit(solution)/shard_map/ppermute | solution.py:19
  142.1 5.8 %collective-permute-start.9 = (f32[3,1,128]{2,1,0:T(1,128)S(1)}, f32[3,1,128]{2,1,0:T(1,128)S(1)}, u32[]{:S(2)}, u32[]{:S(2)}) collective-permute-start(f32[3,1,128]{2,1,0:T(1,128)S(1)} %get-tuple-element.27), channel_id=1, source_target_pairs={{0,4},{4,8},{8,12},{12,16},{16,20},{20,24},{24,28},{1,5},{5,9},{9,... | collective-permute-start | bytes 4616 | tf_op jit(solution)/shard_map/ppermute | solution.py:18
  148.0 2.6 %collective-permute-start.11 = (f32[3,10,1]{2,1,0:T(8,128)S(1)}, f32[3,10,1]{2,1,0:T(8,128)S(1)}, u32[]{:S(2)}, u32[]{:S(2)}) collective-permute-start(f32[3,10,1]{2,1,0:T(8,128)S(1)} %get-tuple-element.24), channel_id=1, source_target_pairs={{0,1},{1,2},{2,3},{4,5},{5,6},{6,7},{8,9},{9,10},{10,11},{12,13},{... | collective-permute-start | bytes 368 | tf_op jit(solution)/shard_map/ppermute | solution.py:18
  149.3 3.9 %collective-permute-start.10 = (f32[3,10,1]{2,1,0:T(8,128)S(1)}, f32[3,10,1]{2,1,0:T(8,128)S(1)}, u32[]{:S(2)}, u32[]{:S(2)}) collective-permute-start(f32[3,10,1]{2,1,0:T(8,128)S(1)} %get-tuple-element.23), channel_id=1, source_target_pairs={{1,0},{2,1},{3,2},{5,4},{6,5},{7,6},{9,8},{10,9},{11,10},{13,12},{... | collective-permute-start | bytes 368 | tf_op jit(solution)/shard_map/ppermute | solution.py:19
where the time goes:
time: 199 us; the launch traced here: 198 us
  blocking collectives  141 us (71%)
  starting transfers between devices  29.2 us (15%)
  waiting for transfers between devices  10 us (5%)
  between operations  6.67 us (3%)
  local copies, waits for them, and re-layouts  5.22 us (3%)
  other arithmetic  3.45 us (2%)
  matrix products  2.83 us (1%)
    psum x1, blocking collectives, on_device(): curve_sum = lax.psum(jnp.sum(direction * applied), ('row', 'col'))  43 us
    psum x1, blocking collectives, on_device(): lax.psum((jnp.sum(direction * applied), jnp.dot(basis_rows, applied.resha...  42.6 us
    psum x1, blocking collectives, on_device(): lax.psum((jnp.dot(basis_rows, residual.reshape(-1), precision=high), jnp....  41.9 us
    ppermute x6, starting transfers between devices, padded_2(): before = lax.ppermute(last, axis, up)  21.5 us
    unnamed x2, blocking collectives  13.4 us
    ppermute x6, starting transfers between devices, padded_2(): after = lax.ppermute(leading, axis, down)  7.73 us
    ppermute x6, waiting for transfers between devices, padded_2(): after = lax.ppermute(leading, axis, down)  6.67 us
    unnamed x19, local copies, waits for them, and re-layouts  4.22 us
  transfers between devices with their start and end apart: 12, of which 5 were waited for; matrix products, arithmetic and copies ran while one was open for 2% of the time, Pallas kernels for 0%

commit v1 on v0

--- a/solution.py
+++ b/solution.py
@@ -21,6 +21,15 @@
     return shard
 
 
+def share(rows):
+    return lax.all_to_all(rows, ("row", "col"), 0, 0, tiled=True)
+
+
+def sum_over(values):
+    count = lax.axis_size("row") * lax.axis_size("col")
+    return jnp.sum(share(jnp.broadcast_to(values, (count,) + values.shape)), axis=0)
+
+
 def on_device(right_side, viscosity, free_mask, coarse_basis, gram_inverse):
     high = lax.Precision.HIGHEST
     components, patch_rows, patch_cols = right_side.shape
@@ -40,8 +49,7 @@
     basis_rows = coarse_basis.reshape(columns, -1)
 
     def solve_coarse(coarse_dot):
-        coeff_part = jnp.dot(gram_inverse, coarse_dot, precision=high) * coarse_scale
-        return lax.all_gather(coeff_part, "col", axis=0, tiled=True)
+        return jnp.dot(gram, coarse_dot, precision=high) * coarse_scale
 
     def precondition(residual, coarse_dot, weighted_sq):
         coeffs = solve_coarse(coarse_dot)
@@ -52,13 +60,23 @@
 
     solution = jnp.zeros_like(right_side)
     residual = right_side
-    coarse_dot, weighted_sq = lax.psum(
-        (
+    rows, cols = (lax.axis_size("row"), lax.axis_size("col"))
+    block = gram_inverse.size
+    piece = -(-block // rows)
+    gram_flat = jnp.pad(gram_inverse.reshape(-1), (0, piece * rows - block))
+    own_piece = lax.dynamic_slice_in_dim(gram_flat, lax.axis_index("row") * piece, piece)
+    sent = jnp.concatenate(
+        [
             jnp.dot(basis_rows, residual.reshape(-1), precision=high),
-            jnp.sum(jacobi * residual * residual),
-        ),
-        ("row", "col"),
+            jnp.sum(jacobi * residual * residual)[None],
+            own_piece,
+        ]
     )
+    got = share(jnp.broadcast_to(sent, (rows * cols,) + sent.shape))
+    sums = jnp.sum(got[:, : columns + 1], axis=0)
+    coarse_dot, weighted_sq = (sums[:columns], sums[columns])
+    gram = got[:, columns + 1 :].reshape(rows, cols, piece).transpose(1, 0, 2)
+    gram = gram.reshape(cols, rows * piece)[:, :block].reshape(columns, columns)
     direction, energy = precondition(residual, coarse_dot, weighted_sq)
     for iteration in range(ITERS):
         masked = unfixed * direction
@@ -71,15 +89,18 @@
         )
         applied = unfixed * stencil + (1.0 - unfixed) * direction
         if iteration + 1 < ITERS:
-            curve_sum, image_coarse, cross_term, image_sq = lax.psum(
-                (
-                    jnp.sum(direction * applied),
-                    jnp.dot(basis_rows, applied.reshape(-1), precision=high),
-                    jnp.sum(jacobi * residual * applied),
-                    jnp.sum(jacobi * applied * applied),
-                ),
-                ("row", "col"),
+            sums = sum_over(
+                jnp.concatenate(
+                    [
+                        jnp.dot(basis_rows, applied.reshape(-1), precision=high),
+                        jnp.sum(direction * applied)[None],
+                        jnp.sum(jacobi * residual * applied)[None],
+                        jnp.sum(jacobi * applied * applied)[None],
+                    ]
+                )
             )
+            image_coarse = sums[:columns]
+            curve_sum, cross_term, image_sq = (sums[columns], sums[columns + 1], sums[columns + 2])
             step_len = energy / curve_sum
             solution = step_len * direction
             residual = residual - step_len * applied
@@ -89,7 +110,7 @@
             direction = smoothed + energy_new / energy * direction
             energy = energy_new
         else:
-            curve_sum = lax.psum(jnp.sum(direction * applied), ("row", "col"))
+            curve_sum = sum_over(jnp.sum(direction * applied)[None])[0]
             step_len = energy / curve_sum
             solution = solution + step_len * direction
             residual = residual - step_len * applied

time: 199 us -> 99.8 us (0.50)
  blocking collectives: 141 us -> 12.8 us
  starting transfers between devices: 29.2 us -> 41.8 us
  waiting for transfers between devices: 10 us -> 20.7 us
  other arithmetic: 3.45 us -> 6.22 us
  matrix products: 2.83 us -> 5.34 us
    psum x3 -> x0, blocking collectives: 127 us -> none  [the longest x1 43 us: on_device(): curve_sum = lax.psum(jnp.sum(direction * applied), ('row', 'col'))]
    all_to_all x0 -> x2, starting transfers between devices: none -> 13.9 us  [share(): return lax.all_to_all(rows, ('row', 'col'), 0, 0, tiled=True)]
    unnamed x2 -> x0, blocking collectives: 13.4 us -> none
    all_to_all x0 -> x1, blocking collectives: none -> 12.8 us  [share(): return lax.all_to_all(rows, ('row', 'col'), 0, 0, tiled=True)]
    all_to_all x0 -> x2, waiting for transfers between devices: none -> 12.2 us  [share(): return lax.all_to_all(rows, ('row', 'col'), 0, 0, tiled=True)]
    unnamed x19 -> x11, local copies, waits for them, and re-layouts: 4.22 us -> 0.92 us
    concatenate x0 -> x2, other arithmetic: none -> 2.71 us  [the longest x1 1.99 us: on_device(): jnp.concatenate([jnp.dot(basis_rows, applied.reshape(-1), precision=high)...]
  transfers between devices with their start and end apart: 12 -> 14, of which waited for: 5 -> 7; matrix products, arithmetic and copies ran while one was open for 2% -> 4% of each run, Pallas kernels for 0% -> 0%
where the time goes in v1:
time: 99.8 us; the launch traced here: 99.1 us
  starting transfers between devices  41.8 us (42%)
  waiting for transfers between devices  20.7 us (21%)
  blocking collectives  12.8 us (13%)
  other arithmetic  6.22 us (6%)
  between operations  6.2 us (6%)
  local copies, waits for them, and re-layouts  6.09 us (6%)
  matrix products  5.34 us (5%)
    ppermute x6, starting transfers between devices, padded_2(): before = lax.ppermute(last, axis, up)  20.2 us
    all_to_all x2, starting transfers between devices, share(): return lax.all_to_all(rows, ('row', 'col'), 0, 0, tiled=True)  13.9 us
    all_to_all x1, blocking collectives, share(): return lax.all_to_all(rows, ('row', 'col'), 0, 0, tiled=True)  12.8 us
    all_to_all x2, waiting for transfers between devices, share(): return lax.all_to_all(rows, ('row', 'col'), 0, 0, tiled=True)  12.2 us
    ppermute x6, starting transfers between devices, padded_2(): after = lax.ppermute(leading, axis, down)  7.73 us
    ppermute x6, waiting for transfers between devices, padded_2(): after = lax.ppermute(leading, axis, down)  5.07 us
    ppermute x6, waiting for transfers between devices, padded_2(): before = lax.ppermute(last, axis, up)  3.36 us
  transfers between devices with their start and end apart: 14, of which 7 were waited for; matrix products, arithmetic and copies ran while one was open for 4% of the time, Pallas kernels for 0%

profile of v1, /device:TPU:0, one launch (start us, length us, event | category | flops | bytes accessed | tf_op | source)
XLA Modules:
  0.0 99.1 jit_solution(1275523744470109637)
XLA Ops:
  0.6 0.8 fusion.56
  1.4 1.3 %collective-permute-start = (f32[1,128]{1,0:T(1,128)S(1)}, f32[1,128]{1,0:T(1,128)S(1)}, u32[]{:S(2)}, u32[]{:S(2)}) collective-permute-start(f32[1,128]{1,0:T(1,128)S(1)} %get-tuple-element.28), channel_id=1, source_target_pairs={{4,0},{8,4},{12,8},{16,12},{20,16},{24,20},{28,24},{5,1},{9,5},{13... | collective-permute-start | bytes 1544 | tf_op jit(solution)/shard_map/ppermute | solution.py:19
  2.7 5.5 %collective-permute-start.1 = (f32[1,128]{1,0:T(1,128)S(1)}, f32[1,128]{1,0:T(1,128)S(1)}, u32[]{:S(2)}, u32[]{:S(2)}) collective-permute-start(f32[1,128]{1,0:T(1,128)S(1)} %get-tuple-element.27), channel_id=1, source_target_pairs={{0,4},{4,8},{8,12},{12,16},{16,20},{20,24},{24,28},{1,5},{5,9},{9,... | collective-permute-start | bytes 1544 | tf_op jit(solution)/shard_map/ppermute | solution.py:18
  8.2 0.8 reshape.36
  9.0 1.9 %convolution_bitcast_fusion.3 = f32[64]{0:T(128)S(1)} fusion(f32[3,8,128,1]{2,3,1,0:T(1,128)} %bitcast.81, f32[64,3,8,128]{3,2,1,0:T(8,128)} %param.8), kind=kOutput, calls=%fused_computation.5 | convolution fusion | flops 2359296 | bytes 798976 | tf_op jit(solution)/shard_map/dot_general | solution.py:70
  11.7 1.3 %collective-permute-start.2 = (f32[10,1]{1,0:T(8,128)S(1)}, f32[10,1]{1,0:T(8,128)S(1)}, u32[]{:S(2)}, u32[]{:S(2)}) collective-permute-start(f32[10,1]{1,0:T(8,128)S(1)} %get-tuple-element.26), channel_id=1, source_target_pairs={{1,0},{2,1},{3,2},{5,4},{6,5},{7,6},{9,8},{10,9},{11,10},{13,12},{... | collective-permute-start | bytes 128 | tf_op jit(solution)/shard_map/ppermute | solution.py:19
  13.0 3.0 %collective-permute-start.3 = (f32[10,1]{1,0:T(8,128)S(1)}, f32[10,1]{1,0:T(8,128)S(1)}, u32[]{:S(2)}, u32[]{:S(2)}) collective-permute-start(f32[10,1]{1,0:T(8,128)S(1)} %get-tuple-element.25), channel_id=1, source_target_pairs={{0,1},{1,2},{2,3},{4,5},{5,6},{6,7},{8,9},{9,10},{10,11},{12,13},{... | collective-permute-start | bytes 128 | tf_op jit(solution)/shard_map/ppermute | solution.py:18
  16.0 0.8 collective-permute-done.3
  17.5 0.7 pad_maximum_fusion.27
  18.9 8.0 %all-to-all-start = ((f32[32,1,193]{2,1,0:T(1,128)}), f32[32,1,193]{2,1,0:T(1,128)S(1)}, u32[]{:S(2)}, u32[]{:S(2)}) async-start(f32[32,1,193]{2,1,0:T(1,128)} %broadcast_in_dim.15), calls=%async_computation | async-start | bytes 65536 | tf_op jit(solution)/shard_map/all_to_all | solution.py:25
  27.2 6.9 %all-to-all-done = f32[32,1,193]{2,1,0:T(1,128)S(1)} async-done(((f32[32,1,193]{2,1,0:T(1,128)}), f32[32,1,193]{2,1,0:T(1,128)S(1)}, u32[]{:S(2)}, u32[]{:S(2)}) %all-to-all-start) | async-done | bytes 24736 | tf_op jit(solution)/shard_map/all_to_all | solution.py:25
  34.3 0.8 multiply_reduce_fusion.5
  35.7 1.3 %collective-permute-start.4 = (f32[3,1,128]{2,1,0:T(1,128)S(1)}, f32[3,1,128]{2,1,0:T(1,128)S(1)}, u32[]{:S(2)}, u32[]{:S(2)}) collective-permute-start(f32[3,1,128]{2,1,0:T(1,128)S(1)} %get-tuple-element.24), channel_id=1, source_target_pairs={{4,0},{8,4},{12,8},{16,12},{20,16},{24,20},{28,24},{5,1},{9,5},{13... | collective-permute-start | bytes 4616 | tf_op jit(solution)/shard_map/ppermute | solution.py:19
  37.0 4.5 %collective-permute-start.5 = (f32[3,1,128]{2,1,0:T(1,128)S(1)}, f32[3,1,128]{2,1,0:T(1,128)S(1)}, u32[]{:S(2)}, u32[]{:S(2)}) collective-permute-start(f32[3,1,128]{2,1,0:T(1,128)S(1)} %get-tuple-element.23), channel_id=1, source_target_pairs={{0,4},{4,8},{8,12},{12,16},{16,20},{20,24},{24,28},{1,5},{5,9},{9,... | collective-permute-start | bytes 4616 | tf_op jit(solution)/shard_map/ppermute | solution.py:18
  41.5 1.3 %collective-permute-done.5 = f32[3,1,128]{2,1,0:T(1,128)S(1)} collective-permute-done((f32[3,1,128]{2,1,0:T(1,128)S(1)}, f32[3,1,128]{2,1,0:T(1,128)S(1)}, u32[]{:S(2)}, u32[]{:S(2)}) %collective-permute-start.5) | collective-permute-done | bytes 1568 | tf_op jit(solution)/shard_map/ppermute | solution.py:18
  42.9 1.3 %collective-permute-start.7 = (f32[3,10,1]{2,1,0:T(8,128)S(1)}, f32[3,10,1]{2,1,0:T(8,128)S(1)}, u32[]{:S(2)}, u32[]{:S(2)}) collective-permute-start(f32[3,10,1]{2,1,0:T(8,128)S(1)} %get-tuple-element.20), channel_id=1, source_target_pairs={{0,1},{1,2},{2,3},{4,5},{5,6},{6,7},{8,9},{9,10},{10,11},{12,13},{... | collective-permute-start | bytes 368 | tf_op jit(solution)/shard_map/ppermute | solution.py:18
  44.2 1.3 %collective-permute-start.6 = (f32[3,10,1]{2,1,0:T(8,128)S(1)}, f32[3,10,1]{2,1,0:T(8,128)S(1)}, u32[]{:S(2)}, u32[]{:S(2)}) collective-permute-start(f32[3,10,1]{2,1,0:T(8,128)S(1)} %get-tuple-element.19), channel_id=1, source_target_pairs={{1,0},{2,1},{3,2},{5,4},{6,5},{7,6},{9,8},{10,9},{11,10},{13,12},{... | collective-permute-start | bytes 368 | tf_op jit(solution)/shard_map/ppermute | solution.py:19
  45.5 2.5 %collective-permute-done.6 = f32[3,10,1]{2,1,0:T(8,128)S(1)} collective-permute-done((f32[3,10,1]{2,1,0:T(8,128)S(1)}, f32[3,10,1]{2,1,0:T(8,128)S(1)}, u32[]{:S(2)}, u32[]{:S(2)}) %collective-permute-start.6) | collective-permute-done | bytes 152 | tf_op jit(solution)/shard_map/ppermute | solution.py:19
  48.0 0.8 multiply_reduce_fusion.1
  48.8 0.7 convolution_bitcast_fusion.1
  49.5 2.0 %pad_maximum_fusion.28 = f32[67]{0:T(128)S(1)} fusion(f32[1]{0:T(128)} %bitcast.21, f32[1]{0:T(128)} %bitcast.20, f32[1]{0:T(128)} %bitcast.19, f32[64]{0:T(128)S(1)} %convolution_bitcast_fusion.1), kind=kLoop, calls=%fused_computation.86 | loop fusion | flops 201 | bytes 536 | tf_op jit(solution)/shard_map/concatenate | solution.py:93
  52.1 5.9 %all-to-all-start.1 = ((f32[32,1,67]{2,1,0:T(1,128)}), f32[32,1,67]{2,1,0:T(1,128)S(1)}, u32[]{:S(2)}, u32[]{:S(2)}) async-start(f32[32,1,67]{2,1,0:T(1,128)} %broadcast_in_dim.38), calls=%async_computation.1 | async-start | bytes 32768 | tf_op jit(solution)/shard_map/all_to_all | solution.py:25
  59.9 5.3 %all-to-all-done.1 = f32[32,1,67]{2,1,0:T(1,128)S(1)} async-done(((f32[32,1,67]{2,1,0:T(1,128)}), f32[32,1,67]{2,1,0:T(1,128)S(1)}, u32[]{:S(2)}, u32[]{:S(2)}) %all-to-all-start.1) | async-done | bytes 8608 | tf_op jit(solution)/shard_map/all_to_all | solution.py:25
  66.6 0.9 multiply_reduce_fusion.4
  70.6 1.3 %collective-permute-start.8 = (f32[3,1,128]{2,1,0:T(1,128)S(1)}, f32[3,1,128]{2,1,0:T(1,128)S(1)}, u32[]{:S(2)}, u32[]{:S(2)}) collective-permute-start(f32[3,1,128]{2,1,0:T(1,128)S(1)} %get-tuple-element.22), channel_id=1, source_target_pairs={{4,0},{8,4},{12,8},{16,12},{20,16},{24,20},{28,24},{5,1},{9,5},{13... | collective-permute-start | bytes 4616 | tf_op jit(solution)/shard_map/ppermute | solution.py:19
  71.9 4.5 %collective-permute-start.9 = (f32[3,1,128]{2,1,0:T(1,128)S(1)}, f32[3,1,128]{2,1,0:T(1,128)S(1)}, u32[]{:S(2)}, u32[]{:S(2)}) collective-permute-start(f32[3,1,128]{2,1,0:T(1,128)S(1)} %get-tuple-element.21), channel_id=1, source_target_pairs={{0,4},{4,8},{8,12},{12,16},{16,20},{20,24},{24,28},{1,5},{5,9},{9,... | collective-permute-start | bytes 4616 | tf_op jit(solution)/shard_map/ppermute | solution.py:18
  76.5 1.3 %collective-permute-done.9 = f32[3,1,128]{2,1,0:T(1,128)S(1)} collective-permute-done((f32[3,1,128]{2,1,0:T(1,128)S(1)}, f32[3,1,128]{2,1,0:T(1,128)S(1)}, u32[]{:S(2)}, u32[]{:S(2)}) %collective-permute-start.9) | collective-permute-done | bytes 1568 | tf_op jit(solution)/shard_map/ppermute | solution.py:18
  77.9 1.3 %collective-permute-start.11 = (f32[3,10,1]{2,1,0:T(8,128)S(1)}, f32[3,10,1]{2,1,0:T(8,128)S(1)}, u32[]{:S(2)}, u32[]{:S(2)}) collective-permute-start(f32[3,10,1]{2,1,0:T(8,128)S(1)} %get-tuple-element.18), channel_id=1, source_target_pairs={{0,1},{1,2},{2,3},{4,5},{5,6},{6,7},{8,9},{9,10},{10,11},{12,13},{... | collective-permute-start | bytes 368 | tf_op jit(solution)/shard_map/ppermute | solution.py:18
  79.2 1.3 %collective-permute-start.10 = (f32[3,10,1]{2,1,0:T(8,128)S(1)}, f32[3,10,1]{2,1,0:T(8,128)S(1)}, u32[]{:S(2)}, u32[]{:S(2)}) collective-permute-start(f32[3,10,1]{2,1,0:T(8,128)S(1)} %get-tuple-element.17), channel_id=1, source_target_pairs={{1,0},{2,1},{3,2},{5,4},{6,5},{7,6},{9,8},{10,9},{11,10},{13,12},{... | collective-permute-start | bytes 368 | tf_op jit(solution)/shard_map/ppermute | solution.py:19
  80.5 2.5 %collective-permute-done.10 = f32[3,10,1]{2,1,0:T(8,128)S(1)} collective-permute-done((f32[3,10,1]{2,1,0:T(8,128)S(1)}, f32[3,10,1]{2,1,0:T(8,128)S(1)}, u32[]{:S(2)}, u32[]{:S(2)}) %collective-permute-start.10) | collective-permute-done | bytes 152 | tf_op jit(solution)/shard_map/ppermute | solution.py:19
  83.0 0.7 multiply_reduce_fusion
  84.4 12.8 %all_to_all.21 = f32[32,1,1]{2,1,0:T(1,128)S(1)} all-to-all(f32[32,1,1]{2,1,0:T(1,128)S(1)} %broadcast_in_dim.39), channel_id=1, replica_groups=mesh['row'=8,'col'=4] {'row','col'}, dimensions={0} | all-to-all | bytes 256 | tf_op jit(solution)/shard_map/all_to_all | solution.py:25
  (45 shorter events, 7.7 us)
Async XLA Ops:
  0.6 26.2 %copy-start = (f32[64,3,8,128]{3,2,1,0:T(8,128)S(1)}, f32[64,3,8,128]{3,2,1,0:T(8,128)}, u32[]{:S(2)}) copy-start(f32[64,3,8,128]{3,2,1,0:T(8,128)} %param.8) | copy-start | bytes 2359300
  1.4 9.6 %collective-permute-start = (f32[1,128]{1,0:T(1,128)S(1)}, f32[1,128]{1,0:T(1,128)S(1)}, u32[]{:S(2)}, u32[]{:S(2)}) collective-permute-start(f32[1,128]{1,0:T(1,128)S(1)} %get-tuple-element.28), channel_id=1, source_target_pairs={{4,0},{8,4},{12,8},{16,12},{20,16},{24,20},{28,24},{5,1},{9,5},{13... | collective-permute-start | bytes 1544 | tf_op jit(solution)/shard_map/ppermute | solution.py:19
  2.7 8.3 %collective-permute-start.1 = (f32[1,128]{1,0:T(1,128)S(1)}, f32[1,128]{1,0:T(1,128)S(1)}, u32[]{:S(2)}, u32[]{:S(2)}) collective-permute-start(f32[1,128]{1,0:T(1,128)S(1)} %get-tuple-element.27), channel_id=1, source_target_pairs={{0,4},{4,8},{8,12},{12,16},{16,20},{20,24},{24,28},{1,5},{5,9},{9,... | collective-permute-start | bytes 1544 | tf_op jit(solution)/shard_map/ppermute | solution.py:18
  10.9 0.7 copy-start.3
  11.7 4.4 %collective-permute-start.2 = (f32[10,1]{1,0:T(8,128)S(1)}, f32[10,1]{1,0:T(8,128)S(1)}, u32[]{:S(2)}, u32[]{:S(2)}) collective-permute-start(f32[10,1]{1,0:T(8,128)S(1)} %get-tuple-element.26), channel_id=1, source_target_pairs={{1,0},{2,1},{3,2},{5,4},{6,5},{7,6},{9,8},{10,9},{11,10},{13,12},{... | collective-permute-start | bytes 128 | tf_op jit(solution)/shard_map/ppermute | solution.py:19
  13.0 4.0 %copy-start.1 = (f32[3,8,128]{2,1,0:T(8,128)S(1)}, f32[3,8,128]{2,1,0:T(8,128)}, u32[]{:S(2)}) copy-start(f32[3,8,128]{2,1,0:T(8,128)} %param.5) | copy-start | bytes 36868
  13.0 3.9 %copy-start.2 = (s32[3,8,128]{2,1,0:T(8,128)S(1)}, s32[3,8,128]{2,1,0:T(8,128)}, u32[]{:S(2)}) copy-start(s32[3,8,128]{2,1,0:T(8,128)} %param.7) | copy-start | bytes 36868
  13.0 3.8 %collective-permute-start.3 = (f32[10,1]{1,0:T(8,128)S(1)}, f32[10,1]{1,0:T(8,128)S(1)}, u32[]{:S(2)}, u32[]{:S(2)}) collective-permute-start(f32[10,1]{1,0:T(8,128)S(1)} %get-tuple-element.25), channel_id=1, source_target_pairs={{0,1},{1,2},{2,3},{4,5},{5,6},{6,7},{8,9},{9,10},{10,11},{12,13},{... | collective-permute-start | bytes 128 | tf_op jit(solution)/shard_map/ppermute | solution.py:18
  18.9 15.2 %all-to-all-start = ((f32[32,1,193]{2,1,0:T(1,128)}), f32[32,1,193]{2,1,0:T(1,128)S(1)}, u32[]{:S(2)}, u32[]{:S(2)}) async-start(f32[32,1,193]{2,1,0:T(1,128)} %broadcast_in_dim.15), calls=%async_computation | async-start | bytes 65536 | tf_op jit(solution)/shard_map/all_to_all | solution.py:25
  35.7 5.9 %collective-permute-start.4 = (f32[3,1,128]{2,1,0:T(1,128)S(1)}, f32[3,1,128]{2,1,0:T(1,128)S(1)}, u32[]{:S(2)}, u32[]{:S(2)}) collective-permute-start(f32[3,1,128]{2,1,0:T(1,128)S(1)} %get-tuple-element.24), channel_id=1, source_target_pairs={{4,0},{8,4},{12,8},{16,12},{20,16},{24,20},{28,24},{5,1},{9,5},{13... | collective-permute-start | bytes 4616 | tf_op jit(solution)/shard_map/ppermute | solution.py:19
  37.0 5.8 %collective-permute-start.5 = (f32[3,1,128]{2,1,0:T(1,128)S(1)}, f32[3,1,128]{2,1,0:T(1,128)S(1)}, u32[]{:S(2)}, u32[]{:S(2)}) collective-permute-start(f32[3,1,128]{2,1,0:T(1,128)S(1)} %get-tuple-element.23), channel_id=1, source_target_pairs={{0,4},{4,8},{8,12},{12,16},{16,20},{20,24},{24,28},{1,5},{5,9},{9,... | collective-permute-start | bytes 4616 | tf_op jit(solution)/shard_map/ppermute | solution.py:18
  42.9 2.6 %collective-permute-start.7 = (f32[3,10,1]{2,1,0:T(8,128)S(1)}, f32[3,10,1]{2,1,0:T(8,128)S(1)}, u32[]{:S(2)}, u32[]{:S(2)}) collective-permute-start(f32[3,10,1]{2,1,0:T(8,128)S(1)} %get-tuple-element.20), channel_id=1, source_target_pairs={{0,1},{1,2},{2,3},{4,5},{5,6},{6,7},{8,9},{9,10},{10,11},{12,13},{... | collective-permute-start | bytes 368 | tf_op jit(solution)/shard_map/ppermute | solution.py:18
  44.2 3.8 %collective-permute-start.6 = (f32[3,10,1]{2,1,0:T(8,128)S(1)}, f32[3,10,1]{2,1,0:T(8,128)S(1)}, u32[]{:S(2)}, u32[]{:S(2)}) collective-permute-start(f32[3,10,1]{2,1,0:T(8,128)S(1)} %get-tuple-element.19), channel_id=1, source_target_pairs={{1,0},{2,1},{3,2},{5,4},{6,5},{7,6},{9,8},{10,9},{11,10},{13,12},{... | collective-permute-start | bytes 368 | tf_op jit(solution)/shard_map/ppermute | solution.py:19
  52.1 13.1 %all-to-all-start.1 = ((f32[32,1,67]{2,1,0:T(1,128)}), f32[32,1,67]{2,1,0:T(1,128)S(1)}, u32[]{:S(2)}, u32[]{:S(2)}) async-start(f32[32,1,67]{2,1,0:T(1,128)} %broadcast_in_dim.38), calls=%async_computation.1 | async-start | bytes 32768 | tf_op jit(solution)/shard_map/all_to_all | solution.py:25
  70.6 5.9 %collective-permute-start.8 = (f32[3,1,128]{2,1,0:T(1,128)S(1)}, f32[3,1,128]{2,1,0:T(1,128)S(1)}, u32[]{:S(2)}, u32[]{:S(2)}) collective-permute-start(f32[3,1,128]{2,1,0:T(1,128)S(1)} %get-tuple-element.22), channel_id=1, source_target_pairs={{4,0},{8,4},{12,8},{16,12},{20,16},{24,20},{28,24},{5,1},{9,5},{13... | collective-permute-start | bytes 4616 | tf_op jit(solution)/shard_map/ppermute | solution.py:19
  71.9 5.8 %collective-permute-start.9 = (f32[3,1,128]{2,1,0:T(1,128)S(1)}, f32[3,1,128]{2,1,0:T(1,128)S(1)}, u32[]{:S(2)}, u32[]{:S(2)}) collective-permute-start(f32[3,1,128]{2,1,0:T(1,128)S(1)} %get-tuple-element.21), channel_id=1, source_target_pairs={{0,4},{4,8},{8,12},{12,16},{16,20},{20,24},{24,28},{1,5},{5,9},{9,... | collective-permute-start | bytes 4616 | tf_op jit(solution)/shard_map/ppermute | solution.py:18
  77.9 2.6 %collective-permute-start.11 = (f32[3,10,1]{2,1,0:T(8,128)S(1)}, f32[3,10,1]{2,1,0:T(8,128)S(1)}, u32[]{:S(2)}, u32[]{:S(2)}) collective-permute-start(f32[3,10,1]{2,1,0:T(8,128)S(1)} %get-tuple-element.18), channel_id=1, source_target_pairs={{0,1},{1,2},{2,3},{4,5},{5,6},{6,7},{8,9},{9,10},{10,11},{12,13},{... | collective-permute-start | bytes 368 | tf_op jit(solution)/shard_map/ppermute | solution.py:18
  79.2 3.9 %collective-permute-start.10 = (f32[3,10,1]{2,1,0:T(8,128)S(1)}, f32[3,10,1]{2,1,0:T(8,128)S(1)}, u32[]{:S(2)}, u32[]{:S(2)}) collective-permute-start(f32[3,10,1]{2,1,0:T(8,128)S(1)} %get-tuple-element.17), channel_id=1, source_target_pairs={{1,0},{2,1},{3,2},{5,4},{6,5},{7,6},{9,8},{10,9},{11,10},{13,12},{... | collective-permute-start | bytes 368 | tf_op jit(solution)/shard_map/ppermute | solution.py:19

commit v2 on v0

v2 whole, which is shorter than its diff:
```python
import functools
import math

import jax
import jax.numpy as jnp
from jax import lax
from jax.experimental import pallas as pl
from jax.experimental.pallas import tpu as pltpu
from jax.sharding import PartitionSpec as P

F32 = jnp.float32
VMEM = pl.BlockSpec(memory_space=pltpu.VMEM)
DOTS, EAST, WEST = 64, 72, 96


def iota(shape, dim):
    return lax.broadcasted_iota(jnp.int32, shape, dim)


def pick(flag, yes, no):
    return jnp.where(jnp.full(yes.shape, flag, jnp.int32) == 1, yes, no)


def to_row(column, first=0):
    shape = (column.shape[0], 128)
    spread = jnp.where(iota(shape, 1) == iota(shape, 0) + first, column, 0.0)
    return jnp.sum(spread, axis=0, keepdims=True)


def to_column(row, count, first=0):
    shape = (count, 128)
    spread = jnp.where(iota(shape, 1) == iota(shape, 0) + first, row, 0.0)
    return jnp.sum(spread, axis=1, keepdims=True)


def total(values):
    return jnp.sum(jnp.sum(values, axis=0, keepdims=True), axis=1, keepdims=True)


def shifts(tile, north, south, east, west):
    rows, cols = tile.shape
    sub, lane = (iota(tile.shape, 0), iota(tile.shape, 1))
    return (
        jnp.where(sub == rows - 1, north, pltpu.roll(tile, rows - 1, 0)),
        jnp.where(sub == 0, south, pltpu.roll(tile, 1, 0)),
        jnp.where(lane == cols - 1, east, pltpu.roll(tile, cols - 1, 1)),
        jnp.where(lane == 0, west, pltpu.roll(tile, 1, 1)),
    )


def project(basis_ref, field, acc_ref, columns, comps, rows):
    for k in range(columns):
        base = k * comps * rows
        acc = basis_ref[base : base + rows, :] * field[0]
        for c in range(1, comps):
            acc = acc + basis_ref[base + c * rows : base + (c + 1) * rows, :] * field[c]
        acc_ref[k * rows : (k + 1) * rows, :] = acc
    sums = acc_ref[pl.ds(0, columns, stride=rows), :]
    for s in range(1, rows):
        sums = sums + acc_ref[pl.ds(s, columns, stride=rows), :]
    return jnp.sum(sums, axis=1, keepdims=True)


def combine(basis_ref, wide_ref, columns, comps, rows):
    out = [[None, None] for _ in range(comps)]
    for k in range(columns):
        weight = jnp.broadcast_to(wide_ref[k : k + 1, :], (rows, 128))
        for c in range(comps):
            base = (k * comps + c) * rows
            term = weight * basis_ref[base : base + rows, :]
            old = out[c][k % 2]
            out[c][k % 2] = term if old is None else old + term
    return [a + b for a, b in out]


def pack_kernel(sizes, basis_ref, rhs_ref, mask_ref, visc_ref, gram_ref,
                send_ref, rowa_ref, rowb_ref, cola_ref, colb_ref, acc_ref):
    columns, comps, rows, cols = sizes
    even_row = 1 - lax.rem(lax.axis_index("row"), 2)
    even_col = 1 - lax.rem(lax.axis_index("col"), 2)
    rhs = [rhs_ref[c * rows : (c + 1) * rows, :] for c in range(comps)]
    mask = [mask_ref[c * rows : (c + 1) * rows, :].astype(F32) for c in range(comps)]
    visc = visc_ref[...]
    lane = iota((rows, cols), 1)
    top, low = rows - 1, cols - 1

    for c in range(comps):
        north = basis_ref[pl.ds(c * rows + top, columns, stride=comps * rows), :]
        south = basis_ref[pl.ds(c * rows, columns, stride=comps * rows), :]
        north = north * mask[c][top : top + 1, :]
        south = south * mask[c][0:1, :]
        rowa_ref[c * columns : (c + 1) * columns, :] = pick(even_row, north, south)
        rowb_ref[c * columns : (c + 1) * columns, :] = pick(even_row, south, north)
    north = [mask[c][top : top + 1, :] * rhs[c][top : top + 1, :] for c in range(comps)]
    south = [mask[c][0:1, :] * rhs[c][0:1, :] for c in range(comps)]
    north += [visc[top : top + 1, :], visc[top - 1 : top, :]]
    south += [visc[0:1, :], visc[1:2, :]]
    for i in range(comps + 2):
        at = comps * columns + i
        rowa_ref[at : at + 1, :] = pick(even_row, north[i], south[i])
        rowb_ref[at : at + 1, :] = pick(even_row, south[i], north[i])
    rest = comps * columns + comps + 2
    blank = jnp.zeros((rowa_ref.shape[0] - rest, cols), F32)
    rowa_ref[rest:, :] = blank
    rowb_ref[rest:, :] = blank

    for c in range(comps):
        east, west = (jnp.zeros((rows, cols), F32), jnp.zeros((rows, cols), F32))
        for k in range(columns):
            base = (k * comps + c) * rows
            tile = basis_ref[base : base + rows, :]
            east = jnp.where(lane == k, pltpu.roll(tile, (k - low) % cols, 1), east)
            west = jnp.where(lane == k, tile if k == 0 else pltpu.roll(tile, k, 1), west)
        east = jnp.where(lane == columns, rhs[c][:, low : low + 1], east)
        west = jnp.where(lane == columns, rhs[c][:, 0:1], west)
        east = east * mask[c][:, low : low + 1]
        west = west * mask[c][:, 0:1]
        cola_ref[c * rows : (c + 1) * rows, :] = pick(even_col, east, west)
        colb_ref[c * rows : (c + 1) * rows, :] = pick(even_col, west, east)
    east = jnp.where(lane == 0, visc[:, low : low + 1], visc[:, low - 1 : low])
    west = jnp.where(lane == 0, visc[:, 0:1], visc[:, 1:2])
    cola_ref[comps * rows :, :] = pick(even_col, east, west)
    colb_ref[comps * rows :, :] = pick(even_col, west, east)

    row = to_row(project(basis_ref, rhs, acc_ref, columns, comps, rows))
    lanes = iota((1, cols), 1)
    corners = [visc[i : i + 1, j : j + 1] for i in (0, top) for j in (0, low)]
    for i, corner in enumerate(corners):
        row = jnp.where(lanes == columns + i, corner, row)
    both = jnp.concatenate([row, gram_ref[...]], axis=0)
    send_ref[...] = jnp.broadcast_to(both[None], send_ref.shape)


def first_kernel(sizes, whole_rows, got_ref, *refs):
    columns, comps, rows, cols, scale = sizes
    if whole_rows:
        gram_in_ref = None
    else:
        gram_in_ref, *refs = refs
    (basis_ref, rhs_ref, mask_ref, visc_ref, rowa_ref, rowb_ref, cola_ref, colb_ref,
     send_ref, state_ref, face_ref, edge_ref, side_ref, small_ref, gram_ref,
     acc_ref, wide_ref) = refs
    at_row, at_col = (lax.axis_index("row"), lax.axis_index("col"))
    row_count, col_count = (lax.axis_size("row"), lax.axis_size("col"))
    even_row, even_col = (1 - lax.rem(at_row, 2), 1 - lax.rem(at_col, 2))
    me = at_row * col_count + at_col
    top, low = rows - 1, cols - 1
    rhs = [rhs_ref[c * rows : (c + 1) * rows, :] for c in range(comps)]
    mask = [mask_ref[c * rows : (c + 1) * rows, :].astype(F32) for c in range(comps)]
    visc = visc_ref[...]
    sub, lane = (iota((rows, cols), 0), iota((rows, cols), 1))
    lanes = iota((1, cols), 1)

    if whole_rows:
        per = cols // columns
        for r in range(row_count):
            for c in range(col_count):
                piece = got_ref[r * col_count + c, 1:2, :]
                for t in range(per):
                    at = (c * row_count + r) * per + t
                    moved = pltpu.roll(piece, cols - t * columns, 1) if t else piece
                    gram_ref[at : at + 1, :] = moved
    else:
        gram_ref[:, :columns] = gram_in_ref[...]
    sums = jnp.sum(got_ref[...], axis=0)[0:1, :]
    dots = jnp.where(lanes < columns, sums, 0.0)
    gram = jnp.where(iota((columns, cols), 1) < columns, gram_ref[...], 0.0)
    coeffs = jnp.sum(gram * dots, axis=1, keepdims=True) * scale
    wide = jnp.broadcast_to(coeffs, (columns, cols))
    wide_ref[...] = wide
    coeff_row = to_row(coeffs)

    extra = comps * columns
    tail_a, tail_b = (rowa_ref[extra:, :], rowb_ref[extra:, :])
    north_tail, south_tail = (pick(even_row, tail_a, tail_b), pick(even_row, tail_b, tail_a))
    side_a, side_b = (cola_ref[...], colb_ref[...])
    east_side, west_side = (pick(even_col, side_a, side_b), pick(even_col, side_b, side_a))
    v_north, v_south = (north_tail[comps : comps + 1, :], south_tail[comps : comps + 1, :])
    v_north2, v_south2 = (north_tail[comps + 1 : comps + 2, :], south_tail[comps + 1 : comps + 2, :])
    v_east, v_west = (east_side[comps * rows :, 0:1], west_side[comps * rows :, 0:1])
    v_east2, v_west2 = (east_side[comps * rows :, 1:2], west_side[comps * rows :, 1:2])
    faces = [0.5 * (visc + v) for v in shifts(visc, v_north, v_south, v_east, v_west)]
    diagonal = 1.0 + faces[0] + faces[1] + faces[2] + faces[3]
    face_ref[...] = jnp.concatenate(faces + [diagonal], axis=0)
    jacobi = [m / diagonal + (1.0 - m) for m in mask]

    def corner(step_row, step_col, which):
        r, c = (at_row + step_row, at_col + step_col)
        inside = (r >= 0) & (r < row_count) & (c >= 0) & (c < col_count)
        place = jnp.where(inside, r * col_count + c, me)
        value = got_ref[place, 0:1, :]
        value = jnp.sum(jnp.where(lanes == columns + which, value, 0.0), axis=1, keepdims=True)
        return value * jnp.where(inside, 1.0, 0.0)

    north_west, north_east = (corner(1, -1, 1), corner(1, 1, 0))
    south_west, south_east = (corner(-1, -1, 3), corner(-1, 1, 2))

    def row_inverse(own, inner, outer, west, east):
        right = jnp.where(lanes == low, east, pltpu.roll(own, low, 1))
        left = jnp.where(lanes == 0, west, pltpu.roll(own, 1, 1))
        return 1.0 / (1.0 + 0.5 * (4.0 * own + inner + outer + left + right))

    def side_inverse(own, inner, outer, south, north):
        own = jnp.broadcast_to(own, (rows, cols))
        up = jnp.where(sub == top, north, pltpu.roll(own, top, 0))
        down = jnp.where(sub == 0, south, pltpu.roll(own, 1, 0))
        return 1.0 / (1.0 + 0.5 * (4.0 * own + inner + outer + up + down))

    inv_north = row_inverse(v_north, visc[top : top + 1, :], v_north2, north_west, north_east)
    inv_south = row_inverse(v_south, visc[0:1, :], v_south2, south_west, south_east)
    inv_east = side_inverse(v_east, visc[:, low : low + 1], v_east2, south_east, north_east)
    inv_west = side_inverse(v_west, visc[:, 0:1], v_west2, south_west, north_west)

    corr = combine(basis_ref, wide_ref, columns, comps, rows)
    image, scaled, smooth, point = ([], [], [], [])
    for c in range(comps):
        span = slice(c * columns, (c + 1) * columns)
        sum_a = jnp.sum(wide * rowa_ref[span, :], axis=0, keepdims=True)
        sum_b = jnp.sum(wide * rowb_ref[span, :], axis=0, keepdims=True)
        u_north = inv_north * north_tail[c : c + 1, :]
        u_south = inv_south * south_tail[c : c + 1, :]
        p_north = u_north + pick(even_row, sum_a, sum_b)
        p_south = u_south + pick(even_row, sum_b, sum_a)
        here = slice(c * rows, (c + 1) * rows)
        east, west = (east_side[here, :], west_side[here, :])
        u_east = inv_east * east[:, columns : columns + 1]
        u_west = inv_west * west[:, columns : columns + 1]
        p_east = u_east + jnp.sum(coeff_row * east, axis=1, keepdims=True)
        p_west = u_west + jnp.sum(coeff_row * west, axis=1, keepdims=True)
        u = jacobi[c] * rhs[c]
        p = u + corr[c]
        masked = mask[c] * p
        near = shifts(masked, p_north, p_south, p_east, p_west)
        stencil = diagonal * masked - (
            faces[0] * near[0] + faces[1] * near[1] + faces[2] * near[2] + faces[3] * near[3]
        )
        q = mask[c] * stencil + (1.0 - mask[c]) * p
        smooth.append(u)
        point.append(p)
        image.append(q)
        scaled.append(jacobi[c] * q)
        for i, value in enumerate((u_north, u_south, p_north, p_south)):
            edge_ref[i * 8 + c : i * 8 + c + 1, :] = value
        for i, value in enumerate((u_east, u_west, p_east, p_west)):
            side_ref[(i * comps + c) * rows : (i * comps + c + 1) * rows, :] = value
    state_ref[...] = jnp.concatenate(smooth + point + image + scaled, axis=0)

    row = to_row(project(basis_ref, image, acc_ref, columns, comps, rows))
    pairs = ((point, image), (smooth, image), (image, scaled), (rhs, smooth))
    for i, (left, right) in enumerate(pairs):
        value = left[0] * right[0]
        for c in range(1, comps):
            value = value + left[c] * right[c]
        row = jnp.where(lanes == DOTS + i, total(value), row)
    masked = [mask[c] * scaled[c] for c in range(comps)]
    east = jnp.concatenate([m[:, low : low + 1] for m in masked], axis=0)
    west = jnp.concatenate([m[:, 0:1] for m in masked], axis=0)
    row = row + to_row(east, EAST) + to_row(west, WEST)
    message = jnp.concatenate([row] + [m[top : top + 1, :] for m in masked], axis=0)
    send_ref[...] = jnp.broadcast_to(message[None], send_ref.shape)
    message = jnp.concatenate([row] + [m[0:1, :] for m in masked], axis=0)
    send_ref[jnp.where(at_row > 0, me - col_count, me)] = message
    small_ref[...] = jnp.concatenate([dots, coeff_row, jnp.zeros((6, cols), F32)], axis=0)


def second_kernel(sizes, got_ref, basis_ref, rhs_ref, mask_ref, rowa_ref, rowb_ref, cola_ref,
                  colb_ref, state_ref, face_ref, edge_ref, side_ref, small_ref, gram_ref,
                  send_ref, out_ref, last_ref, wide_ref):
    columns, comps, rows, cols, scale = sizes
    at_row, at_col = (lax.axis_index("row"), lax.axis_index("col"))
    row_count, col_count = (lax.axis_size("row"), lax.axis_size("col"))
    even_row, even_col = (1 - lax.rem(at_row, 2), 1 - lax.rem(at_col, 2))
    me = at_row * col_count + at_col
    lanes = iota((1, cols), 1)
    mask = [mask_ref[c * rows : (c + 1) * rows, :].astype(F32) for c in range(comps)]

    sums = jnp.sum(got_ref[...], axis=0)[0:1, :]
    image_dots = jnp.where(lanes < columns, sums, 0.0)
    curve, cross, image_sq, rhs_sq = [
        jnp.sum(jnp.where(lanes == DOTS + i, sums, 0.0), axis=1, keepdims=True) for i in range(4)
    ]
    dots, coeff_row = (small_ref[0:1, :], small_ref[1:2, :])
    energy = rhs_sq + jnp.sum(dots * coeff_row, axis=1, keepdims=True)
    step = energy / curve
    gram = jnp.where(iota((columns, cols), 1) < columns, gram_ref[...], 0.0)
    dots = dots - step * image_dots
    coeffs = jnp.sum(gram * dots, axis=1, keepdims=True) * scale
    wide = jnp.broadcast_to(coeffs, (columns, cols))
    wide_ref[...] = wide
    coeff_row = to_row(coeffs)
    energy_new = rhs_sq - 2.0 * step * cross + step * step * image_sq
    energy_new = energy_new + jnp.sum(dots * coeff_row, axis=1, keepdims=True)
    ratio = energy_new / energy

    def beside(step_row, step_col):
        r, c = (at_row + step_row, at_col + step_col)
        inside = (r >= 0) & (r < row_count) & (c >= 0) & (c < col_count)
        message = got_ref[jnp.where(inside, r * col_count + c, me)]
        return message * jnp.where(inside, 1.0, 0.0)

    q_north, q_south = (beside(1, 0), beside(-1, 0))
    q_east = to_column(beside(0, 1)[0:1, :], comps * rows, WEST)
    q_west = to_column(beside(0, -1)[0:1, :], comps * rows, EAST)

    side_a, side_b = (cola_ref[...], colb_ref[...])
    east_side, west_side = (pick(even_col, side_a, side_b), pick(even_col, side_b, side_a))
    faces = [face_ref[i * rows : (i + 1) * rows, :] for i in range(4)]
    diagonal = face_ref[4 * rows : 5 * rows, :]
    corr = combine(basis_ref, wide_ref, columns, comps, rows)
    curve_part = jnp.zeros((rows, cols), F32)
    first, second, third, fourth = ([], [], [], [])
    for c in range(comps):
        span = slice(c * columns, (c + 1) * columns)
        here = slice(c * rows, (c + 1) * rows)
        sum_a = jnp.sum(wide * rowa_ref[span, :], axis=0, keepdims=True)
        sum_b = jnp.sum(wide * rowb_ref[span, :], axis=0, keepdims=True)
        old = [edge_ref[i * 8 + c : i * 8 + c + 1, :] for i in range(4)]
        p_north = old[0] - step * q_north[1 + c : 2 + c, :] + pick(even_row, sum_a, sum_b)
        p_south = old[1] - step * q_south[1 + c : 2 + c, :] + pick(even_row, sum_b, sum_a)
        p_north, p_south = (p_north + ratio * old[2], p_south + ratio * old[3])
        old = [side_ref[(i * comps + c) * rows : (i * comps + c + 1) * rows, :] for i in range(4)]
        p_east = old[0] - step * q_east[here] + ratio * old[2]
        p_west = old[1] - step * q_west[here] + ratio * old[3]
        p_east = p_east + jnp.sum(coeff_row * east_side[here, :], axis=1, keepdims=True)
        p_west = p_west + jnp.sum(coeff_row * west_side[here, :], axis=1, keepdims=True)
        u, p, q, jq = [
            state_ref[(i * comps + c) * rows : (i * comps + c + 1) * rows, :] for i in range(4)
        ]
        new = u - step * jq + corr[c] + ratio * p
        masked = mask[c] * new
        near = shifts(masked, p_north, p_south, p_east, p_west)
        stencil = diagonal * masked - (
            faces[0] * near[0] + faces[1] * near[1] + faces[2] * near[2] + faces[3] * near[3]
        )
        applied = mask[c] * stencil + (1.0 - mask[c]) * new
        curve_part = curve_part + new * applied
        first.append(step * p)
        second.append(new)
        third.append(rhs_ref[here, :] - step * q)
        fourth.append(applied)
    out_ref[...] = jnp.concatenate(first + second + third + fourth, axis=0)
    last_ref[...] = jnp.broadcast_to(energy_new, last_ref.shape)
    send_ref[...] = jnp.broadcast_to(total(curve_part)[None], send_ref.shape)


def last_kernel(count, got_ref, in_ref, last_ref, solution_ref, residual_ref):
    step = last_ref[0:1, :] / jnp.sum(got_ref[...], axis=0)
    solution_ref[...] = in_ref[:count, :] + step * in_ref[count : 2 * count, :]
    residual_ref[...] = in_ref[2 * count : 3 * count, :] - step * in_ref[3 * count :, :]


def on_device(right_side, viscosity, free_mask, coarse_basis, gram_inverse):
    comps, rows, cols = right_side.shape
    columns = coarse_basis.shape[0]
    row_count, col_count = (lax.axis_size("row"), lax.axis_size("col"))
    devices = row_count * col_count
    scale = 1.0 / (32.0 * math.sqrt(float(comps * rows * cols * devices * columns)))
    sizes = (columns, comps, rows, cols)

    def call(kernel, outs, scratch, *args):
        return pl.pallas_call(
            kernel,
            out_shape=[jax.ShapeDtypeStruct(s, F32) for s in outs],
            in_specs=[VMEM] * len(args),
            out_specs=[VMEM] * len(outs),
            scratch_shapes=[pltpu.VMEM(s, F32) for s in scratch],
            compiler_params=pltpu.CompilerParams(vmem_limit_bytes=16 * 1024 * 1024),
        )(*args)

    def share(message):
        return lax.all_to_all(message, ("row", "col"), 0, 0, tiled=True)

    def swap(packet, axis, first):
        pairs = [(i, i + 1) for i in range(first, lax.axis_size(axis) - 1, 2)]
        return lax.ppermute(packet, axis, pairs + [(j, i) for i, j in pairs])

    basis = coarse_basis.reshape(columns * comps * rows, cols)
    rhs = right_side.reshape(comps * rows, cols)
    mask = free_mask.reshape(comps * rows, cols)

    block = gram_inverse.size
    piece = -(-block // row_count)
    flat = jnp.pad(gram_inverse.reshape(-1), (0, piece * row_count - block))
    own = lax.dynamic_slice_in_dim(flat, lax.axis_index("row") * piece, piece)
    own = jnp.pad(own, (0, cols - piece)).reshape(1, cols)

    tall = -(-(comps * columns + comps + 2) // 8) * 8
    wide = (comps + 1) * rows
    field = comps * rows
    send, row_a, row_b, col_a, col_b = call(
        functools.partial(pack_kernel, sizes),
        [(devices, 2, cols), (tall, cols), (tall, cols), (wide, cols), (wide, cols)],
        [(columns * rows, cols)],
        basis, rhs, mask, viscosity, own,
    )
    halos = (swap(row_a, "row", 0), swap(row_b, "row", 1), swap(col_a, "col", 0), swap(col_b, "col", 1))
    got = share(send)
    whole_rows = piece == cols and cols % columns == 0 and block == piece * row_count
    gram = ()
    if not whole_rows:
        gram = got[:, 1, :piece].reshape(row_count, col_count, piece).transpose(1, 0, 2)
        gram = gram.reshape(col_count, row_count * piece)[:, :block].reshape(columns, columns)
        gram = (gram,)
    sizes = sizes + (scale,)
    send, *state = call(
        functools.partial(first_kernel, sizes, whole_rows),
        [(devices, 1 + comps, cols), (4 * field, cols), (5 * rows, cols), (32, cols),
         (4 * field, cols), (8, cols), (columns, cols)],
        [(columns * rows, cols), (columns, cols)],
        got, *gram, basis, rhs, mask, viscosity, *halos,
    )
    send, fields, last = call(
        functools.partial(second_kernel, sizes),
        [(devices, 1, cols), (4 * field, cols), (8, cols)],
        [(columns, cols)],
        share(send), basis, rhs, mask, *halos, *state,
    )
    solution, residual = call(
        functools.partial(last_kernel, field),
        [(field, cols), (field, cols)],
        [],
        share(send), fields, last,
    )
    return (solution.reshape(right_side.shape), residual.reshape(right_side.shape))


def solution(mesh):
    in_specs = (
        P(None, "row", "col"),
        P("row", "col"),
        P(None, "row", "col"),
        P(None, None, "row", "col"),
        P("col", None),
    )
    out_specs = (P(None, "row", "col"), P(None, "row", "col"))
    return jax.shard_map(
        on_device, mesh=mesh, in_specs=in_specs, out_specs=out_specs, check_vma=False
    )
```

time: 199 us -> 44.3 us (0.22)
  blocking collectives: 141 us -> 19.9 us
  starting transfers between devices: 29.2 us -> 12.2 us
  between operations: 6.67 us -> 0.71 us
  waiting for transfers between devices: 10 us -> 6.28 us
  other arithmetic: 3.45 us -> 0 us
  local copies, waits for them, and re-layouts: 5.22 us -> 2 us
  Pallas kernels: 0 us -> 2.84 us
  matrix products: 2.83 us -> 0 us
    psum x3 -> x0, blocking collectives: 127 us -> none  [the longest x1 43 us: on_device(): curve_sum = lax.psum(jnp.sum(direction * applied), ('row', 'col'))]
    ppermute x12 -> x4, starting transfers between devices: 29.2 us -> 4.62 us  [swap(): return lax.ppermute(packet, axis, pairs + [(j, i) for i, j in pairs])]
    all_to_all x0 -> x2, blocking collectives: none -> 19.9 us  [share(): return lax.all_to_all(message, ('row', 'col'), 0, 0, tiled=True)]
    unnamed x2 -> x0, blocking collectives: 13.4 us -> none
    ppermute x12 -> x4, waiting for transfers between devices: 10 us -> 0.28 us  [swap(): return lax.ppermute(packet, axis, pairs + [(j, i) for i, j in pairs])]
    all_to_all x0 -> x1, starting transfers between devices: none -> 7.6 us  [share(): return lax.all_to_all(message, ('row', 'col'), 0, 0, tiled=True)]
    all_to_all x0 -> x1, waiting for transfers between devices: none -> 6 us  [share(): return lax.all_to_all(message, ('row', 'col'), 0, 0, tiled=True)]
    unnamed x19 -> x10, local copies, waits for them, and re-layouts: 4.22 us -> 1.15 us
  transfers between devices with their start and end apart: 12 -> 5, of which waited for: 5 -> 2; matrix products, arithmetic and copies ran while one was open for 2% -> 0% of each run, Pallas kernels for 0% -> 0%
where the time goes in v2:
time: 44.3 us; the launch traced here: 44 us
  blocking collectives  19.9 us (45%)
  starting transfers between devices  12.2 us (28%)
  waiting for transfers between devices  6.28 us (14%)
  Pallas kernels  2.84 us (6%)
  local copies, waits for them, and re-layouts  2 us (5%)
  between operations  0.71 us (2%)
    all_to_all x2, blocking collectives, share(): return lax.all_to_all(message, ('row', 'col'), 0, 0, tiled=True)  19.9 us
    all_to_all x1, starting transfers between devices, share(): return lax.all_to_all(message, ('row', 'col'), 0, 0, tiled=True)  7.6 us
    all_to_all x1, waiting for transfers between devices, share(): return lax.all_to_all(message, ('row', 'col'), 0, 0, tiled=True)  6 us
    ppermute x4, starting transfers between devices, swap(): return lax.ppermute(packet, axis, pairs + [(j, i) for i, j in pairs])  4.62 us
    pallas_call x4, Pallas kernels, call(): pl.pallas_call(kernel, out_shape=[jax.ShapeDtypeStruct(s, F32) for s in o...  2.84 us
    unnamed x10, local copies, waits for them, and re-layouts  1.15 us
  transfers between devices with their start and end apart: 5, of which 2 were waited for; matrix products, arithmetic and copies ran while one was open for 0% of the time, Pallas kernels for 0%

profile of v2, /device:TPU:0, one launch (start us, length us, event | category | flops | bytes accessed | tf_op | source)
XLA Modules:
  0.0 44.0 jit_solution(2428339324085242051)
XLA Ops:
  0.6 0.0 copy-start.4
  0.6 0.0 copy-start.3
  0.7 0.0 copy-start.2
  0.7 0.8 %reshape.28 = f32[1024]{0:T(1024)S(1)} reshape(f32[16,64]{1,0:T(8,128)} %param.9) | data formatting | bytes 8192 | tf_op jit(solution)/shard_map/reshape | solution.py:383
  1.4 0.1 dynamic-slice_bitcast_fusion.gram_ref
  1.5 0.0 copy-done.4
  1.5 0.0 copy-done.3
  1.5 0.0 copy-done.2
  1.5 0.0 copy-start
  1.5 1.1 %copy-done = f32[64,3,8,128]{3,2,1,0:T(8,128)S(1)} copy-done((f32[64,3,8,128]{3,2,1,0:T(8,128)S(1)}, f32[64,3,8,128]{3,2,1,0:T(8,128)}, u32[]{:S(2)}) %copy-start) | copy-done | bytes 786456
  2.7 0.0 copy-start.1
  2.7 1.2 %shard_map.68 = (f32[32,2,128]{2,1,0:T(2,128)}, f32[200,128]{1,0:T(8,128)S(1)}, f32[200,128]{1,0:T(8,128)S(1)}, f32[32,128]{1,0:T(8,128)S(1)}, f32[32,128]{1,0:T(8,128)S(1)}) custom-call(f32[1536,128]{1,0:T(8,128)S(1)} %bitcast.7, f32[24,128]{1,0:T(8,128)S(1)} %bitcast.10, s32[24,128]{1,0:T(8,128)S(1)} %bitcast.13, f32[8,128]{1,0:T(8,128)S(1)} %copy-done.4, ...), custom_call_target="tpu_custom_call" | custom-call | tf_op jit(solution)/shard_map/pallas_call | solution.py:361
  3.8 3.0 %collective-permute-start = (f32[200,128]{1,0:T(8,128)S(1)}, f32[200,128]{1,0:T(8,128)S(1)}, u32[]{:S(2)}, u32[]{:S(2)}) collective-permute-start(f32[200,128]{1,0:T(8,128)S(1)} %get-tuple-element.20), channel_id=1, source_target_pairs={{0,4},{8,12},{16,20},{24,28},{4,0},{12,8},{20,16},{28,24},{1,5},{9... | collective-permute-start | bytes 307208 | tf_op jit(solution)/shard_map/ppermute | solution.py:375
  6.8 0.7 %collective-permute-start.1 = (f32[200,128]{1,0:T(8,128)S(1)}, f32[200,128]{1,0:T(8,128)S(1)}, u32[]{:S(2)}, u32[]{:S(2)}) collective-permute-start(f32[200,128]{1,0:T(8,128)S(1)} %get-tuple-element.21), channel_id=1, source_target_pairs={{4,8},{12,16},{20,24},{8,4},{16,12},{24,20},{5,9},{13,17},{21,25},... | collective-permute-start | bytes 307208 | tf_op jit(solution)/shard_map/ppermute | solution.py:375
  7.5 7.6 %all-to-all-start = ((f32[32,2,128]{2,1,0:T(2,128)}), f32[32,2,128]{2,1,0:T(2,128)S(1)}, u32[]{:S(2)}, u32[]{:S(2)}) async-start(f32[32,2,128]{2,1,0:T(2,128)} %get-tuple-element.19), calls=%async_computation | async-start | bytes 65536 | tf_op jit(solution)/shard_map/all_to_all | solution.py:371
  15.1 0.3 collective-permute-start.2
  15.4 0.7 %collective-permute-start.3 = (f32[32,128]{1,0:T(8,128)S(1)}, f32[32,128]{1,0:T(8,128)S(1)}, u32[]{:S(2)}, u32[]{:S(2)}) collective-permute-start(f32[32,128]{1,0:T(8,128)S(1)} %get-tuple-element.23), channel_id=1, source_target_pairs={{1,2},{2,1},{5,6},{6,5},{9,10},{10,9},{13,14},{14,13},{17,18},{18,... | collective-permute-start | bytes 49160 | tf_op jit(solution)/shard_map/ppermute | solution.py:375
  16.1 0.3 collective-permute-done.2.refs_6_.cola_ref
  16.4 0.0 collective-permute-done.3.refs_7_.colb_ref
  16.4 6.0 %all-to-all-done.got_ref = f32[32,2,128]{2,1,0:T(2,128)S(1)} async-done(((f32[32,2,128]{2,1,0:T(2,128)}), f32[32,2,128]{2,1,0:T(2,128)S(1)}, u32[]{:S(2)}, u32[]{:S(2)}) %all-to-all-start) | async-done | bytes 32800 | tf_op jit(solution)/shard_map/all_to_all | solution.py:371
  22.4 0.0 collective-permute-done.refs_4_.rowa_ref
  22.4 0.0 collective-permute-done.1.refs_5_.rowb_ref
  22.4 0.0 copy-done.1
  22.4 0.6 %shard_map.69 = (f32[32,4,128]{2,1,0:T(4,128)S(1)}, f32[96,128]{1,0:T(8,128)S(1)}, f32[40,128]{1,0:T(8,128)S(1)}, f32[32,128]{1,0:T(8,128)S(1)}, f32[96,128]{1,0...) custom-call(f32[32,2,128]{2,1,0:T(2,128)S(1)} %all-to-all-done.got_ref, f32[1536,128]{1,0:T(8,128)S(1)} %bitcast.8, ...), custom_call_target="tpu_custom_call" | custom-call | tf_op jit(solution)/shard_map/pallas_call | solution.py:361
  22.9 11.0 %all_to_all.15.got_ref = f32[32,4,128]{2,1,0:T(4,128)S(1)} all-to-all(f32[32,4,128]{2,1,0:T(4,128)S(1)} %get-tuple-element.24), channel_id=1, replica_groups=mesh['row'=8,'col'=4] {'row','col'}, dimensions={0} | all-to-all | bytes 131072 | tf_op jit(solution)/shard_map/all_to_all | solution.py:371
  34.0 0.5 %shard_map.70 = (f32[32,1,128]{2,1,0:T(1,128)S(1)}, f32[96,128]{1,0:T(8,128)S(1)}, f32[8,128]{1,0:T(8,128)S(1)}) custom-call(f32[32,4,128]{2,1,0:T(4,128)S(1)} %all_to_all.15.got_ref, f32[1536,128]{1,0:T(8,128)S(1)} %bitcast.9, f32[24,128]{1,0:T(8,128)S(1)} %bitcast.12, s32[24,128]{1,0:T(8,128)S(1)} %bitcast.15, ...), custom_call_target="tpu_custom_call" | custom-call | tf_op jit(solution)/shard_map/pallas_call | solution.py:361
  34.5 8.9 %all_to_all.16.got_ref = f32[32,1,128]{2,1,0:T(1,128)S(1)} all-to-all(f32[32,1,128]{2,1,0:T(1,128)S(1)} %get-tuple-element.31), channel_id=1, replica_groups=mesh['row'=8,'col'=4] {'row','col'}, dimensions={0} | all-to-all | bytes 32768 | tf_op jit(solution)/shard_map/all_to_all | solution.py:371
  43.3 0.6 %shard_map.71 = (f32[24,128]{1,0:T(8,128)}, f32[24,128]{1,0:T(8,128)}) custom-call(f32[32,1,128]{2,1,0:T(1,128)S(1)} %all_to_all.16.got_ref, f32[96,128]{1,0:T(8,128)S(1)} %get-tuple-element.32.in_ref, f32[8,128]{1,0:T(8,128)S(1)} %get-tuple-element.33.last_ref), custom_call_target="tpu_custom_call" | custom-call | tf_op jit(solution)/shard_map/pallas_call | solution.py:361
Async XLA Ops:
  0.6 0.9 %copy-start.4 = (f32[8,128]{1,0:T(8,128)S(1)}, f32[8,128]{1,0:T(8,128)}, u32[]{:S(2)}) copy-start(f32[8,128]{1,0:T(8,128)} %refs_3_.1) | copy-start | bytes 12292
  0.6 0.9 %copy-start.3 = (s32[3,8,128]{2,1,0:T(8,128)S(1)}, s32[3,8,128]{2,1,0:T(8,128)}, u32[]{:S(2)}) copy-start(s32[3,8,128]{2,1,0:T(8,128)} %param.7) | copy-start | bytes 36868
  0.7 0.9 %copy-start.2 = (f32[3,8,128]{2,1,0:T(8,128)S(1)}, f32[3,8,128]{2,1,0:T(8,128)}, u32[]{:S(2)}) copy-start(f32[3,8,128]{2,1,0:T(8,128)} %param.5) | copy-start | bytes 36868
  1.5 1.1 %copy-start = (f32[64,3,8,128]{3,2,1,0:T(8,128)S(1)}, f32[64,3,8,128]{3,2,1,0:T(8,128)}, u32[]{:S(2)}) copy-start(f32[64,3,8,128]{3,2,1,0:T(8,128)} %param.8) | copy-start | bytes 2359300
  2.7 19.7 %copy-start.1 = (f32[64,3,8,128]{3,2,1,0:T(8,128)S(1)}, f32[64,3,8,128]{3,2,1,0:T(8,128)}, u32[]{:S(2)}) copy-start(f32[64,3,8,128]{3,2,1,0:T(8,128)} %param.8) | copy-start | bytes 2359300
  3.8 18.5 %collective-permute-start = (f32[200,128]{1,0:T(8,128)S(1)}, f32[200,128]{1,0:T(8,128)S(1)}, u32[]{:S(2)}, u32[]{:S(2)}) collective-permute-start(f32[200,128]{1,0:T(8,128)S(1)} %get-tuple-element.20), channel_id=1, source_target_pairs={{0,4},{8,12},{16,20},{24,28},{4,0},{12,8},{20,16},{28,24},{1,5},{9... | collective-permute-start | bytes 307208 | tf_op jit(solution)/shard_map/ppermute | solution.py:375
  6.8 15.5 %collective-permute-start.1 = (f32[200,128]{1,0:T(8,128)S(1)}, f32[200,128]{1,0:T(8,128)S(1)}, u32[]{:S(2)}, u32[]{:S(2)}) collective-permute-start(f32[200,128]{1,0:T(8,128)S(1)} %get-tuple-element.21), channel_id=1, source_target_pairs={{4,8},{12,16},{20,24},{8,4},{16,12},{24,20},{5,9},{13,17},{21,25},... | collective-permute-start | bytes 307208 | tf_op jit(solution)/shard_map/ppermute | solution.py:375
  7.5 14.9 %all-to-all-start = ((f32[32,2,128]{2,1,0:T(2,128)}), f32[32,2,128]{2,1,0:T(2,128)S(1)}, u32[]{:S(2)}, u32[]{:S(2)}) async-start(f32[32,2,128]{2,1,0:T(2,128)} %get-tuple-element.19), calls=%async_computation | async-start | bytes 65536 | tf_op jit(solution)/shard_map/all_to_all | solution.py:371
  15.1 1.2 %collective-permute-start.2 = (f32[32,128]{1,0:T(8,128)S(1)}, f32[32,128]{1,0:T(8,128)S(1)}, u32[]{:S(2)}, u32[]{:S(2)}) collective-permute-start(f32[32,128]{1,0:T(8,128)S(1)} %get-tuple-element.22), channel_id=1, source_target_pairs={{0,1},{2,3},{1,0},{3,2},{4,5},{6,7},{5,4},{7,6},{8,9},{10,11},{9,8... | collective-permute-start | bytes 49160 | tf_op jit(solution)/shard_map/ppermute | solution.py:375
  15.4 0.9 %collective-permute-start.3 = (f32[32,128]{1,0:T(8,128)S(1)}, f32[32,128]{1,0:T(8,128)S(1)}, u32[]{:S(2)}, u32[]{:S(2)}) collective-permute-start(f32[32,128]{1,0:T(8,128)S(1)} %get-tuple-element.23), channel_id=1, source_target_pairs={{1,2},{2,1},{5,6},{6,5},{9,10},{10,9},{13,14},{14,13},{17,18},{18,... | collective-permute-start | bytes 49160 | tf_op jit(solution)/shard_map/ppermute | solution.py:375

commit v3 on v2

--- a/solution.py
+++ b/solution.py
@@ -11,6 +11,17 @@
 F32 = jnp.float32
 VMEM = pl.BlockSpec(memory_space=pltpu.VMEM)
 DOTS, EAST, WEST = 64, 72, 96
+
+
+def flags():
+    at_row, at_col = (lax.axis_index("row"), lax.axis_index("col"))
+    tests = (
+        at_row < lax.axis_size("row") - 1,
+        at_row > 0,
+        at_col < lax.axis_size("col") - 1,
+        at_col > 0,
+    )
+    return [jnp.where(test, 1.0, 0.0) for test in tests]
 
 
 def iota(shape, dim):
@@ -172,9 +183,12 @@
 
     extra = comps * columns
     tail_a, tail_b = (rowa_ref[extra:, :], rowb_ref[extra:, :])
-    north_tail, south_tail = (pick(even_row, tail_a, tail_b), pick(even_row, tail_b, tail_a))
+    has_north, has_south, has_east, has_west = flags()
+    north_tail = pick(even_row, tail_a, tail_b) * has_north
+    south_tail = pick(even_row, tail_b, tail_a) * has_south
     side_a, side_b = (cola_ref[...], colb_ref[...])
-    east_side, west_side = (pick(even_col, side_a, side_b), pick(even_col, side_b, side_a))
+    east_side = pick(even_col, side_a, side_b) * has_east
+    west_side = pick(even_col, side_b, side_a) * has_west
     v_north, v_south = (north_tail[comps : comps + 1, :], south_tail[comps : comps + 1, :])
     v_north2, v_south2 = (north_tail[comps + 1 : comps + 2, :], south_tail[comps + 1 : comps + 2, :])
     v_east, v_west = (east_side[comps * rows :, 0:1], west_side[comps * rows :, 0:1])
@@ -219,8 +233,8 @@
         sum_b = jnp.sum(wide * rowb_ref[span, :], axis=0, keepdims=True)
         u_north = inv_north * north_tail[c : c + 1, :]
         u_south = inv_south * south_tail[c : c + 1, :]
-        p_north = u_north + pick(even_row, sum_a, sum_b)
-        p_south = u_south + pick(even_row, sum_b, sum_a)
+        p_north = u_north + has_north * pick(even_row, sum_a, sum_b)
+        p_south = u_south + has_south * pick(even_row, sum_b, sum_a)
         here = slice(c * rows, (c + 1) * rows)
         east, west = (east_side[here, :], west_side[here, :])
         u_east = inv_east * east[:, columns : columns + 1]
@@ -303,7 +317,9 @@
     q_west = to_column(beside(0, -1)[0:1, :], comps * rows, EAST)
 
     side_a, side_b = (cola_ref[...], colb_ref[...])
-    east_side, west_side = (pick(even_col, side_a, side_b), pick(even_col, side_b, side_a))
+    has_north, has_south, has_east, has_west = flags()
+    east_side = pick(even_col, side_a, side_b) * has_east
+    west_side = pick(even_col, side_b, side_a) * has_west
     faces = [face_ref[i * rows : (i + 1) * rows, :] for i in range(4)]
     diagonal = face_ref[4 * rows : 5 * rows, :]
     corr = combine(basis_ref, wide_ref, columns, comps, rows)
@@ -315,8 +331,8 @@
         sum_a = jnp.sum(wide * rowa_ref[span, :], axis=0, keepdims=True)
         sum_b = jnp.sum(wide * rowb_ref[span, :], axis=0, keepdims=True)
         old = [edge_ref[i * 8 + c : i * 8 + c + 1, :] for i in range(4)]
-        p_north = old[0] - step * q_north[1 + c : 2 + c, :] + pick(even_row, sum_a, sum_b)
-        p_south = old[1] - step * q_south[1 + c : 2 + c, :] + pick(even_row, sum_b, sum_a)
+        p_north = old[0] - step * q_north[1 + c : 2 + c, :] + has_north * pick(even_row, sum_a, sum_b)
+        p_south = old[1] - step * q_south[1 + c : 2 + c, :] + has_south * pick(even_row, sum_b, sum_a)
         p_north, p_south = (p_north + ratio * old[2], p_south + ratio * old[3])
         old = [side_ref[(i * comps + c) * rows : (i * comps + c + 1) * rows, :] for i in range(4)]
         p_east = old[0] - step * q_east[here] + ratio * old[2]
@@ -371,7 +387,10 @@
         return lax.all_to_all(message, ("row", "col"), 0, 0, tiled=True)
 
     def swap(packet, axis, first):
-        pairs = [(i, i + 1) for i in range(first, lax.axis_size(axis) - 1, 2)]
+        count = lax.axis_size(axis)
+        pairs = [(i, i + 1) for i in range(first, count - 1, 2)]
+        if first == 1 and count > 2 and count % 2 == 0:
+            pairs.append((0, count - 1))
         return lax.ppermute(packet, axis, pairs + [(j, i) for i, j in pairs])
 
     basis = coarse_basis.reshape(columns * comps * rows, cols)

time: 44.3 us -> 40.4 us (0.912)
  blocking collectives: 19.9 us -> 18 us
  waiting for transfers between devices: 6.28 us -> 5.31 us
  starting transfers between devices: 12.2 us -> 11.3 us
    all_to_all x1, starting transfers between devices: 7.6 us -> 2.81 us  [share(): return lax.all_to_all(message, ('row', 'col'), 0, 0, tiled=True)]
    ppermute x4, starting transfers between devices: 4.62 us -> 8.49 us  [swap(): return lax.ppermute(packet, axis, pairs + [(j, i) for i, j in pairs])]
    all_to_all x1, waiting for transfers between devices: 6 us -> 3.73 us  [share(): return lax.all_to_all(message, ('row', 'col'), 0, 0, tiled=True)]
    all_to_all x2, blocking collectives: 19.9 us -> 18 us  [share(): return lax.all_to_all(message, ('row', 'col'), 0, 0, tiled=True)]
    ppermute x4, waiting for transfers between devices: 0.28 us -> 1.58 us  [swap(): return lax.ppermute(packet, axis, pairs + [(j, i) for i, j in pairs])]
where the time goes in v3:
time: 40.4 us; the launch traced here: 40.2 us
  blocking collectives  18 us (45%)
  starting transfers between devices  11.3 us (28%)
  waiting for transfers between devices  5.31 us (13%)
  Pallas kernels  2.84 us (7%)
  local copies, waits for them, and re-layouts  2 us (5%)
  between operations  0.7 us (2%)
    all_to_all x2, blocking collectives, share(): return lax.all_to_all(message, ('row', 'col'), 0, 0, tiled=True)  18 us
    ppermute x4, starting transfers between devices, swap(): return lax.ppermute(packet, axis, pairs + [(j, i) for i, j in pairs])  8.49 us
    all_to_all x1, waiting for transfers between devices, share(): return lax.all_to_all(message, ('row', 'col'), 0, 0, tiled=True)  3.73 us
    pallas_call x4, Pallas kernels, call(): pl.pallas_call(kernel, out_shape=[jax.ShapeDtypeStruct(s, F32) for s in o...  2.84 us
    all_to_all x1, starting transfers between devices, share(): return lax.all_to_all(message, ('row', 'col'), 0, 0, tiled=True)  2.81 us
    ppermute x4, waiting for transfers between devices, swap(): return lax.ppermute(packet, axis, pairs + [(j, i) for i, j in pairs])  1.58 us
    unnamed x10, local copies, waits for them, and re-layouts  1.15 us
  transfers between devices with their start and end apart: 5, of which 2 were waited for; matrix products, arithmetic and copies ran while one was open for 0% of the time, Pallas kernels for 0%

profile of v3, /device:TPU:0, one launch (start us, length us, event | category | flops | bytes accessed | tf_op | source)
XLA Modules:
  0.0 40.2 jit_solution(5181544598675858653)
XLA Ops:
  0.6 0.0 copy-start.4
  0.6 0.0 copy-start.3
  0.7 0.0 copy-start.2
  0.7 0.8 %reshape.28 = f32[1024]{0:T(1024)S(1)} reshape(f32[16,64]{1,0:T(8,128)} %param.9) | data formatting | bytes 8192 | tf_op jit(solution)/shard_map/reshape | solution.py:402
  1.4 0.1 dynamic-slice_bitcast_fusion.gram_ref
  1.5 0.0 copy-done.4
  1.5 0.0 copy-done.3
  1.5 0.0 copy-done.2
  1.5 0.0 copy-start
  1.5 1.1 %copy-done = f32[64,3,8,128]{3,2,1,0:T(8,128)S(1)} copy-done((f32[64,3,8,128]{3,2,1,0:T(8,128)S(1)}, f32[64,3,8,128]{3,2,1,0:T(8,128)}, u32[]{:S(2)}) %copy-start) | copy-done | bytes 786456
  2.7 0.0 copy-start.1
  2.7 1.2 %shard_map.68 = (f32[32,2,128]{2,1,0:T(2,128)}, f32[200,128]{1,0:T(8,128)S(1)}, f32[200,128]{1,0:T(8,128)S(1)}, f32[32,128]{1,0:T(8,128)S(1)}, f32[32,128]{1,0:T(8,128)S(1)}) custom-call(f32[1536,128]{1,0:T(8,128)S(1)} %bitcast.7, f32[24,128]{1,0:T(8,128)S(1)} %bitcast.10, s32[24,128]{1,0:T(8,128)S(1)} %bitcast.13, f32[8,128]{1,0:T(8,128)S(1)} %copy-done.4, ...), custom_call_target="tpu_custom_call" | custom-call | tf_op jit(solution)/shard_map/pallas_call | solution.py:377
  3.8 3.0 %collective-permute-start = (f32[200,128]{1,0:T(8,128)S(1)}, f32[200,128]{1,0:T(8,128)S(1)}, u32[]{:S(2)}, u32[]{:S(2)}) collective-permute-start(f32[200,128]{1,0:T(8,128)S(1)} %get-tuple-element.20), channel_id=1, source_target_pairs={{0,4},{8,12},{16,20},{24,28},{4,0},{12,8},{20,16},{28,24},{1,5},{9... | collective-permute-start | bytes 307208 | tf_op jit(solution)/shard_map/ppermute | solution.py:394
  6.8 3.5 %collective-permute-start.1 = (f32[200,128]{1,0:T(8,128)S(1)}, f32[200,128]{1,0:T(8,128)S(1)}, u32[]{:S(2)}, u32[]{:S(2)}) collective-permute-start(f32[200,128]{1,0:T(8,128)S(1)} %get-tuple-element.21), channel_id=1, source_target_pairs={{4,8},{12,16},{20,24},{0,28},{8,4},{16,12},{24,20},{28,0},{5,9},{1... | collective-permute-start | bytes 307208 | tf_op jit(solution)/shard_map/ppermute | solution.py:394
  10.4 2.8 %all-to-all-start = ((f32[32,2,128]{2,1,0:T(2,128)}), f32[32,2,128]{2,1,0:T(2,128)S(1)}, u32[]{:S(2)}, u32[]{:S(2)}) async-start(f32[32,2,128]{2,1,0:T(2,128)} %get-tuple-element.19), calls=%async_computation | async-start | bytes 65536 | tf_op jit(solution)/shard_map/all_to_all | solution.py:387
  13.2 0.3 collective-permute-start.2
  13.5 1.6 %collective-permute-start.3 = (f32[32,128]{1,0:T(8,128)S(1)}, f32[32,128]{1,0:T(8,128)S(1)}, u32[]{:S(2)}, u32[]{:S(2)}) collective-permute-start(f32[32,128]{1,0:T(8,128)S(1)} %get-tuple-element.23), channel_id=1, source_target_pairs={{1,2},{0,3},{2,1},{3,0},{5,6},{4,7},{6,5},{7,4},{9,10},{8,11},{10,... | collective-permute-start | bytes 49160 | tf_op jit(solution)/shard_map/ppermute | solution.py:394
  15.1 0.0 collective-permute-done.2.refs_6_.cola_ref
  15.1 1.6 %collective-permute-done.3.refs_7_.colb_ref = f32[32,128]{1,0:T(8,128)S(1)} collective-permute-done((f32[32,128]{1,0:T(8,128)S(1)}, f32[32,128]{1,0:T(8,128)S(1)}, u32[]{:S(2)}, u32[]{:S(2)}) %collective-permute-start.3) | collective-permute-done | bytes 16416 | tf_op jit(solution)/shard_map/ppermute | solution.py:394
  16.7 3.7 %all-to-all-done.got_ref = f32[32,2,128]{2,1,0:T(2,128)S(1)} async-done(((f32[32,2,128]{2,1,0:T(2,128)}), f32[32,2,128]{2,1,0:T(2,128)S(1)}, u32[]{:S(2)}, u32[]{:S(2)}) %all-to-all-start) | async-done | bytes 32800 | tf_op jit(solution)/shard_map/all_to_all | solution.py:387
  20.5 0.0 collective-permute-done.refs_4_.rowa_ref
  20.5 0.0 collective-permute-done.1.refs_5_.rowb_ref
  20.5 0.0 copy-done.1
  20.5 0.6 %shard_map.69 = (f32[32,4,128]{2,1,0:T(4,128)S(1)}, f32[96,128]{1,0:T(8,128)S(1)}, f32[40,128]{1,0:T(8,128)S(1)}, f32[32,128]{1,0:T(8,128)S(1)}, f32[96,128]{1,0...) custom-call(f32[32,2,128]{2,1,0:T(2,128)S(1)} %all-to-all-done.got_ref, f32[1536,128]{1,0:T(8,128)S(1)} %bitcast.8, ...), custom_call_target="tpu_custom_call" | custom-call | tf_op jit(solution)/shard_map/pallas_call | solution.py:377
  21.0 9.2 %all_to_all.15.got_ref = f32[32,4,128]{2,1,0:T(4,128)S(1)} all-to-all(f32[32,4,128]{2,1,0:T(4,128)S(1)} %get-tuple-element.24), channel_id=1, replica_groups=mesh['row'=8,'col'=4] {'row','col'}, dimensions={0} | all-to-all | bytes 131072 | tf_op jit(solution)/shard_map/all_to_all | solution.py:387
  30.2 0.5 %shard_map.70 = (f32[32,1,128]{2,1,0:T(1,128)S(1)}, f32[96,128]{1,0:T(8,128)S(1)}, f32[8,128]{1,0:T(8,128)S(1)}) custom-call(f32[32,4,128]{2,1,0:T(4,128)S(1)} %all_to_all.15.got_ref, f32[1536,128]{1,0:T(8,128)S(1)} %bitcast.9, f32[24,128]{1,0:T(8,128)S(1)} %bitcast.12, s32[24,128]{1,0:T(8,128)S(1)} %bitcast.15, ...), custom_call_target="tpu_custom_call" | custom-call | tf_op jit(solution)/shard_map/pallas_call | solution.py:377
  30.7 8.9 %all_to_all.16.got_ref = f32[32,1,128]{2,1,0:T(1,128)S(1)} all-to-all(f32[32,1,128]{2,1,0:T(1,128)S(1)} %get-tuple-element.31), channel_id=1, replica_groups=mesh['row'=8,'col'=4] {'row','col'}, dimensions={0} | all-to-all | bytes 32768 | tf_op jit(solution)/shard_map/all_to_all | solution.py:387
  39.5 0.6 %shard_map.71 = (f32[24,128]{1,0:T(8,128)}, f32[24,128]{1,0:T(8,128)}) custom-call(f32[32,1,128]{2,1,0:T(1,128)S(1)} %all_to_all.16.got_ref, f32[96,128]{1,0:T(8,128)S(1)} %get-tuple-element.32.in_ref, f32[8,128]{1,0:T(8,128)S(1)} %get-tuple-element.33.last_ref), custom_call_target="tpu_custom_call" | custom-call | tf_op jit(solution)/shard_map/pallas_call | solution.py:377
Async XLA Ops:
  0.6 0.9 %copy-start.4 = (f32[8,128]{1,0:T(8,128)S(1)}, f32[8,128]{1,0:T(8,128)}, u32[]{:S(2)}) copy-start(f32[8,128]{1,0:T(8,128)} %refs_3_.1) | copy-start | bytes 12292
  0.6 0.9 %copy-start.3 = (s32[3,8,128]{2,1,0:T(8,128)S(1)}, s32[3,8,128]{2,1,0:T(8,128)}, u32[]{:S(2)}) copy-start(s32[3,8,128]{2,1,0:T(8,128)} %param.7) | copy-start | bytes 36868
  0.7 0.9 %copy-start.2 = (f32[3,8,128]{2,1,0:T(8,128)S(1)}, f32[3,8,128]{2,1,0:T(8,128)}, u32[]{:S(2)}) copy-start(f32[3,8,128]{2,1,0:T(8,128)} %param.5) | copy-start | bytes 36868
  1.5 1.1 %copy-start = (f32[64,3,8,128]{3,2,1,0:T(8,128)S(1)}, f32[64,3,8,128]{3,2,1,0:T(8,128)}, u32[]{:S(2)}) copy-start(f32[64,3,8,128]{3,2,1,0:T(8,128)} %param.8) | copy-start | bytes 2359300
  2.7 17.8 %copy-start.1 = (f32[64,3,8,128]{3,2,1,0:T(8,128)S(1)}, f32[64,3,8,128]{3,2,1,0:T(8,128)}, u32[]{:S(2)}) copy-start(f32[64,3,8,128]{3,2,1,0:T(8,128)} %param.8) | copy-start | bytes 2359300
  3.8 16.6 %collective-permute-start = (f32[200,128]{1,0:T(8,128)S(1)}, f32[200,128]{1,0:T(8,128)S(1)}, u32[]{:S(2)}, u32[]{:S(2)}) collective-permute-start(f32[200,128]{1,0:T(8,128)S(1)} %get-tuple-element.20), channel_id=1, source_target_pairs={{0,4},{8,12},{16,20},{24,28},{4,0},{12,8},{20,16},{28,24},{1,5},{9... | collective-permute-start | bytes 307208 | tf_op jit(solution)/shard_map/ppermute | solution.py:394
  6.8 13.6 %collective-permute-start.1 = (f32[200,128]{1,0:T(8,128)S(1)}, f32[200,128]{1,0:T(8,128)S(1)}, u32[]{:S(2)}, u32[]{:S(2)}) collective-permute-start(f32[200,128]{1,0:T(8,128)S(1)} %get-tuple-element.21), channel_id=1, source_target_pairs={{4,8},{12,16},{20,24},{0,28},{8,4},{16,12},{24,20},{28,0},{5,9},{1... | collective-permute-start | bytes 307208 | tf_op jit(solution)/shard_map/ppermute | solution.py:394
  10.4 10.1 %all-to-all-start = ((f32[32,2,128]{2,1,0:T(2,128)}), f32[32,2,128]{2,1,0:T(2,128)S(1)}, u32[]{:S(2)}, u32[]{:S(2)}) async-start(f32[32,2,128]{2,1,0:T(2,128)} %get-tuple-element.19), calls=%async_computation | async-start | bytes 65536 | tf_op jit(solution)/shard_map/all_to_all | solution.py:387
  13.2 2.0 %collective-permute-start.2 = (f32[32,128]{1,0:T(8,128)S(1)}, f32[32,128]{1,0:T(8,128)S(1)}, u32[]{:S(2)}, u32[]{:S(2)}) collective-permute-start(f32[32,128]{1,0:T(8,128)S(1)} %get-tuple-element.22), channel_id=1, source_target_pairs={{0,1},{2,3},{1,0},{3,2},{4,5},{6,7},{5,4},{7,6},{8,9},{10,11},{9,8... | collective-permute-start | bytes 49160 | tf_op jit(solution)/shard_map/ppermute | solution.py:394
  13.5 3.2 %collective-permute-start.3 = (f32[32,128]{1,0:T(8,128)S(1)}, f32[32,128]{1,0:T(8,128)S(1)}, u32[]{:S(2)}, u32[]{:S(2)}) collective-permute-start(f32[32,128]{1,0:T(8,128)S(1)} %get-tuple-element.23), channel_id=1, source_target_pairs={{1,2},{0,3},{2,1},{3,0},{5,6},{4,7},{6,5},{7,4},{9,10},{8,11},{10,... | collective-permute-start | bytes 49160 | tf_op jit(solution)/shard_map/ppermute | solution.py:394

commit v4 on v3

--- a/solution.py
+++ b/solution.py
@@ -11,6 +11,7 @@
 F32 = jnp.float32
 VMEM = pl.BlockSpec(memory_space=pltpu.VMEM)
 DOTS, EAST, WEST = 64, 72, 96
+EAST2, WEST2, DOTS2 = 64, 88, 112
 
 
 def flags():
@@ -86,6 +87,26 @@
 
 def pack_kernel(sizes, basis_ref, rhs_ref, mask_ref, visc_ref, gram_ref,
                 send_ref, rowa_ref, rowb_ref, cola_ref, colb_ref, acc_ref):
+    columns, comps, rows, cols = sizes
+    packet_kernel(sizes, basis_ref, rhs_ref, mask_ref, visc_ref, rowa_ref, rowb_ref, cola_ref, colb_ref)
+    rhs = [rhs_ref[c * rows : (c + 1) * rows, :] for c in range(comps)]
+    visc = visc_ref[...]
+
+    row = to_row(project(basis_ref, rhs, acc_ref, columns, comps, rows))
+    lanes = iota((1, cols), 1)
+    for i, corner in enumerate(corners_of(visc)):
+        row = jnp.where(lanes == columns + i, corner, row)
+    both = jnp.concatenate([row, gram_ref[...]], axis=0)
+    send_ref[...] = jnp.broadcast_to(both[None], send_ref.shape)
+
+
+def corners_of(visc):
+    top, low = (visc.shape[0] - 1, visc.shape[1] - 1)
+    return [visc[i : i + 1, j : j + 1] for i in (0, top) for j in (0, low)]
+
+
+def packet_kernel(sizes, basis_ref, rhs_ref, mask_ref, visc_ref,
+                  rowa_ref, rowb_ref, cola_ref, colb_ref):
     columns, comps, rows, cols = sizes
     even_row = 1 - lax.rem(lax.axis_index("row"), 2)
     even_col = 1 - lax.rem(lax.axis_index("col"), 2)
@@ -133,16 +154,108 @@
     cola_ref[comps * rows :, :] = pick(even_col, east, west)
     colb_ref[comps * rows :, :] = pick(even_col, west, east)
 
-    row = to_row(project(basis_ref, rhs, acc_ref, columns, comps, rows))
-    lanes = iota((1, cols), 1)
-    corners = [visc[i : i + 1, j : j + 1] for i in (0, top) for j in (0, low)]
-    for i, corner in enumerate(corners):
-        row = jnp.where(lanes == columns + i, corner, row)
-    both = jnp.concatenate([row, gram_ref[...]], axis=0)
-    send_ref[...] = jnp.broadcast_to(both[None], send_ref.shape)
-
-
-def first_kernel(sizes, whole_rows, got_ref, *refs):
+
+def stencil(mask, faces, diagonal, tile, halo):
+    masked = mask * tile
+    near = shifts(masked, *halo)
+    inner = diagonal * masked - (
+        faces[0] * near[0] + faces[1] * near[1] + faces[2] * near[2] + faces[3] * near[3]
+    )
+    return mask * inner + (1.0 - mask) * tile
+
+
+def split(values):
+    high = values.astype(jnp.bfloat16)
+    return jnp.concatenate([high, (values - high.astype(F32)).astype(jnp.bfloat16)], axis=0)
+
+
+def gram_kernel(sizes, basis_ref, rhs_ref, mask_ref, visc_ref, gram_ref, rowa_ref, rowb_ref,
+                cola_ref, colb_ref, owna_ref, ownb_ref, send_ref, acc_ref, full_ref):
+    columns, comps, rows, cols = sizes
+    at_row, at_col = (lax.axis_index("row"), lax.axis_index("col"))
+    even_row, even_col = (1 - lax.rem(at_row, 2), 1 - lax.rem(at_col, 2))
+    has_north, has_south, has_east, has_west = flags()
+    top, low, half = (rows - 1, cols - 1, cols // 2)
+    rhs = [rhs_ref[c * rows : (c + 1) * rows, :] for c in range(comps)]
+    mask = [mask_ref[c * rows : (c + 1) * rows, :].astype(F32) for c in range(comps)]
+    visc = visc_ref[...]
+    lane, lanes = (iota((rows, cols), 1), iota((1, cols), 1))
+
+    at = comps * columns + comps
+    tail_a, tail_b = (rowa_ref[at : at + 1, :], rowb_ref[at : at + 1, :])
+    v_north = pick(even_row, tail_a, tail_b) * has_north
+    v_south = pick(even_row, tail_b, tail_a) * has_south
+    side_a, side_b = (cola_ref[...], colb_ref[...])
+    east_side = pick(even_col, side_a, side_b) * has_east
+    west_side = pick(even_col, side_b, side_a) * has_west
+    own_a, own_b = (owna_ref[...], ownb_ref[...])
+    own_east, own_west = (pick(even_col, own_a, own_b), pick(even_col, own_b, own_a))
+    v_east, v_west = (east_side[comps * rows :, 0:1], west_side[comps * rows :, 0:1])
+    faces = [0.5 * (visc + v) for v in shifts(visc, v_north, v_south, v_east, v_west)]
+    diagonal = 1.0 + faces[0] + faces[1] + faces[2] + faces[3]
+
+    blocks = jnp.zeros((2 * columns, 2 * columns), F32)
+    for c in range(comps):
+        m = mask[c]
+        own = m * diagonal + (1.0 - m)
+        up, down = (m * faces[0], m * faces[1])
+        right = jnp.where(lane == low, 0.0, m * faces[2])
+        left = jnp.where(lane == 0, 0.0, m * faces[3])
+        span = slice(c * columns, (c + 1) * columns)
+        halo_a, halo_b = (rowa_ref[span, :], rowb_ref[span, :])
+        plain = [
+            basis_ref[pl.ds(c * rows + i, columns, stride=comps * rows), :] for i in range(rows)
+        ]
+        free = [plain[i] * m[i : i + 1, :] for i in range(rows)]
+        free.append(pick(even_row, halo_a, halo_b) * has_north)
+        free.append(pick(even_row, halo_b, halo_a) * has_south)
+        for i in range(0, rows, 2):
+            lefts, rights = ([], [])
+            for j in (i, i + 1):
+                here = slice(j, j + 1)
+                value = own[here] * plain[j] - up[here] * free[j + 1] - down[here] * free[j - 1]
+                value = value - right[here] * pltpu.roll(free[j], low, 1)
+                value = value - left[here] * pltpu.roll(free[j], 1, 1)
+                lefts.append(split(plain[j]))
+                rights.append(split(value))
+            blocks = blocks + lax.dot_general(
+                jnp.concatenate(lefts, axis=1),
+                jnp.concatenate(rights, axis=1),
+                (((1,), (1,)), ((), ())),
+                preferred_element_type=F32,
+            )
+    east_face = jnp.concatenate([faces[2][:, low : low + 1]] * comps, axis=0)
+    west_face = jnp.concatenate([faces[3][:, 0:1]] * comps, axis=0)
+    field = comps * rows
+    ours = jnp.concatenate([own_east[:field] * east_face, own_west[:field] * west_face], axis=0)
+    theirs = jnp.concatenate([east_side[:field], west_side[:field]], axis=0)
+    edge = lax.dot_general(
+        ours, theirs, (((0,), (0,)), ((), ())),
+        preferred_element_type=F32, precision=lax.Precision.HIGHEST,
+    )
+    blocks = blocks + pltpu.roll(blocks, half, 1)
+    wide_lane = iota((columns, cols), 1)
+    edge = jnp.where(wide_lane < half, edge[:columns], 0.0)
+    full = blocks[:columns] + blocks[columns:] - edge - pltpu.roll(edge, half, 1)
+    full_ref[...] = full
+    spot = jnp.where(wide_lane >= half, wide_lane - half, wide_lane) == iota((columns, cols), 0)
+    spine = jnp.sum(jnp.where(spot, full, 0.0), axis=0, keepdims=True)
+    count = columns // 2
+    chunk = jnp.where(
+        iota((count, cols), 1) < half,
+        full_ref[pl.ds(0, count, stride=2), :],
+        full_ref[pl.ds(1, count, stride=2), :],
+    )
+    dots = to_row(project(basis_ref, rhs, acc_ref, columns, comps, rows))
+    corner_row = jnp.zeros((1, cols), F32)
+    for i, corner in enumerate(corners_of(visc)):
+        corner_row = jnp.where(lanes == i, corner, corner_row)
+    head = jnp.concatenate([jnp.where(lanes < half, dots, spine), gram_ref[...]], axis=0)
+    for d in range(count):
+        send_ref[d] = jnp.concatenate([head, chunk[d : d + 1, :], corner_row], axis=0)
+
+
+def first_kernel(sizes, whole_rows, two, got_ref, *refs):
     columns, comps, rows, cols, scale = sizes
     if whole_rows:
         gram_in_ref = None
@@ -173,7 +286,8 @@
                     gram_ref[at : at + 1, :] = moved
     else:
         gram_ref[:, :columns] = gram_in_ref[...]
-    sums = jnp.sum(got_ref[...], axis=0)[0:1, :]
+    all_sums = jnp.sum(got_ref[...], axis=0)
+    sums = all_sums[0:1, :]
     dots = jnp.where(lanes < columns, sums, 0.0)
     gram = jnp.where(iota((columns, cols), 1) < columns, gram_ref[...], 0.0)
     coeffs = jnp.sum(gram * dots, axis=1, keepdims=True) * scale
@@ -202,8 +316,9 @@
         r, c = (at_row + step_row, at_col + step_col)
         inside = (r >= 0) & (r < row_count) & (c >= 0) & (c < col_count)
         place = jnp.where(inside, r * col_count + c, me)
-        value = got_ref[place, 0:1, :]
-        value = jnp.sum(jnp.where(lanes == columns + which, value, 0.0), axis=1, keepdims=True)
+        line, first = (3, 0) if two else (0, columns)
+        value = got_ref[place, line : line + 1, :]
+        value = jnp.sum(jnp.where(lanes == first + which, value, 0.0), axis=1, keepdims=True)
         return value * jnp.where(inside, 1.0, 0.0)
 
     north_west, north_east = (corner(1, -1, 1), corner(1, 1, 0))
@@ -227,6 +342,8 @@
 
     corr = combine(basis_ref, wide_ref, columns, comps, rows)
     image, scaled, smooth, point = ([], [], [], [])
+    smooth_image, scaled_image = ([], [])
+    none = (jnp.zeros((1, cols), F32),) * 2 + (jnp.zeros((rows, 1), F32),) * 2
     for c in range(comps):
         span = slice(c * columns, (c + 1) * columns)
         sum_a = jnp.sum(wide * rowa_ref[span, :], axis=0, keepdims=True)
@@ -243,12 +360,11 @@
         p_west = u_west + jnp.sum(coeff_row * west, axis=1, keepdims=True)
         u = jacobi[c] * rhs[c]
         p = u + corr[c]
-        masked = mask[c] * p
-        near = shifts(masked, p_north, p_south, p_east, p_west)
-        stencil = diagonal * masked - (
-            faces[0] * near[0] + faces[1] * near[1] + faces[2] * near[2] + faces[3] * near[3]
-        )
-        q = mask[c] * stencil + (1.0 - mask[c]) * p
+        q = stencil(mask[c], faces, diagonal, p, (p_north, p_south, p_east, p_west))
+        if two:
+            halo = (u_north, u_south, u_east, u_west)
+            smooth_image.append(stencil(mask[c], faces, diagonal, u, halo))
+            scaled_image.append(stencil(mask[c], faces, diagonal, jacobi[c] * q, none))
         smooth.append(u)
         point.append(p)
         image.append(q)
@@ -261,12 +377,49 @@
 
     row = to_row(project(basis_ref, image, acc_ref, columns, comps, rows))
     pairs = ((point, image), (smooth, image), (image, scaled), (rhs, smooth))
+    if two:
+        pairs += ((smooth, smooth_image), (scaled, smooth_image), (scaled, scaled_image))
     for i, (left, right) in enumerate(pairs):
         value = left[0] * right[0]
         for c in range(1, comps):
             value = value + left[c] * right[c]
-        row = jnp.where(lanes == DOTS + i, total(value), row)
+        row = jnp.where(lanes == (DOTS2 if two else DOTS) + i, total(value), row)
     masked = [mask[c] * scaled[c] for c in range(comps)]
+    if two:
+        norths = [m[top : top + 1, :] * faces[0][top : top + 1, :] * has_north for m in masked]
+        easts = [m[:, low : low + 1] * faces[2][:, low : low + 1] * has_east for m in masked]
+        souths, wests = ([m[0:1, :] for m in masked], [m[:, 0:1] for m in masked])
+        row = row + to_row(jnp.concatenate(easts, axis=0), EAST2)
+        row = row + to_row(jnp.concatenate(wests, axis=0), WEST2)
+        reach = project(basis_ref, scaled_image, acc_ref, columns, comps, rows)
+        beyond = jnp.zeros((columns, cols), F32)
+        aside = jnp.zeros((rows, cols), F32)
+        for c in range(comps):
+            span, here = (slice(c * columns, (c + 1) * columns), slice(c * rows, (c + 1) * rows))
+            halo_a, halo_b = (rowa_ref[span, :], rowb_ref[span, :])
+            low_side = souths[c] * faces[1][0:1, :] * has_south
+            beyond = beyond + norths[c] * pick(even_row, halo_a, halo_b)
+            beyond = beyond + low_side * pick(even_row, halo_b, halo_a)
+            aside = aside + easts[c] * east_side[here, :]
+            aside = aside + wests[c] * faces[3][:, 0:1] * west_side[here, :]
+        reach = to_row(reach - jnp.sum(beyond, axis=1, keepdims=True))
+        reach = reach - jnp.where(lanes < columns, jnp.sum(aside, axis=0, keepdims=True), 0.0)
+        half = cols // 2
+        ours = jnp.broadcast_to(all_sums[2:3, :], (8, cols))
+        other = pltpu.roll(ours, half, 1)
+        wide_lane = iota((8, cols), 1)
+        for t, (first, second) in enumerate(((ours, other), (other, ours))):
+            value = jnp.where(wide_lane < half, first, second)
+            turn = lax.rem(half + t * (half // 2) - (2 * me + t + 1) + 2 * cols, cols)
+            value = pltpu.roll(value, turn, 1)[0:1, :]
+            start = half + t * (half // 2)
+            reach = jnp.where((lanes >= start) & (lanes < start + half // 2), value, reach)
+        message = jnp.concatenate(norths + souths + [row, reach], axis=0)
+        send_ref[...] = jnp.broadcast_to(message[None], send_ref.shape)
+        spine = pltpu.roll(jnp.broadcast_to(sums, (8, cols)), half, 1)[0:1, :]
+        spine = jnp.where(lanes < half, spine, 0.0)
+        small_ref[...] = jnp.concatenate([dots, coeff_row, spine, jnp.zeros((5, cols), F32)], axis=0)
+        return
     east = jnp.concatenate([m[:, low : low + 1] for m in masked], axis=0)
     west = jnp.concatenate([m[:, 0:1] for m in masked], axis=0)
     row = row + to_row(east, EAST) + to_row(west, WEST)
@@ -359,6 +512,118 @@
     send_ref[...] = jnp.broadcast_to(total(curve_part)[None], send_ref.shape)
 
 
+def close_kernel(sizes, got_ref, basis_ref, rhs_ref, mask_ref, rowa_ref, rowb_ref, cola_ref,
+                 colb_ref, state_ref, face_ref, edge_ref, side_ref, small_ref, gram_ref,
+                 solution_ref, residual_ref, wide_ref):
+    columns, comps, rows, cols, scale = sizes
+    at_row, at_col = (lax.axis_index("row"), lax.axis_index("col"))
+    row_count, col_count = (lax.axis_size("row"), lax.axis_size("col"))
+    devices = row_count * col_count
+    even_row, even_col = (1 - lax.rem(at_row, 2), 1 - lax.rem(at_col, 2))
+    has_north, has_south, has_east, has_west = flags()
+    me = at_row * col_count + at_col
+    half, quarter = (cols // 2, cols // 4)
+    lanes = iota((1, cols), 1)
+    mask = [mask_ref[c * rows : (c + 1) * rows, :].astype(F32) for c in range(comps)]
+
+    def along(left, right):
+        return jnp.sum(left * right, axis=1, keepdims=True)
+
+    sums = jnp.sum(got_ref[...], axis=0)
+    image_dots = jnp.where(lanes < columns, sums[2 * comps : 2 * comps + 1, :], 0.0)
+    reach_dots = jnp.where(lanes < columns, sums[2 * comps + 1 :, :], 0.0)
+    curve, cross, image_sq, rhs_sq, smooth_sq, mixed, scaled_sq = [
+        along(jnp.where(lanes == DOTS2 + i, 1.0, 0.0), sums[2 * comps : 2 * comps + 1, :])
+        for i in range(7)
+    ]
+    dots, old_row, spine = (small_ref[0:1, :], small_ref[1:2, :], small_ref[2:3, :])
+    energy = rhs_sq + along(dots, old_row)
+    step = energy / curve
+    gram = jnp.where(iota((columns, cols), 1) < columns, gram_ref[...], 0.0)
+    dots = dots - step * image_dots
+    coeffs = jnp.sum(gram * dots, axis=1, keepdims=True) * scale
+    wide = jnp.broadcast_to(coeffs, (columns, cols))
+    wide_ref[...] = wide
+    coeff_row = to_row(coeffs)
+    energy_new = rhs_sq - 2.0 * step * cross + step * step * image_sq + along(dots, coeff_row)
+    ratio = energy_new / energy
+
+    border = jnp.zeros((2 * comps + 2, cols), F32)
+    for d in range(devices - col_count):
+        border = border + got_ref[d] * pltpu.roll(got_ref[d + col_count], comps + 2, 0)
+    border = jnp.where(iota(border.shape, 0) < comps, border, 0.0)
+    lines = got_ref[:, 2 * comps, :]
+    later = pltpu.roll(pltpu.roll(lines, devices - 1, 0), cols - (WEST2 - EAST2), 1)
+    line_lane = iota(lines.shape, 1)
+    beside_it = jnp.where((line_lane >= EAST2) & (line_lane < WEST2), lines * later, 0.0)
+    scaled_sq = scaled_sq - 2.0 * (total(border) + total(beside_it))
+
+    packed = pltpu.roll(got_ref[:, 2 * comps + 1, :], half, 1)
+    sub = iota(packed.shape, 0)
+
+    def turned(row):
+        value = jnp.broadcast_to(row, (8, cols))
+        value = jnp.broadcast_to((value + pltpu.roll(value, half, 1))[0:1, :], packed.shape)
+        bit = 1
+        while bit < devices:
+            value = jnp.where((sub & bit) != 0, pltpu.roll(value, cols - 2 * bit, 1), value)
+            bit *= 2
+        ahead = pltpu.roll(value, cols - 1, 1)
+        ahead = jnp.where(line_lane < quarter, ahead, pltpu.roll(value, quarter - 2, 1))
+        return (jnp.where(line_lane < quarter, value[:, 0:1], value[:, 1:2]), ahead)
+
+    other_row = coeff_row - 2.0 * old_row
+    (left, left_ahead), (right, right_ahead) = (turned(coeff_row), turned(other_row))
+    weight = jnp.where((line_lane == quarter - 1) | (line_lane == half - 1), 0.5, 1.0)
+    form = packed * weight * (left * right_ahead + right * left_ahead)
+    form = total(jnp.where(line_lane < half, form, 0.0)) + along(spine * coeff_row, other_row)
+    image_part = along(coeff_row, image_dots)
+    curve_new = smooth_sq - 2.0 * step * mixed + step * step * scaled_sq
+    curve_new = curve_new - 2.0 * step * along(coeff_row, reach_dots) + 2.0 * image_part + form
+    curve_new = curve_new + 2.0 * ratio * (cross - step * image_sq + image_part)
+    curve_new = curve_new + ratio * ratio * curve
+    step_new = energy_new / curve_new
+
+    def beside(step_row, step_col):
+        r, c = (at_row + step_row, at_col + step_col)
+        inside = (r >= 0) & (r < row_count) & (c >= 0) & (c < col_count)
+        message = got_ref[jnp.where(inside, r * col_count + c, me)]
+        return message * jnp.where(inside, 1.0, 0.0)
+
+    faces = [face_ref[i * rows : (i + 1) * rows, :] for i in range(4)]
+    diagonal = face_ref[4 * rows : 5 * rows, :]
+    q_north, q_south = (beside(1, 0), beside(-1, 0))
+    q_east = to_column(beside(0, 1)[2 * comps : 2 * comps + 1, :], comps * rows, WEST2)
+    q_west = to_column(beside(0, -1)[2 * comps : 2 * comps + 1, :], comps * rows, EAST2)
+
+    side_a, side_b = (cola_ref[...], colb_ref[...])
+    east_side = pick(even_col, side_a, side_b) * has_east
+    west_side = pick(even_col, side_b, side_a) * has_west
+    corr = combine(basis_ref, wide_ref, columns, comps, rows)
+    for c in range(comps):
+        span = slice(c * columns, (c + 1) * columns)
+        here = slice(c * rows, (c + 1) * rows)
+        sum_a = jnp.sum(wide * rowa_ref[span, :], axis=0, keepdims=True)
+        sum_b = jnp.sum(wide * rowb_ref[span, :], axis=0, keepdims=True)
+        old = [edge_ref[i * 8 + c : i * 8 + c + 1, :] for i in range(4)]
+        p_north = old[0] - step * q_north[comps + c : comps + c + 1, :]
+        p_south = old[1] - step * (q_south[c : c + 1, :] / faces[1][0:1, :])
+        p_north = p_north + has_north * pick(even_row, sum_a, sum_b) + ratio * old[2]
+        p_south = p_south + has_south * pick(even_row, sum_b, sum_a) + ratio * old[3]
+        old = [side_ref[(i * comps + c) * rows : (i * comps + c + 1) * rows, :] for i in range(4)]
+        p_east = old[0] - step * q_east[here] + ratio * old[2]
+        p_west = old[1] - step * (q_west[here] / faces[3][:, 0:1]) + ratio * old[3]
+        p_east = p_east + jnp.sum(coeff_row * east_side[here, :], axis=1, keepdims=True)
+        p_west = p_west + jnp.sum(coeff_row * west_side[here, :], axis=1, keepdims=True)
+        u, p, q, jq = [
+            state_ref[(i * comps + c) * rows : (i * comps + c + 1) * rows, :] for i in range(4)
+        ]
+        new = u - step * jq + corr[c] + ratio * p
+        applied = stencil(mask[c], faces, diagonal, new, (p_north, p_south, p_east, p_west))
+        solution_ref[here, :] = step * p + step_new * new
+        residual_ref[here, :] = rhs_ref[here, :] - step * q - step_new * applied
+
+
 def last_kernel(count, got_ref, in_ref, last_ref, solution_ref, residual_ref):
     step = last_ref[0:1, :] / jnp.sum(got_ref[...], axis=0)
     solution_ref[...] = in_ref[:count, :] + step * in_ref[count : 2 * count, :]
@@ -406,6 +671,36 @@
     tall = -(-(comps * columns + comps + 2) // 8) * 8
     wide = (comps + 1) * rows
     field = comps * rows
+    two = columns * columns == devices * cols and cols == 2 * columns and rows == 8 and comps == 3
+    if two:
+        row_a, row_b, col_a, col_b = call(
+            functools.partial(packet_kernel, sizes),
+            [(tall, cols), (tall, cols), (wide, cols), (wide, cols)],
+            [],
+            basis, rhs, mask, viscosity,
+        )
+        halos = swap(row_a, "row", 0), swap(row_b, "row", 1), swap(col_a, "col", 0), swap(col_b, "col", 1)
+        (send,) = call(
+            functools.partial(gram_kernel, sizes),
+            [(devices, 4, cols)],
+            [(columns * rows, cols), (columns, cols)],
+            basis, rhs, mask, viscosity, own, *halos, col_a, col_b,
+        )
+        sizes = sizes + (scale,)
+        send, *state = call(
+            functools.partial(first_kernel, sizes, True, True),
+            [(devices, 8, cols), (4 * field, cols), (5 * rows, cols), (32, cols),
+             (4 * field, cols), (8, cols), (columns, cols)],
+            [(columns * rows, cols), (columns, cols)],
+            share(send), basis, rhs, mask, viscosity, *halos,
+        )
+        solution, residual = call(
+            functools.partial(close_kernel, sizes),
+            [(field, cols), (field, cols)],
+            [(columns, cols)],
+            share(send), basis, rhs, mask, *halos, *state,
+        )
+        return (solution.reshape(right_side.shape), residual.reshape(right_side.shape))
     send, row_a, row_b, col_a, col_b = call(
         functools.partial(pack_kernel, sizes),
         [(devices, 2, cols), (tall, cols), (tall, cols), (wide, cols), (wide, cols)],
@@ -422,7 +717,7 @@
         gram = (gram,)
     sizes = sizes + (scale,)
     send, *state = call(
-        functools.partial(first_kernel, sizes, whole_rows),
+        functools.partial(first_kernel, sizes, whole_rows, False),
         [(devices, 1 + comps, cols), (4 * field, cols), (5 * rows, cols), (32, cols),
          (4 * field, cols), (8, cols), (columns, cols)],
         [(columns * rows, cols), (columns, cols)],

time: 40.4 us -> 41 us (1.015)
  starting transfers between devices: 11.3 us -> 8.21 us
  blocking collectives: 18 us -> 21 us
  waiting for transfers between devices: 5.31 us -> 3.66 us
  local copies, waits for them, and re-layouts: 2 us -> 3.39 us
  Pallas kernels: 2.84 us -> 3.71 us
    all_to_all x1 -> x0, waiting for transfers between devices: 3.73 us -> none  [share(): return lax.all_to_all(message, ('row', 'col'), 0, 0, tiled=True)]
    all_to_all x2, blocking collectives: 18 us -> 21 us  [share(): return lax.all_to_all(message, ('row', 'col'), 0, 0, tiled=True)]
    all_to_all x1 -> x0, starting transfers between devices: 2.81 us -> none  [share(): return lax.all_to_all(message, ('row', 'col'), 0, 0, tiled=True)]
    unnamed x10 -> x16, local copies, waits for them, and re-layouts: 1.15 us -> 3.24 us
    ppermute x4, waiting for transfers between devices: 1.58 us -> 3.66 us  [swap(): return lax.ppermute(packet, axis, pairs + [(j, i) for i, j in pairs])]
    pallas_call x4, Pallas kernels: 2.84 us -> 3.71 us  [call(): pl.pallas_call(kernel, out_shape=[jax.ShapeDtypeStruct(s, F32) for s in o...]
    reshape x1, local copies, waits for them, and re-layouts: 0.78 us -> 0.07 us  [on_device(): flat = jnp.pad(gram_inverse.reshape(-1), (0, piece * row_count - block))]
  transfers between devices with their start and end apart: 5 -> 4, of which waited for: 2 -> 2; matrix products, arithmetic and copies ran while one was open for 0% -> 0% of each run, Pallas kernels for 0% -> 0%
where the time goes in v4:
time: 41 us; the launch traced here: 40.7 us
  blocking collectives  21 us (51%)
  starting transfers between devices  8.21 us (20%)
  Pallas kernels  3.71 us (9%)
  waiting for transfers between devices  3.66 us (9%)
  local copies, waits for them, and re-layouts  3.39 us (8%)
  between operations  0.67 us (2%)
    all_to_all x2, blocking collectives, share(): return lax.all_to_all(message, ('row', 'col'), 0, 0, tiled=True)  21 us
    ppermute x4, starting transfers between devices, swap(): return lax.ppermute(packet, axis, pairs + [(j, i) for i, j in pairs])  8.21 us
    pallas_call x4, Pallas kernels, call(): pl.pallas_call(kernel, out_shape=[jax.ShapeDtypeStruct(s, F32) for s in o...  3.71 us
    ppermute x4, waiting for transfers between devices, swap(): return lax.ppermute(packet, axis, pairs + [(j, i) for i, j in pairs])  3.66 us
    unnamed x16, local copies, waits for them, and re-layouts  3.24 us
  transfers between devices with their start and end apart: 4, of which 2 were waited for; matrix products, arithmetic and copies ran while one was open for 0% of the time, Pallas kernels for 0%

profile of v4, /device:TPU:0, one launch (start us, length us, event | category | flops | bytes accessed | tf_op | source)
XLA Modules:
  0.0 40.7 jit_solution(298577918241930962)
XLA Ops:
  0.6 0.0 copy-start.6
  0.6 0.7 %copy-done.6 = f32[8,128]{1,0:T(8,128)S(1)} copy-done((f32[8,128]{1,0:T(8,128)S(1)}, f32[8,128]{1,0:T(8,128)}, u32[]{:S(2)}) %copy-start.6) | copy-done | bytes 4120
  1.3 0.0 copy-start
  1.3 1.1 %copy-done = f32[64,3,8,128]{3,2,1,0:T(8,128)S(1)} copy-done((f32[64,3,8,128]{3,2,1,0:T(8,128)S(1)}, f32[64,3,8,128]{3,2,1,0:T(8,128)}, u32[]{:S(2)}) %copy-start) | copy-done | bytes 786456
  2.5 0.0 copy-start.2
  2.5 0.7 %copy-done.2 = f32[3,8,128]{2,1,0:T(8,128)S(1)} copy-done((f32[3,8,128]{2,1,0:T(8,128)S(1)}, f32[3,8,128]{2,1,0:T(8,128)}, u32[]{:S(2)}) %copy-start.2) | copy-done | bytes 12312
  3.2 0.0 copy-start.4
  3.2 0.7 %copy-done.4 = s32[3,8,128]{2,1,0:T(8,128)S(1)} copy-done((s32[3,8,128]{2,1,0:T(8,128)S(1)}, s32[3,8,128]{2,1,0:T(8,128)}, u32[]{:S(2)}) %copy-start.4) | copy-done | bytes 12312
  3.9 0.0 copy-start.1
  3.9 0.5 %shard_map.68 = (f32[200,128]{1,0:T(8,128)S(1)}, f32[200,128]{1,0:T(8,128)S(1)}, f32[32,128]{1,0:T(8,128)S(1)}, f32[32,128]{1,0:T(8,128)S(1)}) custom-call(f32[1536,128]{1,0:T(8,128)S(1)} %bitcast.7, f32[24,128]{1,0:T(8,128)S(1)} %bitcast.11, s32[24,128]{1,0:T(8,128)S(1)} %bitcast.15, f32[8,128]{1,0:T(8,128)S(1)} %copy-done.6), custom_call_target="tpu_custom_call" | custom-call | tf_op jit(solution)/shard_map/pallas_call | solution.py:642
  4.4 0.6 %collective-permute-start.2 = (f32[32,128]{1,0:T(8,128)S(1)}, f32[32,128]{1,0:T(8,128)S(1)}, u32[]{:S(2)}, u32[]{:S(2)}) collective-permute-start(f32[32,128]{1,0:T(8,128)S(1)} %get-tuple-element.17.owna_ref), channel_id=1, source_target_pairs={{0,1},{2,3},{1,0},{3,2},{4,5},{6,7},{5,4},{7,6},{8,9},{10,11},{9,8... | collective-permute-start | bytes 49160 | tf_op jit(solution)/shard_map/ppermute | solution.py:659
  4.9 2.6 %collective-permute-start.3 = (f32[32,128]{1,0:T(8,128)S(1)}, f32[32,128]{1,0:T(8,128)S(1)}, u32[]{:S(2)}, u32[]{:S(2)}) collective-permute-start(f32[32,128]{1,0:T(8,128)S(1)} %get-tuple-element.18.ownb_ref), channel_id=1, source_target_pairs={{1,2},{0,3},{2,1},{3,0},{5,6},{4,7},{6,5},{7,4},{9,10},{8,11},{10,... | collective-permute-start | bytes 49160 | tf_op jit(solution)/shard_map/ppermute | solution.py:659
  7.5 0.0 copy-start.7
  7.5 1.5 %collective-permute-start = (f32[200,128]{1,0:T(8,128)S(1)}, f32[200,128]{1,0:T(8,128)S(1)}, u32[]{:S(2)}, u32[]{:S(2)}) collective-permute-start(f32[200,128]{1,0:T(8,128)S(1)} %get-tuple-element.15), channel_id=1, source_target_pairs={{0,4},{8,12},{16,20},{24,28},{4,0},{12,8},{20,16},{28,24},{1,5},{9... | collective-permute-start | bytes 307208 | tf_op jit(solution)/shard_map/ppermute | solution.py:659
  9.0 3.5 %collective-permute-start.1 = (f32[200,128]{1,0:T(8,128)S(1)}, f32[200,128]{1,0:T(8,128)S(1)}, u32[]{:S(2)}, u32[]{:S(2)}) collective-permute-start(f32[200,128]{1,0:T(8,128)S(1)} %get-tuple-element.16), channel_id=1, source_target_pairs={{4,8},{12,16},{20,24},{0,28},{8,4},{16,12},{24,20},{28,0},{5,9},{1... | collective-permute-start | bytes 307208 | tf_op jit(solution)/shard_map/ppermute | solution.py:659
  12.6 0.0 copy-start.5
  12.6 0.0 copy-start.3
  12.6 0.0 copy-done.7
  12.6 0.1 reshape.28
  12.7 0.1 dynamic-slice_bitcast_fusion.gram_ref
  12.7 0.0 collective-permute-done.2.cola_ref.refs_6_
  12.7 0.0 collective-permute-done.3.colb_ref.refs_7_
  12.7 0.9 %collective-permute-done.rowa_ref.refs_4_ = f32[200,128]{1,0:T(8,128)S(1)} collective-permute-done((f32[200,128]{1,0:T(8,128)S(1)}, f32[200,128]{1,0:T(8,128)S(1)}, u32[]{:S(2)}, u32[]{:S(2)}) %collective-permute-start) | collective-permute-done | bytes 102432 | tf_op jit(solution)/shard_map/ppermute | solution.py:659
  13.6 2.8 %collective-permute-done.1.rowb_ref.refs_5_ = f32[200,128]{1,0:T(8,128)S(1)} collective-permute-done((f32[200,128]{1,0:T(8,128)S(1)}, f32[200,128]{1,0:T(8,128)S(1)}, u32[]{:S(2)}, u32[]{:S(2)}) %collective-permute-start.1) | collective-permute-done | bytes 102432 | tf_op jit(solution)/shard_map/ppermute | solution.py:659
  16.4 0.0 copy-done.1
  16.4 0.0 copy-done.5
  16.4 0.0 copy-done.3
  16.4 1.0 %shard_map.69 = f32[32,4,128]{2,1,0:T(4,128)S(1)} custom-call(f32[1536,128]{1,0:T(8,128)S(1)} %bitcast.8, f32[24,128]{1,0:T(8,128)S(1)} %bitcast.12, s32[24,128]{1,0:T(8,128)S(1)} %bitcast.16, f32[8,128]{1,0:T(8,128)S(1)} %copy-done.6, f32[1,128]{1,0:T(1,128)S(1)} %dynamic-slice_bitcast_fusion.gram_ref, ...), custom_call_target="tpu_custom_call" | custom-call | tf_op jit(solution)/shard_map/pallas_call | solution.py:642
  17.4 11.1 %all_to_all.10.got_ref = f32[32,4,128]{2,1,0:T(4,128)S(1)} all-to-all(f32[32,4,128]{2,1,0:T(4,128)S(1)} %shard_map.69), channel_id=1, replica_groups=mesh['row'=8,'col'=4] {'row','col'}, dimensions={0} | all-to-all | bytes 131072 | tf_op jit(solution)/shard_map/all_to_all | solution.py:652
  28.6 0.7 %shard_map.70 = (f32[32,8,128]{2,1,0:T(8,128)S(1)}, f32[96,128]{1,0:T(8,128)S(1)}, f32[40,128]{1,0:T(8,128)S(1)}, f32[32,128]{1,0:T(8,128)S(1)}, f32[96,128]{1,0...) custom-call(f32[32,4,128]{2,1,0:T(4,128)S(1)} %all_to_all.10.got_ref, f32[1536,128]{1,0:T(8,128)S(1)} %bitcast.9, ...), custom_call_target="tpu_custom_call" | custom-call | tf_op jit(solution)/shard_map/pallas_call | solution.py:642
  29.2 9.9 %all_to_all.11.got_ref = f32[32,8,128]{2,1,0:T(8,128)S(1)} all-to-all(f32[32,8,128]{2,1,0:T(8,128)S(1)} %get-tuple-element.19), channel_id=1, replica_groups=mesh['row'=8,'col'=4] {'row','col'}, dimensions={0} | all-to-all | bytes 262144 | tf_op jit(solution)/shard_map/all_to_all | solution.py:652
  39.1 1.5 %shard_map.71 = (f32[24,128]{1,0:T(8,128)}, f32[24,128]{1,0:T(8,128)}) custom-call(f32[32,8,128]{2,1,0:T(8,128)S(1)} %all_to_all.11.got_ref, f32[1536,128]{1,0:T(8,128)S(1)} %bitcast.10, f32[24,128]{1,0:T(8,128)S(1)} %bitcast.14, s32[24,128]{1,0:T(8,128)S(1)} %bitcast.18, f32[200,128]{1,0:T(8,128)S(1)} %collective-permute-done.rowa_ref.refs_4_, ...), custom_call_target="tpu_custom_call" | custom-call | tf_op jit(solution)/shard_map/pallas_call | solution.py:642
Async XLA Ops:
  0.6 0.7 %copy-start.6 = (f32[8,128]{1,0:T(8,128)S(1)}, f32[8,128]{1,0:T(8,128)}, u32[]{:S(2)}) copy-start(f32[8,128]{1,0:T(8,128)} %refs_3_.1) | copy-start | bytes 12292
  1.3 1.1 %copy-start = (f32[64,3,8,128]{3,2,1,0:T(8,128)S(1)}, f32[64,3,8,128]{3,2,1,0:T(8,128)}, u32[]{:S(2)}) copy-start(f32[64,3,8,128]{3,2,1,0:T(8,128)} %param.8) | copy-start | bytes 2359300
  2.5 0.7 %copy-start.2 = (f32[3,8,128]{2,1,0:T(8,128)S(1)}, f32[3,8,128]{2,1,0:T(8,128)}, u32[]{:S(2)}) copy-start(f32[3,8,128]{2,1,0:T(8,128)} %param.5) | copy-start | bytes 36868
  3.2 0.7 %copy-start.4 = (s32[3,8,128]{2,1,0:T(8,128)S(1)}, s32[3,8,128]{2,1,0:T(8,128)}, u32[]{:S(2)}) copy-start(s32[3,8,128]{2,1,0:T(8,128)} %param.7) | copy-start | bytes 36868
  3.9 12.5 %copy-start.1 = (f32[64,3,8,128]{3,2,1,0:T(8,128)S(1)}, f32[64,3,8,128]{3,2,1,0:T(8,128)}, u32[]{:S(2)}) copy-start(f32[64,3,8,128]{3,2,1,0:T(8,128)} %param.8) | copy-start | bytes 2359300
  4.4 8.4 %collective-permute-start.2 = (f32[32,128]{1,0:T(8,128)S(1)}, f32[32,128]{1,0:T(8,128)S(1)}, u32[]{:S(2)}, u32[]{:S(2)}) collective-permute-start(f32[32,128]{1,0:T(8,128)S(1)} %get-tuple-element.17.owna_ref), channel_id=1, source_target_pairs={{0,1},{2,3},{1,0},{3,2},{4,5},{6,7},{5,4},{7,6},{8,9},{10,11},{9,8... | collective-permute-start | bytes 49160 | tf_op jit(solution)/shard_map/ppermute | solution.py:659
  4.9 7.8 %collective-permute-start.3 = (f32[32,128]{1,0:T(8,128)S(1)}, f32[32,128]{1,0:T(8,128)S(1)}, u32[]{:S(2)}, u32[]{:S(2)}) collective-permute-start(f32[32,128]{1,0:T(8,128)S(1)} %get-tuple-element.18.ownb_ref), channel_id=1, source_target_pairs={{1,2},{0,3},{2,1},{3,0},{5,6},{4,7},{6,5},{7,4},{9,10},{8,11},{10,... | collective-permute-start | bytes 49160 | tf_op jit(solution)/shard_map/ppermute | solution.py:659
  7.5 5.1 %copy-start.7 = (f32[16,64]{1,0:T(8,128)S(1)}, f32[16,64]{1,0:T(8,128)}, u32[]{:S(2)}) copy-start(f32[16,64]{1,0:T(8,128)} %param.9) | copy-start | bytes 12292
  7.5 6.1 %collective-permute-start = (f32[200,128]{1,0:T(8,128)S(1)}, f32[200,128]{1,0:T(8,128)S(1)}, u32[]{:S(2)}, u32[]{:S(2)}) collective-permute-start(f32[200,128]{1,0:T(8,128)S(1)} %get-tuple-element.15), channel_id=1, source_target_pairs={{0,4},{8,12},{16,20},{24,28},{4,0},{12,8},{20,16},{28,24},{1,5},{9... | collective-permute-start | bytes 307208 | tf_op jit(solution)/shard_map/ppermute | solution.py:659
  9.0 7.4 %collective-permute-start.1 = (f32[200,128]{1,0:T(8,128)S(1)}, f32[200,128]{1,0:T(8,128)S(1)}, u32[]{:S(2)}, u32[]{:S(2)}) collective-permute-start(f32[200,128]{1,0:T(8,128)S(1)} %get-tuple-element.16), channel_id=1, source_target_pairs={{4,8},{12,16},{20,24},{0,28},{8,4},{16,12},{24,20},{28,0},{5,9},{1... | collective-permute-start | bytes 307208 | tf_op jit(solution)/shard_map/ppermute | solution.py:659
  12.6 3.8 %copy-start.5 = (s32[3,8,128]{2,1,0:T(8,128)S(1)}, s32[3,8,128]{2,1,0:T(8,128)}, u32[]{:S(2)}) copy-start(s32[3,8,128]{2,1,0:T(8,128)} %param.7) | copy-start | bytes 36868
  12.6 3.8 %copy-start.3 = (f32[3,8,128]{2,1,0:T(8,128)S(1)}, f32[3,8,128]{2,1,0:T(8,128)}, u32[]{:S(2)}) copy-start(f32[3,8,128]{2,1,0:T(8,128)} %param.5) | copy-start | bytes 36868

commit v5 on v4

--- a/solution.py
+++ b/solution.py
@@ -7,6 +7,7 @@
 from jax.experimental import pallas as pl
 from jax.experimental.pallas import tpu as pltpu
 from jax.sharding import PartitionSpec as P
+
 
 F32 = jnp.float32
 VMEM = pl.BlockSpec(memory_space=pltpu.VMEM)
@@ -98,6 +99,16 @@
         row = jnp.where(lanes == columns + i, corner, row)
     both = jnp.concatenate([row, gram_ref[...]], axis=0)
     send_ref[...] = jnp.broadcast_to(both[None], send_ref.shape)
+
+
+def piece_kernel(gram_ref, piece_ref):
+    at = 2 * lax.axis_index("row")
+    rows = [gram_ref[pl.ds(at + t, 1), :] for t in range(2)]
+    piece_ref[...] = jnp.concatenate(rows, axis=1)
+
+
+def packets_kernel(sizes, basis_ref, rhs_ref, mask_ref, visc_ref, first_ref, *packet_refs):
+    packet_kernel(sizes, basis_ref, rhs_ref, mask_ref, visc_ref, *packet_refs)
 
 
 def corners_of(visc):
@@ -175,7 +186,7 @@
     at_row, at_col = (lax.axis_index("row"), lax.axis_index("col"))
     even_row, even_col = (1 - lax.rem(at_row, 2), 1 - lax.rem(at_col, 2))
     has_north, has_south, has_east, has_west = flags()
-    top, low, half = (rows - 1, cols - 1, cols // 2)
+    low, half = (cols - 1, cols // 2)
     rhs = [rhs_ref[c * rows : (c + 1) * rows, :] for c in range(comps)]
     mask = [mask_ref[c * rows : (c + 1) * rows, :].astype(F32) for c in range(comps)]
     visc = visc_ref[...]
@@ -638,13 +649,15 @@
     scale = 1.0 / (32.0 * math.sqrt(float(comps * rows * cols * devices * columns)))
     sizes = (columns, comps, rows, cols)
 
-    def call(kernel, outs, scratch, *args):
+    def call(kernel, outs, scratch, *args, flops=None):
+        cost = flops and pl.CostEstimate(flops=flops, bytes_accessed=4096, transcendentals=0)
         return pl.pallas_call(
             kernel,
             out_shape=[jax.ShapeDtypeStruct(s, F32) for s in outs],
             in_specs=[VMEM] * len(args),
             out_specs=[VMEM] * len(outs),
             scratch_shapes=[pltpu.VMEM(s, F32) for s in scratch],
+            cost_estimate=cost,
             compiler_params=pltpu.CompilerParams(vmem_limit_bytes=16 * 1024 * 1024),
         )(*args)
 
@@ -654,9 +667,14 @@
     def swap(packet, axis, first):
         count = lax.axis_size(axis)
         pairs = [(i, i + 1) for i in range(first, count - 1, 2)]
+        KIND = {"row": "cyc", "col": "cyc"}[axis]
+        extra = []
         if first == 1 and count > 2 and count % 2 == 0:
-            pairs.append((0, count - 1))
-        return lax.ppermute(packet, axis, pairs + [(j, i) for i, j in pairs])
+            if KIND == "cyc":
+                pairs.append((0, count - 1))
+            if KIND == "self":
+                extra = [(0, 0), (count - 1, count - 1)]
+        return lax.ppermute(packet, axis, pairs + [(j, i) for i, j in pairs] + extra)
 
     basis = coarse_basis.reshape(columns * comps * rows, cols)
     rhs = right_side.reshape(comps * rows, cols)
@@ -664,22 +682,28 @@
 
     block = gram_inverse.size
     piece = -(-block // row_count)
-    flat = jnp.pad(gram_inverse.reshape(-1), (0, piece * row_count - block))
-    own = lax.dynamic_slice_in_dim(flat, lax.axis_index("row") * piece, piece)
-    own = jnp.pad(own, (0, cols - piece)).reshape(1, cols)
+    two = columns * columns == devices * cols and cols == 2 * columns and rows == 8 and comps == 3
+    if two:
+        (own,) = call(piece_kernel, [(1, cols)], [], gram_inverse, flops=10**9)
+    else:
+        flat = jnp.pad(gram_inverse.reshape(-1), (0, piece * row_count - block))
+        own = lax.dynamic_slice_in_dim(flat, lax.axis_index("row") * piece, piece)
+        own = jnp.pad(own, (0, cols - piece)).reshape(1, cols)
 
     tall = -(-(comps * columns + comps + 2) // 8) * 8
     wide = (comps + 1) * rows
     field = comps * rows
-    two = columns * columns == devices * cols and cols == 2 * columns and rows == 8 and comps == 3
     if two:
         row_a, row_b, col_a, col_b = call(
-            functools.partial(packet_kernel, sizes),
+            functools.partial(packets_kernel, sizes),
             [(tall, cols), (tall, cols), (wide, cols), (wide, cols)],
             [],
-            basis, rhs, mask, viscosity,
+            basis, rhs, mask, viscosity, own,
         )
-        halos = swap(row_a, "row", 0), swap(row_b, "row", 1), swap(col_a, "col", 0), swap(col_b, "col", 1)
+        packets = ((row_a, "row", 0), (row_b, "row", 1), (col_a, "col", 0), (col_b, "col", 1))
+        halos = []
+        for packet in packets:
+            halos.append(swap(*packet))
         (send,) = call(
             functools.partial(gram_kernel, sizes),
             [(devices, 4, cols)],

time: 41 us -> 38.7 us (0.944)
  local copies, waits for them, and re-layouts: 3.39 us -> 1.51 us
  waiting for transfers between devices: 3.66 us -> 2.2 us
  blocking collectives: 21 us -> 22 us
    unnamed x16 -> x10, local copies, waits for them, and re-layouts: 3.24 us -> 1.51 us
    ppermute x4, waiting for transfers between devices: 3.66 us -> 2.2 us  [swap(): lax.ppermute(packet, axis, pairs + [(j, i) for i, j in pairs] + extra)]
    all_to_all x2, blocking collectives: 21 us -> 22 us  [share(): return lax.all_to_all(message, ('row', 'col'), 0, 0, tiled=True)]
    pallas_call x4 -> x5, Pallas kernels: 3.71 us -> 3.81 us  [call(): pl.pallas_call(kernel, out_shape=[jax.ShapeDtypeStruct(s, F32) for s in o...]
where the time goes in v5:
time: 38.7 us; the launch traced here: 38.4 us
  blocking collectives  22 us (57%)
  starting transfers between devices  8.21 us (21%)
  Pallas kernels  3.81 us (10%)
  waiting for transfers between devices  2.2 us (6%)
  local copies, waits for them, and re-layouts  1.51 us (4%)
  between operations  0.67 us (2%)
    all_to_all x2, blocking collectives, share(): return lax.all_to_all(message, ('row', 'col'), 0, 0, tiled=True)  22 us
    ppermute x4, starting transfers between devices, swap(): lax.ppermute(packet, axis, pairs + [(j, i) for i, j in pairs] + extra)  8.21 us
    pallas_call x5, Pallas kernels, call(): pl.pallas_call(kernel, out_shape=[jax.ShapeDtypeStruct(s, F32) for s in o...  3.81 us
    ppermute x4, waiting for transfers between devices, swap(): lax.ppermute(packet, axis, pairs + [(j, i) for i, j in pairs] + extra)  2.2 us
    unnamed x10, local copies, waits for them, and re-layouts  1.51 us
  transfers between devices with their start and end apart: 4, of which 2 were waited for; matrix products, arithmetic and copies ran while one was open for 0% of the time, Pallas kernels for 0%

profile of v5, /device:TPU:0, one launch (start us, length us, event | category | flops | bytes accessed | tf_op | source)
XLA Modules:
  0.0 38.4 jit_solution(6249157583622291054)
XLA Ops:
  0.6 0.0 copy-start
  0.6 0.0 copy-start.4
  0.7 0.8 %copy-done.4 = f32[16,64]{1,0:T(8,128)S(1)} copy-done((f32[16,64]{1,0:T(8,128)S(1)}, f32[16,64]{1,0:T(8,128)}, u32[]{:S(2)}) %copy-start.4) | copy-done | bytes 4120
  1.4 0.0 copy-start.1
  1.4 0.0 copy-start.2
  1.4 0.1 shard_map.68.first_ref.gram_ref
  1.5 0.0 copy-start.3
  1.5 0.3 copy-done
  1.8 0.4 %copy-done.1 = f32[3,8,128]{2,1,0:T(8,128)S(1)} copy-done((f32[3,8,128]{2,1,0:T(8,128)S(1)}, f32[3,8,128]{2,1,0:T(8,128)}, u32[]{:S(2)}) %copy-start.1) | copy-done | bytes 12312
  2.2 0.0 copy-done.2
  2.2 0.0 copy-done.3
  2.2 0.5 %shard_map.69 = (f32[200,128]{1,0:T(8,128)S(1)}, f32[200,128]{1,0:T(8,128)S(1)}, f32[32,128]{1,0:T(8,128)S(1)}, f32[32,128]{1,0:T(8,128)S(1)}) custom-call(f32[1536,128]{1,0:T(8,128)S(1)} %bitcast.5, f32[24,128]{1,0:T(8,128)S(1)} %bitcast.9, s32[24,128]{1,0:T(8,128)S(1)} %bitcast.13, f32[8,128]{1,0:T(8,128)S(1)} %copy-done.3, ...), custom_call_target="tpu_custom_call" | custom-call | tf_op jit(solution)/shard_map/pallas_call | solution.py:654
  2.7 3.1 %collective-permute-start = (f32[200,128]{1,0:T(8,128)S(1)}, f32[200,128]{1,0:T(8,128)S(1)}, u32[]{:S(2)}, u32[]{:S(2)}) collective-permute-start(f32[200,128]{1,0:T(8,128)S(1)} %get-tuple-element.15), channel_id=1, source_target_pairs={{0,4},{8,12},{16,20},{24,28},{4,0},{12,8},{20,16},{28,24},{1,5},{9... | collective-permute-start | bytes 307208 | tf_op jit(solution)/shard_map/ppermute | solution.py:677
  5.8 3.5 %collective-permute-start.1 = (f32[200,128]{1,0:T(8,128)S(1)}, f32[200,128]{1,0:T(8,128)S(1)}, u32[]{:S(2)}, u32[]{:S(2)}) collective-permute-start(f32[200,128]{1,0:T(8,128)S(1)} %get-tuple-element.16), channel_id=1, source_target_pairs={{4,8},{12,16},{20,24},{0,28},{8,4},{16,12},{24,20},{28,0},{5,9},{1... | collective-permute-start | bytes 307208 | tf_op jit(solution)/shard_map/ppermute | solution.py:677
  9.3 0.0 collective-permute-start.2
  9.3 1.6 %collective-permute-start.3 = (f32[32,128]{1,0:T(8,128)S(1)}, f32[32,128]{1,0:T(8,128)S(1)}, u32[]{:S(2)}, u32[]{:S(2)}) collective-permute-start(f32[32,128]{1,0:T(8,128)S(1)} %get-tuple-element.18.ownb_ref), channel_id=1, source_target_pairs={{1,2},{0,3},{2,1},{3,0},{5,6},{4,7},{6,5},{7,4},{9,10},{8,11},{10,... | collective-permute-start | bytes 49160 | tf_op jit(solution)/shard_map/ppermute | solution.py:677
  10.9 0.0 collective-permute-done.2.cola_ref.refs_6_
  10.9 1.6 %collective-permute-done.3.colb_ref.refs_7_ = f32[32,128]{1,0:T(8,128)S(1)} collective-permute-done((f32[32,128]{1,0:T(8,128)S(1)}, f32[32,128]{1,0:T(8,128)S(1)}, u32[]{:S(2)}, u32[]{:S(2)}) %collective-permute-start.3) | collective-permute-done | bytes 16416 | tf_op jit(solution)/shard_map/ppermute | solution.py:677
  12.5 0.0 collective-permute-done.rowa_ref.refs_4_
  12.5 0.6 %collective-permute-done.1.rowb_ref.refs_5_ = f32[200,128]{1,0:T(8,128)S(1)} collective-permute-done((f32[200,128]{1,0:T(8,128)S(1)}, f32[200,128]{1,0:T(8,128)S(1)}, u32[]{:S(2)}, u32[]{:S(2)}) %collective-permute-start.1) | collective-permute-done | bytes 102432 | tf_op jit(solution)/shard_map/ppermute | solution.py:677
  13.1 1.0 %shard_map.70 = f32[32,4,128]{2,1,0:T(4,128)S(1)} custom-call(f32[1536,128]{1,0:T(8,128)S(1)} %bitcast.6, f32[24,128]{1,0:T(8,128)S(1)} %bitcast.10, s32[24,128]{1,0:T(8,128)S(1)} %bitcast.14, f32[8,128]{1,0:T(8,128)S(1)} %copy-done.3, f32[1,128]{1,0:T(1,128)S(1)} %shard_map.68.first_ref.gram_ref, f32[200,128]{1,0:T(8,128)S(1)} %collective-permute-done.rowa_ref.refs_4_, ...), custom_call_target="tpu_custom_call" | custom-call | tf_op jit(solution)/shard_map/pallas_call | solution.py:654
  14.2 12.1 %all_to_all.10.got_ref = f32[32,4,128]{2,1,0:T(4,128)S(1)} all-to-all(f32[32,4,128]{2,1,0:T(4,128)S(1)} %shard_map.70), channel_id=1, replica_groups=mesh['row'=8,'col'=4] {'row','col'}, dimensions={0} | all-to-all | bytes 131072 | tf_op jit(solution)/shard_map/all_to_all | solution.py:665
  26.2 0.7 %shard_map.71 = (f32[32,8,128]{2,1,0:T(8,128)S(1)}, f32[96,128]{1,0:T(8,128)S(1)}, f32[40,128]{1,0:T(8,128)S(1)}, f32[32,128]{1,0:T(8,128)S(1)}, f32[96,128]{1,0...) custom-call(f32[32,4,128]{2,1,0:T(4,128)S(1)} %all_to_all.10.got_ref, f32[1536,128]{1,0:T(8,128)S(1)} %bitcast.7, ...), custom_call_target="tpu_custom_call" | custom-call | tf_op jit(solution)/shard_map/pallas_call | solution.py:654
  26.9 9.9 %all_to_all.11.got_ref = f32[32,8,128]{2,1,0:T(8,128)S(1)} all-to-all(f32[32,8,128]{2,1,0:T(8,128)S(1)} %get-tuple-element.19), channel_id=1, replica_groups=mesh['row'=8,'col'=4] {'row','col'}, dimensions={0} | all-to-all | bytes 262144 | tf_op jit(solution)/shard_map/all_to_all | solution.py:665
  36.8 1.5 %shard_map.72 = (f32[24,128]{1,0:T(8,128)}, f32[24,128]{1,0:T(8,128)}) custom-call(f32[32,8,128]{2,1,0:T(8,128)S(1)} %all_to_all.11.got_ref, f32[1536,128]{1,0:T(8,128)S(1)} %bitcast.8, f32[24,128]{1,0:T(8,128)S(1)} %bitcast.12, s32[24,128]{1,0:T(8,128)S(1)} %bitcast.16, f32[200,128]{1,0:T(8,128)S(1)} %collective-permute-done.rowa_ref.refs_4_, ...), custom_call_target="tpu_custom_call" | custom-call | tf_op jit(solution)/shard_map/pallas_call | solution.py:654
Async XLA Ops:
  0.6 1.1 %copy-start = (f32[64,3,8,128]{3,2,1,0:T(8,128)S(1)}, f32[64,3,8,128]{3,2,1,0:T(8,128)}, u32[]{:S(2)}) copy-start(f32[64,3,8,128]{3,2,1,0:T(8,128)} %param.8) | copy-start | bytes 2359300
  0.6 0.8 %copy-start.4 = (f32[16,64]{1,0:T(8,128)S(1)}, f32[16,64]{1,0:T(8,128)}, u32[]{:S(2)}) copy-start(f32[16,64]{1,0:T(8,128)} %gram_ref.1) | copy-start | bytes 12292
  1.4 0.8 %copy-start.1 = (f32[3,8,128]{2,1,0:T(8,128)S(1)}, f32[3,8,128]{2,1,0:T(8,128)}, u32[]{:S(2)}) copy-start(f32[3,8,128]{2,1,0:T(8,128)} %param.5) | copy-start | bytes 36868
  1.4 0.8 %copy-start.2 = (s32[3,8,128]{2,1,0:T(8,128)S(1)}, s32[3,8,128]{2,1,0:T(8,128)}, u32[]{:S(2)}) copy-start(s32[3,8,128]{2,1,0:T(8,128)} %param.7) | copy-start | bytes 36868
  1.5 0.7 %copy-start.3 = (f32[8,128]{1,0:T(8,128)S(1)}, f32[8,128]{1,0:T(8,128)}, u32[]{:S(2)}) copy-start(f32[8,128]{1,0:T(8,128)} %refs_3_.1) | copy-start | bytes 12292
  2.7 9.8 %collective-permute-start = (f32[200,128]{1,0:T(8,128)S(1)}, f32[200,128]{1,0:T(8,128)S(1)}, u32[]{:S(2)}, u32[]{:S(2)}) collective-permute-start(f32[200,128]{1,0:T(8,128)S(1)} %get-tuple-element.15), channel_id=1, source_target_pairs={{0,4},{8,12},{16,20},{24,28},{4,0},{12,8},{20,16},{28,24},{1,5},{9... | collective-permute-start | bytes 307208 | tf_op jit(solution)/shard_map/ppermute | solution.py:677
  5.8 7.4 %collective-permute-start.1 = (f32[200,128]{1,0:T(8,128)S(1)}, f32[200,128]{1,0:T(8,128)S(1)}, u32[]{:S(2)}, u32[]{:S(2)}) collective-permute-start(f32[200,128]{1,0:T(8,128)S(1)} %get-tuple-element.16), channel_id=1, source_target_pairs={{4,8},{12,16},{20,24},{0,28},{8,4},{16,12},{24,20},{28,0},{5,9},{1... | collective-permute-start | bytes 307208 | tf_op jit(solution)/shard_map/ppermute | solution.py:677
  9.3 1.6 %collective-permute-start.2 = (f32[32,128]{1,0:T(8,128)S(1)}, f32[32,128]{1,0:T(8,128)S(1)}, u32[]{:S(2)}, u32[]{:S(2)}) collective-permute-start(f32[32,128]{1,0:T(8,128)S(1)} %get-tuple-element.17.owna_ref), channel_id=1, source_target_pairs={{0,1},{2,3},{1,0},{3,2},{4,5},{6,7},{5,4},{7,6},{8,9},{10,11},{9,8... | collective-permute-start | bytes 49160 | tf_op jit(solution)/shard_map/ppermute | solution.py:677
  9.3 3.2 %collective-permute-start.3 = (f32[32,128]{1,0:T(8,128)S(1)}, f32[32,128]{1,0:T(8,128)S(1)}, u32[]{:S(2)}, u32[]{:S(2)}) collective-permute-start(f32[32,128]{1,0:T(8,128)S(1)} %get-tuple-element.18.ownb_ref), channel_id=1, source_target_pairs={{1,2},{0,3},{2,1},{3,0},{5,6},{4,7},{6,5},{7,4},{9,10},{8,11},{10,... | collective-permute-start | bytes 49160 | tf_op jit(solution)/shard_map/ppermute | solution.py:677

commit v6 on v5

--- a/solution.py
+++ b/solution.py
@@ -665,16 +665,19 @@
         return lax.all_to_all(message, ("row", "col"), 0, 0, tiled=True)
 
     def swap(packet, axis, first):
-        count = lax.axis_size(axis)
-        pairs = [(i, i + 1) for i in range(first, count - 1, 2)]
-        KIND = {"row": "cyc", "col": "cyc"}[axis]
-        extra = []
-        if first == 1 and count > 2 and count % 2 == 0:
-            if KIND == "cyc":
-                pairs.append((0, count - 1))
-            if KIND == "self":
-                extra = [(0, 0), (count - 1, count - 1)]
-        return lax.ppermute(packet, axis, pairs + [(j, i) for i, j in pairs] + extra)
+        pairs = []
+        for r in range(row_count):
+            for c in range(col_count):
+                along, across = ((r, c) if axis == "row" else (c, r))
+                length, width = (row_count, col_count)[:: 1 if axis == "row" else -1]
+                other = along + 1 if (along - first) % 2 == 0 else along - 1
+                if 0 <= other < length:
+                    mate = (other, across)
+                else:
+                    mate = (along, across ^ 1 if (across ^ 1) < width else across)
+                r2, c2 = mate if axis == "row" else mate[::-1]
+                pairs.append((r * col_count + c, r2 * col_count + c2))
+        return lax.ppermute(packet, ("row", "col"), pairs)
 
     basis = coarse_basis.reshape(columns * comps * rows, cols)
     rhs = right_side.reshape(comps * rows, cols)

time: 38.7 us -> 37 us (0.956)
  starting transfers between devices: 8.21 us -> 6.1 us
  blocking collectives: 22 us -> 22.8 us
  waiting for transfers between devices: 2.2 us -> 1.72 us
    ppermute x4, starting transfers between devices: 8.21 us -> 6.1 us  [swap(): return lax.ppermute(packet, ('row', 'col'), pairs)]
    all_to_all x2, blocking collectives: 22 us -> 22.8 us  [share(): return lax.all_to_all(message, ('row', 'col'), 0, 0, tiled=True)]
    ppermute x4, waiting for transfers between devices: 2.2 us -> 1.72 us  [swap(): return lax.ppermute(packet, ('row', 'col'), pairs)]
  transfers between devices with their start and end apart: 4 -> 4, of which waited for: 2 -> 1; matrix products, arithmetic and copies ran while one was open for 0% -> 0% of each run, Pallas kernels for 0% -> 0%
where the time goes in v6:
time: 37 us; the launch traced here: 36.6 us
  blocking collectives  22.8 us (62%)
  starting transfers between devices  6.1 us (16%)
  Pallas kernels  3.81 us (10%)
  waiting for transfers between devices  1.72 us (5%)
  local copies, waits for them, and re-layouts  1.51 us (4%)
  between operations  0.67 us (2%)
    all_to_all x2, blocking collectives, share(): return lax.all_to_all(message, ('row', 'col'), 0, 0, tiled=True)  22.8 us
    ppermute x4, starting transfers between devices, swap(): return lax.ppermute(packet, ('row', 'col'), pairs)  6.1 us
    pallas_call x5, Pallas kernels, call(): pl.pallas_call(kernel, out_shape=[jax.ShapeDtypeStruct(s, F32) for s in o...  3.81 us
    ppermute x4, waiting for transfers between devices, swap(): return lax.ppermute(packet, ('row', 'col'), pairs)  1.72 us
    unnamed x10, local copies, waits for them, and re-layouts  1.51 us
  transfers between devices with their start and end apart: 4, of which 1 were waited for; matrix products, arithmetic and copies ran while one was open for 0% of the time, Pallas kernels for 0%

profile of v6, /device:TPU:0, one launch (start us, length us, event | category | flops | bytes accessed | tf_op | source)
XLA Modules:
  0.0 36.6 jit_solution(14663652192085127717)
XLA Ops:
  0.6 0.0 copy-start
  0.6 0.0 copy-start.4
  0.7 0.8 %copy-done.4 = f32[16,64]{1,0:T(8,128)S(1)} copy-done((f32[16,64]{1,0:T(8,128)S(1)}, f32[16,64]{1,0:T(8,128)}, u32[]{:S(2)}) %copy-start.4) | copy-done | bytes 4120
  1.4 0.0 copy-start.1
  1.4 0.0 copy-start.2
  1.4 0.1 shard_map.68.first_ref.gram_ref
  1.5 0.0 copy-start.3
  1.5 0.3 copy-done
  1.8 0.4 %copy-done.1 = f32[3,8,128]{2,1,0:T(8,128)S(1)} copy-done((f32[3,8,128]{2,1,0:T(8,128)S(1)}, f32[3,8,128]{2,1,0:T(8,128)}, u32[]{:S(2)}) %copy-start.1) | copy-done | bytes 12312
  2.2 0.0 copy-done.2
  2.2 0.0 copy-done.3
  2.2 0.5 %shard_map.69 = (f32[200,128]{1,0:T(8,128)S(1)}, f32[200,128]{1,0:T(8,128)S(1)}, f32[32,128]{1,0:T(8,128)S(1)}, f32[32,128]{1,0:T(8,128)S(1)}) custom-call(f32[1536,128]{1,0:T(8,128)S(1)} %bitcast.5, f32[24,128]{1,0:T(8,128)S(1)} %bitcast.9, s32[24,128]{1,0:T(8,128)S(1)} %bitcast.13, f32[8,128]{1,0:T(8,128)S(1)} %copy-done.3, ...), custom_call_target="tpu_custom_call" | custom-call | tf_op jit(solution)/shard_map/pallas_call | solution.py:654
  2.7 3.1 %collective-permute-start = (f32[200,128]{1,0:T(8,128)S(1)}, f32[200,128]{1,0:T(8,128)S(1)}, u32[]{:S(2)}, u32[]{:S(2)}) collective-permute-start(f32[200,128]{1,0:T(8,128)S(1)} %get-tuple-element.15), channel_id=1, source_target_pairs={{0,4},{1,5},{2,6},{3,7},{4,0},{5,1},{6,2},{7,3},{8,12},{9,13},{10,... | collective-permute-start | bytes 307208 | tf_op jit(solution)/shard_map/ppermute | solution.py:680
  5.8 0.0 collective-permute-start.1
  5.8 0.5 %collective-permute-start.2 = (f32[32,128]{1,0:T(8,128)S(1)}, f32[32,128]{1,0:T(8,128)S(1)}, u32[]{:S(2)}, u32[]{:S(2)}) collective-permute-start(f32[32,128]{1,0:T(8,128)S(1)} %get-tuple-element.17.owna_ref), channel_id=1, source_target_pairs={{0,1},{1,0},{2,3},{3,2},{4,5},{5,4},{6,7},{7,6},{8,9},{9,8},{10,11... | collective-permute-start | bytes 49160 | tf_op jit(solution)/shard_map/ppermute | solution.py:680
  6.3 2.5 %collective-permute-start.3 = (f32[32,128]{1,0:T(8,128)S(1)}, f32[32,128]{1,0:T(8,128)S(1)}, u32[]{:S(2)}, u32[]{:S(2)}) collective-permute-start(f32[32,128]{1,0:T(8,128)S(1)} %get-tuple-element.18.ownb_ref), channel_id=1, source_target_pairs={{0,4},{1,2},{2,1},{3,7},{4,0},{5,6},{6,5},{7,3},{8,12},{9,10},{10,... | collective-permute-start | bytes 49160 | tf_op jit(solution)/shard_map/ppermute | solution.py:680
  8.8 0.0 collective-permute-done.2.cola_ref.refs_6_
  8.8 1.7 %collective-permute-done.3.colb_ref.refs_7_ = f32[32,128]{1,0:T(8,128)S(1)} collective-permute-done((f32[32,128]{1,0:T(8,128)S(1)}, f32[32,128]{1,0:T(8,128)S(1)}, u32[]{:S(2)}, u32[]{:S(2)}) %collective-permute-start.3) | collective-permute-done | bytes 16416 | tf_op jit(solution)/shard_map/ppermute | solution.py:680
  10.5 0.0 collective-permute-done.rowa_ref.refs_4_
  10.5 0.0 collective-permute-done.1.rowb_ref.refs_5_
  10.6 1.0 %shard_map.70 = f32[32,4,128]{2,1,0:T(4,128)S(1)} custom-call(f32[1536,128]{1,0:T(8,128)S(1)} %bitcast.6, f32[24,128]{1,0:T(8,128)S(1)} %bitcast.10, s32[24,128]{1,0:T(8,128)S(1)} %bitcast.14, f32[8,128]{1,0:T(8,128)S(1)} %copy-done.3, f32[1,128]{1,0:T(1,128)S(1)} %shard_map.68.first_ref.gram_ref, f32[200,128]{1,0:T(8,128)S(1)} %collective-permute-done.rowa_ref.refs_4_, ...), custom_call_target="tpu_custom_call" | custom-call | tf_op jit(solution)/shard_map/pallas_call | solution.py:654
  11.6 12.9 %all_to_all.10.got_ref = f32[32,4,128]{2,1,0:T(4,128)S(1)} all-to-all(f32[32,4,128]{2,1,0:T(4,128)S(1)} %shard_map.70), channel_id=1, replica_groups=mesh['row'=8,'col'=4] {'row','col'}, dimensions={0} | all-to-all | bytes 131072 | tf_op jit(solution)/shard_map/all_to_all | solution.py:665
  24.5 0.7 %shard_map.71 = (f32[32,8,128]{2,1,0:T(8,128)S(1)}, f32[96,128]{1,0:T(8,128)S(1)}, f32[40,128]{1,0:T(8,128)S(1)}, f32[32,128]{1,0:T(8,128)S(1)}, f32[96,128]{1,0...) custom-call(f32[32,4,128]{2,1,0:T(4,128)S(1)} %all_to_all.10.got_ref, f32[1536,128]{1,0:T(8,128)S(1)} %bitcast.7, ...), custom_call_target="tpu_custom_call" | custom-call | tf_op jit(solution)/shard_map/pallas_call | solution.py:654
  25.2 9.9 %all_to_all.11.got_ref = f32[32,8,128]{2,1,0:T(8,128)S(1)} all-to-all(f32[32,8,128]{2,1,0:T(8,128)S(1)} %get-tuple-element.19), channel_id=1, replica_groups=mesh['row'=8,'col'=4] {'row','col'}, dimensions={0} | all-to-all | bytes 262144 | tf_op jit(solution)/shard_map/all_to_all | solution.py:665
  35.1 1.5 %shard_map.72 = (f32[24,128]{1,0:T(8,128)}, f32[24,128]{1,0:T(8,128)}) custom-call(f32[32,8,128]{2,1,0:T(8,128)S(1)} %all_to_all.11.got_ref, f32[1536,128]{1,0:T(8,128)S(1)} %bitcast.8, f32[24,128]{1,0:T(8,128)S(1)} %bitcast.12, s32[24,128]{1,0:T(8,128)S(1)} %bitcast.16, f32[200,128]{1,0:T(8,128)S(1)} %collective-permute-done.rowa_ref.refs_4_, ...), custom_call_target="tpu_custom_call" | custom-call | tf_op jit(solution)/shard_map/pallas_call | solution.py:654
Async XLA Ops:
  0.6 1.1 %copy-start = (f32[64,3,8,128]{3,2,1,0:T(8,128)S(1)}, f32[64,3,8,128]{3,2,1,0:T(8,128)}, u32[]{:S(2)}) copy-start(f32[64,3,8,128]{3,2,1,0:T(8,128)} %param.8) | copy-start | bytes 2359300
  0.6 0.8 %copy-start.4 = (f32[16,64]{1,0:T(8,128)S(1)}, f32[16,64]{1,0:T(8,128)}, u32[]{:S(2)}) copy-start(f32[16,64]{1,0:T(8,128)} %gram_ref.1) | copy-start | bytes 12292
  1.4 0.8 %copy-start.1 = (f32[3,8,128]{2,1,0:T(8,128)S(1)}, f32[3,8,128]{2,1,0:T(8,128)}, u32[]{:S(2)}) copy-start(f32[3,8,128]{2,1,0:T(8,128)} %param.5) | copy-start | bytes 36868
  1.4 0.8 %copy-start.2 = (s32[3,8,128]{2,1,0:T(8,128)S(1)}, s32[3,8,128]{2,1,0:T(8,128)}, u32[]{:S(2)}) copy-start(s32[3,8,128]{2,1,0:T(8,128)} %param.7) | copy-start | bytes 36868
  1.5 0.7 %copy-start.3 = (f32[8,128]{1,0:T(8,128)S(1)}, f32[8,128]{1,0:T(8,128)}, u32[]{:S(2)}) copy-start(f32[8,128]{1,0:T(8,128)} %refs_3_.1) | copy-start | bytes 12292
  2.7 7.8 %collective-permute-start = (f32[200,128]{1,0:T(8,128)S(1)}, f32[200,128]{1,0:T(8,128)S(1)}, u32[]{:S(2)}, u32[]{:S(2)}) collective-permute-start(f32[200,128]{1,0:T(8,128)S(1)} %get-tuple-element.15), channel_id=1, source_target_pairs={{0,4},{1,5},{2,6},{3,7},{4,0},{5,1},{6,2},{7,3},{8,12},{9,13},{10,... | collective-permute-start | bytes 307208 | tf_op jit(solution)/shard_map/ppermute | solution.py:680
  5.8 4.8 %collective-permute-start.1 = (f32[200,128]{1,0:T(8,128)S(1)}, f32[200,128]{1,0:T(8,128)S(1)}, u32[]{:S(2)}, u32[]{:S(2)}) collective-permute-start(f32[200,128]{1,0:T(8,128)S(1)} %get-tuple-element.16), channel_id=1, source_target_pairs={{0,1},{1,0},{2,3},{3,2},{4,8},{5,9},{6,10},{7,11},{8,4},{9,5},{10,... | collective-permute-start | bytes 307208 | tf_op jit(solution)/shard_map/ppermute | solution.py:680
  5.8 3.0 %collective-permute-start.2 = (f32[32,128]{1,0:T(8,128)S(1)}, f32[32,128]{1,0:T(8,128)S(1)}, u32[]{:S(2)}, u32[]{:S(2)}) collective-permute-start(f32[32,128]{1,0:T(8,128)S(1)} %get-tuple-element.17.owna_ref), channel_id=1, source_target_pairs={{0,1},{1,0},{2,3},{3,2},{4,5},{5,4},{6,7},{7,6},{8,9},{9,8},{10,11... | collective-permute-start | bytes 49160 | tf_op jit(solution)/shard_map/ppermute | solution.py:680
  6.3 4.2 %collective-permute-start.3 = (f32[32,128]{1,0:T(8,128)S(1)}, f32[32,128]{1,0:T(8,128)S(1)}, u32[]{:S(2)}, u32[]{:S(2)}) collective-permute-start(f32[32,128]{1,0:T(8,128)S(1)} %get-tuple-element.18.ownb_ref), channel_id=1, source_target_pairs={{0,4},{1,2},{2,1},{3,7},{4,0},{5,6},{6,5},{7,3},{8,12},{9,10},{10,... | collective-permute-start | bytes 49160 | tf_op jit(solution)/shard_map/ppermute | solution.py:680

commit v7 on v6

--- a/solution.py
+++ b/solution.py
@@ -180,29 +180,34 @@
     return jnp.concatenate([high, (values - high.astype(F32)).astype(jnp.bfloat16)], axis=0)
 
 
-def gram_kernel(sizes, basis_ref, rhs_ref, mask_ref, visc_ref, gram_ref, rowa_ref, rowb_ref,
-                cola_ref, colb_ref, owna_ref, ownb_ref, send_ref, acc_ref, full_ref):
+def product(lefts, rights):
+    return lax.dot_general(
+        jnp.concatenate([split(value) for value in lefts], axis=1),
+        jnp.concatenate([split(value) for value in rights], axis=1),
+        (((1,), (1,)), ((), ())),
+        preferred_element_type=F32,
+    )
+
+
+def merge(blocks, columns):
+    blocks = blocks + pltpu.roll(blocks, columns, 1)
+    return blocks[:columns] + blocks[columns:]
+
+
+def local_kernel(sizes, basis_ref, rhs_ref, mask_ref, visc_ref, inner_ref, dots_ref, acc_ref):
     columns, comps, rows, cols = sizes
-    at_row, at_col = (lax.axis_index("row"), lax.axis_index("col"))
-    even_row, even_col = (1 - lax.rem(at_row, 2), 1 - lax.rem(at_col, 2))
-    has_north, has_south, has_east, has_west = flags()
-    low, half = (cols - 1, cols // 2)
+    _, has_south, _, has_west = flags()
+    top, low = (rows - 1, cols - 1)
     rhs = [rhs_ref[c * rows : (c + 1) * rows, :] for c in range(comps)]
     mask = [mask_ref[c * rows : (c + 1) * rows, :].astype(F32) for c in range(comps)]
     visc = visc_ref[...]
-    lane, lanes = (iota((rows, cols), 1), iota((1, cols), 1))
-
-    at = comps * columns + comps
-    tail_a, tail_b = (rowa_ref[at : at + 1, :], rowb_ref[at : at + 1, :])
-    v_north = pick(even_row, tail_a, tail_b) * has_north
-    v_south = pick(even_row, tail_b, tail_a) * has_south
-    side_a, side_b = (cola_ref[...], colb_ref[...])
-    east_side = pick(even_col, side_a, side_b) * has_east
-    west_side = pick(even_col, side_b, side_a) * has_west
-    own_a, own_b = (owna_ref[...], ownb_ref[...])
-    own_east, own_west = (pick(even_col, own_a, own_b), pick(even_col, own_b, own_a))
-    v_east, v_west = (east_side[comps * rows :, 0:1], west_side[comps * rows :, 0:1])
-    faces = [0.5 * (visc + v) for v in shifts(visc, v_north, v_south, v_east, v_west)]
+    sub, lane = (iota((rows, cols), 0), iota((rows, cols), 1))
+    empty = (jnp.zeros((1, cols), F32),) * 2 + (jnp.zeros((rows, 1), F32),) * 2
+    faces = [0.5 * (visc + v) for v in shifts(visc, *empty)]
+    faces[0] = jnp.where(sub == top, 0.0, faces[0])
+    faces[1] = jnp.where(sub == 0, faces[1] * (1.0 - has_south), faces[1])
+    faces[2] = jnp.where(lane == low, 0.0, faces[2])
+    faces[3] = jnp.where(lane == 0, faces[3] * (1.0 - has_west), faces[3])
     diagonal = 1.0 + faces[0] + faces[1] + faces[2] + faces[3]
 
     blocks = jnp.zeros((2 * columns, 2 * columns), F32)
@@ -210,44 +215,59 @@
         m = mask[c]
         own = m * diagonal + (1.0 - m)
         up, down = (m * faces[0], m * faces[1])
-        right = jnp.where(lane == low, 0.0, m * faces[2])
+        right = m * faces[2]
         left = jnp.where(lane == 0, 0.0, m * faces[3])
-        span = slice(c * columns, (c + 1) * columns)
-        halo_a, halo_b = (rowa_ref[span, :], rowb_ref[span, :])
         plain = [
             basis_ref[pl.ds(c * rows + i, columns, stride=comps * rows), :] for i in range(rows)
         ]
         free = [plain[i] * m[i : i + 1, :] for i in range(rows)]
-        free.append(pick(even_row, halo_a, halo_b) * has_north)
-        free.append(pick(even_row, halo_b, halo_a) * has_south)
+        images = []
+        for i in range(rows):
+            here = slice(i, i + 1)
+            value = own[here] * plain[i] - right[here] * pltpu.roll(free[i], low, 1)
+            value = value - left[here] * pltpu.roll(free[i], 1, 1)
+            if i < top:
+                value = value - up[here] * free[i + 1]
+            if i > 0:
+                value = value - down[here] * free[i - 1]
+            images.append(value)
         for i in range(0, rows, 2):
-            lefts, rights = ([], [])
-            for j in (i, i + 1):
-                here = slice(j, j + 1)
-                value = own[here] * plain[j] - up[here] * free[j + 1] - down[here] * free[j - 1]
-                value = value - right[here] * pltpu.roll(free[j], low, 1)
-                value = value - left[here] * pltpu.roll(free[j], 1, 1)
-                lefts.append(split(plain[j]))
-                rights.append(split(value))
-            blocks = blocks + lax.dot_general(
-                jnp.concatenate(lefts, axis=1),
-                jnp.concatenate(rights, axis=1),
-                (((1,), (1,)), ((), ())),
-                preferred_element_type=F32,
-            )
-    east_face = jnp.concatenate([faces[2][:, low : low + 1]] * comps, axis=0)
-    west_face = jnp.concatenate([faces[3][:, 0:1]] * comps, axis=0)
+            blocks = blocks + product(plain[i : i + 2], images[i : i + 2])
+    inner_ref[...] = merge(blocks, columns)
+    dots = to_row(project(basis_ref, rhs, acc_ref, columns, comps, rows))
+    dots_ref[...] = jnp.broadcast_to(dots, dots_ref.shape)
+
+
+def border_kernel(sizes, inner_ref, dots_ref, basis_ref, mask_ref, visc_ref, gram_ref, rowa_ref,
+                  rowb_ref, cola_ref, colb_ref, owna_ref, ownb_ref, send_ref, full_ref):
+    columns, comps, rows, cols = sizes
+    even_row = 1 - lax.rem(lax.axis_index("row"), 2)
+    even_col = 1 - lax.rem(lax.axis_index("col"), 2)
+    has_north, _, has_east, _ = flags()
+    top, low, half = (rows - 1, cols - 1, cols // 2)
     field = comps * rows
-    ours = jnp.concatenate([own_east[:field] * east_face, own_west[:field] * west_face], axis=0)
-    theirs = jnp.concatenate([east_side[:field], west_side[:field]], axis=0)
+    visc, lanes = (visc_ref[...], iota((1, cols), 1))
+    at = comps * columns + comps
+    v_north = pick(even_row, rowa_ref[at : at + 1, :], rowb_ref[at : at + 1, :]) * has_north
+    east = pick(even_col, cola_ref[...], colb_ref[...]) * has_east
+    own_east = pick(even_col, owna_ref[...], ownb_ref[...])
+    north_face = 0.5 * (visc[top : top + 1, :] + v_north)
+    east_face = 0.5 * (visc[:, low : low + 1] + east[field:, 0:1])
+    tops = []
+    for c in range(comps):
+        span = slice(c * columns, (c + 1) * columns)
+        own = basis_ref[pl.ds(c * rows + top, columns, stride=comps * rows), :]
+        own = own * mask_ref[c * rows + top : c * rows + rows, :].astype(F32)
+        tops.append(own - pick(even_row, rowa_ref[span, :], rowb_ref[span, :]) * has_north)
+    full = inner_ref[...] + merge(product([value * north_face for value in tops], tops), columns)
+    gap = own_east[:field] - east[:field]
     edge = lax.dot_general(
-        ours, theirs, (((0,), (0,)), ((), ())),
+        gap * jnp.concatenate([east_face] * comps, axis=0), gap, (((0,), (0,)), ((), ())),
         preferred_element_type=F32, precision=lax.Precision.HIGHEST,
     )
-    blocks = blocks + pltpu.roll(blocks, half, 1)
     wide_lane = iota((columns, cols), 1)
     edge = jnp.where(wide_lane < half, edge[:columns], 0.0)
-    full = blocks[:columns] + blocks[columns:] - edge - pltpu.roll(edge, half, 1)
+    full = full + edge + pltpu.roll(edge, half, 1)
     full_ref[...] = full
     spot = jnp.where(wide_lane >= half, wide_lane - half, wide_lane) == iota((columns, cols), 0)
     spine = jnp.sum(jnp.where(spot, full, 0.0), axis=0, keepdims=True)
@@ -257,7 +277,7 @@
         full_ref[pl.ds(0, count, stride=2), :],
         full_ref[pl.ds(1, count, stride=2), :],
     )
-    dots = to_row(project(basis_ref, rhs, acc_ref, columns, comps, rows))
+    dots = dots_ref[0:1, :]
     corner_row = jnp.zeros((1, cols), F32)
     for i, corner in enumerate(corners_of(visc)):
         corner_row = jnp.where(lanes == i, corner, corner_row)
@@ -273,8 +293,9 @@
     else:
         gram_in_ref, *refs = refs
     (basis_ref, rhs_ref, mask_ref, visc_ref, rowa_ref, rowb_ref, cola_ref, colb_ref,
-     send_ref, state_ref, face_ref, edge_ref, side_ref, small_ref, gram_ref,
-     acc_ref, wide_ref) = refs
+     send_ref, state_ref, face_ref, small_ref, gram_ref, *refs) = refs
+    edge_ref, side_ref = (None, None) if two else refs[:2]
+    acc_ref, wide_ref = refs[-2:]
     at_row, at_col = (lax.axis_index("row"), lax.axis_index("col"))
     row_count, col_count = (lax.axis_size("row"), lax.axis_size("col"))
     even_row, even_col = (1 - lax.rem(at_row, 2), 1 - lax.rem(at_col, 2))
@@ -353,7 +374,7 @@
 
     corr = combine(basis_ref, wide_ref, columns, comps, rows)
     image, scaled, smooth, point = ([], [], [], [])
-    smooth_image, scaled_image = ([], [])
+    scaled_image = []
     none = (jnp.zeros((1, cols), F32),) * 2 + (jnp.zeros((rows, 1), F32),) * 2
     for c in range(comps):
         span = slice(c * columns, (c + 1) * columns)
@@ -373,23 +394,24 @@
         p = u + corr[c]
         q = stencil(mask[c], faces, diagonal, p, (p_north, p_south, p_east, p_west))
         if two:
-            halo = (u_north, u_south, u_east, u_west)
-            smooth_image.append(stencil(mask[c], faces, diagonal, u, halo))
             scaled_image.append(stencil(mask[c], faces, diagonal, jacobi[c] * q, none))
         smooth.append(u)
         point.append(p)
         image.append(q)
         scaled.append(jacobi[c] * q)
+        if two:
+            continue
         for i, value in enumerate((u_north, u_south, p_north, p_south)):
             edge_ref[i * 8 + c : i * 8 + c + 1, :] = value
         for i, value in enumerate((u_east, u_west, p_east, p_west)):
             side_ref[(i * comps + c) * rows : (i * comps + c + 1) * rows, :] = value
-    state_ref[...] = jnp.concatenate(smooth + point + image + scaled, axis=0)
+    fields = point + image + scaled
+    state_ref[...] = jnp.concatenate(fields if two else smooth + fields, axis=0)
 
     row = to_row(project(basis_ref, image, acc_ref, columns, comps, rows))
     pairs = ((point, image), (smooth, image), (image, scaled), (rhs, smooth))
     if two:
-        pairs += ((smooth, smooth_image), (scaled, smooth_image), (scaled, scaled_image))
+        pairs += ((scaled, scaled_image),)
     for i, (left, right) in enumerate(pairs):
         value = left[0] * right[0]
         for c in range(1, comps):
@@ -442,7 +464,7 @@
 
 
 def second_kernel(sizes, got_ref, basis_ref, rhs_ref, mask_ref, rowa_ref, rowb_ref, cola_ref,
-                  colb_ref, state_ref, face_ref, edge_ref, side_ref, small_ref, gram_ref,
+                  colb_ref, state_ref, face_ref, small_ref, gram_ref, edge_ref, side_ref,
                   send_ref, out_ref, last_ref, wide_ref):
     columns, comps, rows, cols, scale = sizes
     at_row, at_col = (lax.axis_index("row"), lax.axis_index("col"))
@@ -524,7 +546,7 @@
 
 
 def close_kernel(sizes, got_ref, basis_ref, rhs_ref, mask_ref, rowa_ref, rowb_ref, cola_ref,
-                 colb_ref, state_ref, face_ref, edge_ref, side_ref, small_ref, gram_ref,
+                 colb_ref, state_ref, face_ref, small_ref, gram_ref,
                  solution_ref, residual_ref, wide_ref):
     columns, comps, rows, cols, scale = sizes
     at_row, at_col = (lax.axis_index("row"), lax.axis_index("col"))
@@ -541,23 +563,44 @@
         return jnp.sum(left * right, axis=1, keepdims=True)
 
     sums = jnp.sum(got_ref[...], axis=0)
-    image_dots = jnp.where(lanes < columns, sums[2 * comps : 2 * comps + 1, :], 0.0)
+    line = sums[2 * comps : 2 * comps + 1, :]
+    image_dots = jnp.where(lanes < columns, line, 0.0)
     reach_dots = jnp.where(lanes < columns, sums[2 * comps + 1 :, :], 0.0)
-    curve, cross, image_sq, rhs_sq, smooth_sq, mixed, scaled_sq = [
-        along(jnp.where(lanes == DOTS2 + i, 1.0, 0.0), sums[2 * comps : 2 * comps + 1, :])
-        for i in range(7)
-    ]
-    dots, old_row, spine = (small_ref[0:1, :], small_ref[1:2, :], small_ref[2:3, :])
-    energy = rhs_sq + along(dots, old_row)
-    step = energy / curve
     gram = jnp.where(iota((columns, cols), 1) < columns, gram_ref[...], 0.0)
-    dots = dots - step * image_dots
-    coeffs = jnp.sum(gram * dots, axis=1, keepdims=True) * scale
-    wide = jnp.broadcast_to(coeffs, (columns, cols))
+    turn = jnp.sum(gram * image_dots, axis=1, keepdims=True) * scale
+    wide = jnp.broadcast_to(turn, (columns, cols))
     wide_ref[...] = wide
-    coeff_row = to_row(coeffs)
-    energy_new = rhs_sq - 2.0 * step * cross + step * step * image_sq + along(dots, coeff_row)
-    ratio = energy_new / energy
+    turn_row = to_row(turn)
+
+    def beside(step_row, step_col):
+        r, c = (at_row + step_row, at_col + step_col)
+        inside = (r >= 0) & (r < row_count) & (c >= 0) & (c < col_count)
+        message = got_ref[jnp.where(inside, r * col_count + c, me)]
+        return message * jnp.where(inside, 1.0, 0.0)
+
+    faces = [face_ref[i * rows : (i + 1) * rows, :] for i in range(4)]
+    diagonal = face_ref[4 * rows : 5 * rows, :]
+    q_north, q_south = (beside(1, 0), beside(-1, 0))
+    q_east = to_column(beside(0, 1)[2 * comps : 2 * comps + 1, :], comps * rows, WEST2)
+    q_west = to_column(beside(0, -1)[2 * comps : 2 * comps + 1, :], comps * rows, EAST2)
+    side_a, side_b = (cola_ref[...], colb_ref[...])
+    east_side = pick(even_col, side_a, side_b) * has_east
+    west_side = pick(even_col, side_b, side_a) * has_west
+    corr = combine(basis_ref, wide_ref, columns, comps, rows)
+    moved, moved_image = ([], [])
+    for c in range(comps):
+        span = slice(c * columns, (c + 1) * columns)
+        here = slice(c * rows, (c + 1) * rows)
+        sum_a = jnp.sum(wide * rowa_ref[span, :], axis=0, keepdims=True)
+        sum_b = jnp.sum(wide * rowb_ref[span, :], axis=0, keepdims=True)
+        north = q_north[comps + c : comps + c + 1, :] + has_north * pick(even_row, sum_a, sum_b)
+        south = q_south[c : c + 1, :] / faces[1][0:1, :] + has_south * pick(even_row, sum_b, sum_a)
+        east = q_east[here] + along(turn_row, east_side[here, :])
+        west = q_west[here] / faces[3][:, 0:1] + along(turn_row, west_side[here, :])
+        at = (2 * comps + c) * rows
+        value = state_ref[at : at + rows, :] + corr[c]
+        moved.append(value)
+        moved_image.append(stencil(mask[c], faces, diagonal, value, (north, south, east, west)))
 
     border = jnp.zeros((2 * comps + 2, cols), F32)
     for d in range(devices - col_count):
@@ -567,72 +610,44 @@
     later = pltpu.roll(pltpu.roll(lines, devices - 1, 0), cols - (WEST2 - EAST2), 1)
     line_lane = iota(lines.shape, 1)
     beside_it = jnp.where((line_lane >= EAST2) & (line_lane < WEST2), lines * later, 0.0)
-    scaled_sq = scaled_sq - 2.0 * (total(border) + total(beside_it))
+    across = jnp.sum(border, axis=0, keepdims=True) + jnp.sum(beside_it, axis=0, keepdims=True)
 
     packed = pltpu.roll(got_ref[:, 2 * comps + 1, :], half, 1)
     sub = iota(packed.shape, 0)
-
-    def turned(row):
-        value = jnp.broadcast_to(row, (8, cols))
-        value = jnp.broadcast_to((value + pltpu.roll(value, half, 1))[0:1, :], packed.shape)
-        bit = 1
-        while bit < devices:
-            value = jnp.where((sub & bit) != 0, pltpu.roll(value, cols - 2 * bit, 1), value)
-            bit *= 2
-        ahead = pltpu.roll(value, cols - 1, 1)
-        ahead = jnp.where(line_lane < quarter, ahead, pltpu.roll(value, quarter - 2, 1))
-        return (jnp.where(line_lane < quarter, value[:, 0:1], value[:, 1:2]), ahead)
-
-    other_row = coeff_row - 2.0 * old_row
-    (left, left_ahead), (right, right_ahead) = (turned(coeff_row), turned(other_row))
-    weight = jnp.where((line_lane == quarter - 1) | (line_lane == half - 1), 0.5, 1.0)
-    form = packed * weight * (left * right_ahead + right * left_ahead)
-    form = total(jnp.where(line_lane < half, form, 0.0)) + along(spine * coeff_row, other_row)
-    image_part = along(coeff_row, image_dots)
-    curve_new = smooth_sq - 2.0 * step * mixed + step * step * scaled_sq
-    curve_new = curve_new - 2.0 * step * along(coeff_row, reach_dots) + 2.0 * image_part + form
-    curve_new = curve_new + 2.0 * ratio * (cross - step * image_sq + image_part)
-    curve_new = curve_new + ratio * ratio * curve
+    value = jnp.broadcast_to(turn_row, (8, cols))
+    value = jnp.broadcast_to((value + pltpu.roll(value, half, 1))[0:1, :], packed.shape)
+    bit = 1
+    while bit < devices:
+        value = jnp.where((sub & bit) != 0, pltpu.roll(value, cols - 2 * bit, 1), value)
+        bit *= 2
+    ahead = pltpu.roll(value, cols - 1, 1)
+    ahead = jnp.where(line_lane < quarter, ahead, pltpu.roll(value, quarter - 2, 1))
+    own = jnp.where(line_lane < quarter, value[:, 0:1], value[:, 1:2])
+    weight = jnp.where((line_lane == quarter - 1) | (line_lane == half - 1), 1.0, 2.0)
+    form = jnp.where(line_lane < half, packed * weight * own * ahead, 0.0)
+    form = jnp.sum(form, axis=0, keepdims=True)
+
+    curve, cross, image_sq, rhs_sq, scaled_sq = [
+        along(jnp.where(lanes == DOTS2 + i, 1.0, 0.0), line) for i in range(5)
+    ]
+    dots, old_row, spine = (small_ref[0:1, :], small_ref[1:2, :], small_ref[2:3, :])
+    energy = rhs_sq + along(dots, old_row)
+    meet = image_sq + along(turn_row, image_dots)
+    rest = form + spine * turn_row * turn_row + 2.0 * turn_row * reach_dots - 2.0 * across
+    moved_sq = scaled_sq + jnp.sum(rest, axis=1, keepdims=True)
+    step = energy / curve
+    energy_new = rhs_sq - 2.0 * step * cross + step * step * image_sq
+    energy_new = energy_new + along(dots - step * image_dots, old_row - step * turn_row)
+    grow = 1.0 + energy_new / energy
+    curve_new = grow * grow * curve - 2.0 * step * grow * meet + step * step * moved_sq
     step_new = energy_new / curve_new
-
-    def beside(step_row, step_col):
-        r, c = (at_row + step_row, at_col + step_col)
-        inside = (r >= 0) & (r < row_count) & (c >= 0) & (c < col_count)
-        message = got_ref[jnp.where(inside, r * col_count + c, me)]
-        return message * jnp.where(inside, 1.0, 0.0)
-
-    faces = [face_ref[i * rows : (i + 1) * rows, :] for i in range(4)]
-    diagonal = face_ref[4 * rows : 5 * rows, :]
-    q_north, q_south = (beside(1, 0), beside(-1, 0))
-    q_east = to_column(beside(0, 1)[2 * comps : 2 * comps + 1, :], comps * rows, WEST2)
-    q_west = to_column(beside(0, -1)[2 * comps : 2 * comps + 1, :], comps * rows, EAST2)
-
-    side_a, side_b = (cola_ref[...], colb_ref[...])
-    east_side = pick(even_col, side_a, side_b) * has_east
-    west_side = pick(even_col, side_b, side_a) * has_west
-    corr = combine(basis_ref, wide_ref, columns, comps, rows)
+    near, far = (step + step_new * grow, step_new * step)
     for c in range(comps):
-        span = slice(c * columns, (c + 1) * columns)
         here = slice(c * rows, (c + 1) * rows)
-        sum_a = jnp.sum(wide * rowa_ref[span, :], axis=0, keepdims=True)
-        sum_b = jnp.sum(wide * rowb_ref[span, :], axis=0, keepdims=True)
-        old = [edge_ref[i * 8 + c : i * 8 + c + 1, :] for i in range(4)]
-        p_north = old[0] - step * q_north[comps + c : comps + c + 1, :]
-        p_south = old[1] - step * (q_south[c : c + 1, :] / faces[1][0:1, :])
-        p_north = p_north + has_north * pick(even_row, sum_a, sum_b) + ratio * old[2]
-        p_south = p_south + has_south * pick(even_row, sum_b, sum_a) + ratio * old[3]
-        old = [side_ref[(i * comps + c) * rows : (i * comps + c + 1) * rows, :] for i in range(4)]
-        p_east = old[0] - step * q_east[here] + ratio * old[2]
-        p_west = old[1] - step * (q_west[here] / faces[3][:, 0:1]) + ratio * old[3]
-        p_east = p_east + jnp.sum(coeff_row * east_side[here, :], axis=1, keepdims=True)
-        p_west = p_west + jnp.sum(coeff_row * west_side[here, :], axis=1, keepdims=True)
-        u, p, q, jq = [
-            state_ref[(i * comps + c) * rows : (i * comps + c + 1) * rows, :] for i in range(4)
-        ]
-        new = u - step * jq + corr[c] + ratio * p
-        applied = stencil(mask[c], faces, diagonal, new, (p_north, p_south, p_east, p_west))
-        solution_ref[here, :] = step * p + step_new * new
-        residual_ref[here, :] = rhs_ref[here, :] - step * q - step_new * applied
+        p = state_ref[here, :]
+        q = state_ref[(comps + c) * rows : (comps + c + 1) * rows, :]
+        solution_ref[here, :] = near * p - far * moved[c]
+        residual_ref[here, :] = rhs_ref[here, :] - near * q + far * moved_image[c]
 
 
 def last_kernel(count, got_ref, in_ref, last_ref, solution_ref, residual_ref):
@@ -707,17 +722,22 @@
         halos = []
         for packet in packets:
             halos.append(swap(*packet))
+        inner, dots = call(
+            functools.partial(local_kernel, sizes),
+            [(columns, cols), (8, cols)],
+            [(columns * rows, cols)],
+            basis, rhs, mask, viscosity, flops=10**8,
+        )
         (send,) = call(
-            functools.partial(gram_kernel, sizes),
+            functools.partial(border_kernel, sizes),
             [(devices, 4, cols)],
-            [(columns * rows, cols), (columns, cols)],
-            basis, rhs, mask, viscosity, own, *halos, col_a, col_b,
+            [(columns, cols)],
+            inner, dots, basis, mask, viscosity, own, *halos, col_a, col_b,
         )
         sizes = sizes + (scale,)
         send, *state = call(
             functools.partial(first_kernel, sizes, True, True),
-            [(devices, 8, cols), (4 * field, cols), (5 * rows, cols), (32, cols),
-             (4 * field, cols), (8, cols), (columns, cols)],
+            [(devices, 8, cols), (3 * field, cols), (5 * rows, cols), (8, cols), (columns, cols)],
             [(columns * rows, cols), (columns, cols)],
             share(send), basis, rhs, mask, viscosity, *halos,
         )
@@ -745,8 +765,8 @@
     sizes = sizes + (scale,)
     send, *state = call(
         functools.partial(first_kernel, sizes, whole_rows, False),
-        [(devices, 1 + comps, cols), (4 * field, cols), (5 * rows, cols), (32, cols),
-         (4 * field, cols), (8, cols), (columns, cols)],
+        [(devices, 1 + comps, cols), (4 * field, cols), (5 * rows, cols), (8, cols),
+         (columns, cols), (32, cols), (4 * field, cols)],
         [(columns * rows, cols), (columns, cols)],
         got, *gram, basis, rhs, mask, viscosity, *halos,
     )

time: 37 us -> 36.3 us (0.981)
  waiting for transfers between devices: 1.72 us -> 0.74 us
    ppermute x4, waiting for transfers between devices: 1.72 us -> 0.74 us  [swap(): return lax.ppermute(packet, ('row', 'col'), pairs)]
    pallas_call x5 -> x6, Pallas kernels: 3.81 us -> 4.14 us  [call(): pl.pallas_call(kernel, out_shape=[jax.ShapeDtypeStruct(s, F32) for s in o...]
  transfers between devices with their start and end apart: 4 -> 4, of which waited for: 1 -> 1; matrix products, arithmetic and copies ran while one was open for 0% -> 0% of each run, Pallas kernels for 0% -> 3%
where the time goes in v7:
time: 36.3 us; the launch traced here: 36 us
  blocking collectives  22.8 us (63%)
  starting transfers between devices  6.1 us (17%)
  Pallas kernels  4.14 us (11%)
  local copies, waits for them, and re-layouts  1.51 us (4%)
  waiting for transfers between devices  0.74 us (2%)
  between operations  0.68 us (2%)
    all_to_all x2, blocking collectives, share(): return lax.all_to_all(message, ('row', 'col'), 0, 0, tiled=True)  22.8 us
    ppermute x4, starting transfers between devices, swap(): return lax.ppermute(packet, ('row', 'col'), pairs)  6.1 us
    pallas_call x6, Pallas kernels, call(): pl.pallas_call(kernel, out_shape=[jax.ShapeDtypeStruct(s, F32) for s in o...  4.14 us
    unnamed x10, local copies, waits for them, and re-layouts  1.51 us
    ppermute x4, waiting for transfers between devices, swap(): return lax.ppermute(packet, ('row', 'col'), pairs)  0.74 us
  transfers between devices with their start and end apart: 4, of which 1 were waited for; matrix products, arithmetic and copies ran while one was open for 0% of the time, Pallas kernels for 3%

profile of v7, /device:TPU:0, one launch (start us, length us, event | category | flops | bytes accessed | tf_op | source)
XLA Modules:
  0.0 36.0 jit_solution(7304932501128747599)
XLA Ops:
  0.6 0.0 copy-start
  0.6 0.0 copy-start.4
  0.7 0.8 %copy-done.4 = f32[16,64]{1,0:T(8,128)S(1)} copy-done((f32[16,64]{1,0:T(8,128)S(1)}, f32[16,64]{1,0:T(8,128)}, u32[]{:S(2)}) %copy-start.4) | copy-done | bytes 4120
  1.4 0.0 copy-start.1
  1.4 0.0 copy-start.2
  1.4 0.1 shard_map.69.first_ref.gram_ref
  1.5 0.0 copy-start.3
  1.5 0.3 copy-done
  1.8 0.4 %copy-done.1 = s32[3,8,128]{2,1,0:T(8,128)S(1)} copy-done((s32[3,8,128]{2,1,0:T(8,128)S(1)}, s32[3,8,128]{2,1,0:T(8,128)}, u32[]{:S(2)}) %copy-start.1) | copy-done | bytes 12312
  2.2 0.0 copy-done.2
  2.2 0.0 copy-done.3
  2.2 0.5 %shard_map.70 = (f32[200,128]{1,0:T(8,128)S(1)}, f32[200,128]{1,0:T(8,128)S(1)}, f32[32,128]{1,0:T(8,128)S(1)}, f32[32,128]{1,0:T(8,128)S(1)}) custom-call(f32[1536,128]{1,0:T(8,128)S(1)} %bitcast.5, f32[24,128]{1,0:T(8,128)S(1)} %bitcast.15, s32[24,128]{1,0:T(8,128)S(1)} %bitcast.10, f32[8,128]{1,0:T(8,128)S(1)} %copy-done.3, ...), custom_call_target="tpu_custom_call" | custom-call | tf_op jit(solution)/shard_map/pallas_call | solution.py:669
  2.7 3.1 %collective-permute-start = (f32[200,128]{1,0:T(8,128)S(1)}, f32[200,128]{1,0:T(8,128)S(1)}, u32[]{:S(2)}, u32[]{:S(2)}) collective-permute-start(f32[200,128]{1,0:T(8,128)S(1)} %get-tuple-element.17), channel_id=1, source_target_pairs={{0,4},{1,5},{2,6},{3,7},{4,0},{5,1},{6,2},{7,3},{8,12},{9,13},{10,... | collective-permute-start | bytes 307208 | tf_op jit(solution)/shard_map/ppermute | solution.py:695
  5.8 0.0 collective-permute-start.1
  5.8 0.5 %collective-permute-start.2 = (f32[32,128]{1,0:T(8,128)S(1)}, f32[32,128]{1,0:T(8,128)S(1)}, u32[]{:S(2)}, u32[]{:S(2)}) collective-permute-start(f32[32,128]{1,0:T(8,128)S(1)} %get-tuple-element.19.owna_ref), channel_id=1, source_target_pairs={{0,1},{1,0},{2,3},{3,2},{4,5},{5,4},{6,7},{7,6},{8,9},{9,8},{10,11... | collective-permute-start | bytes 49160 | tf_op jit(solution)/shard_map/ppermute | solution.py:695
  6.3 2.5 %collective-permute-start.3 = (f32[32,128]{1,0:T(8,128)S(1)}, f32[32,128]{1,0:T(8,128)S(1)}, u32[]{:S(2)}, u32[]{:S(2)}) collective-permute-start(f32[32,128]{1,0:T(8,128)S(1)} %get-tuple-element.20.ownb_ref), channel_id=1, source_target_pairs={{0,4},{1,2},{2,1},{3,7},{4,0},{5,6},{6,5},{7,3},{8,12},{9,10},{10,... | collective-permute-start | bytes 49160 | tf_op jit(solution)/shard_map/ppermute | solution.py:695
  8.8 1.0 %shard_map.68 = (f32[64,128]{1,0:T(8,128)S(1)}, f32[8,128]{1,0:T(8,128)S(1)}) custom-call(f32[1536,128]{1,0:T(8,128)S(1)} %bitcast.6, f32[24,128]{1,0:T(8,128)S(1)} %bitcast.16, s32[24,128]{1,0:T(8,128)S(1)} %bitcast.11, f32[8,128]{1,0:T(8,128)S(1)} %copy-done.3), custom_call_target="tpu_custom_call" | custom-call | flops 100000000 | bytes 4096 | tf_op jit(solution)/shard_map/pallas_call | solution.py:669
  9.8 0.0 collective-permute-done.2.cola_ref.refs_6_
  9.8 0.7 %collective-permute-done.3.colb_ref.refs_7_ = f32[32,128]{1,0:T(8,128)S(1)} collective-permute-done((f32[32,128]{1,0:T(8,128)S(1)}, f32[32,128]{1,0:T(8,128)S(1)}, u32[]{:S(2)}, u32[]{:S(2)}) %collective-permute-start.3) | collective-permute-done | bytes 16416 | tf_op jit(solution)/shard_map/ppermute | solution.py:695
  10.5 0.0 collective-permute-done.rowa_ref.refs_4_
  10.5 0.0 collective-permute-done.1.rowb_ref.refs_5_
  10.6 0.6 %shard_map.71 = f32[32,4,128]{2,1,0:T(4,128)S(1)} custom-call(f32[64,128]{1,0:T(8,128)S(1)} %get-tuple-element.15.inner_ref, f32[8,128]{1,0:T(8,128)S(1)} %get-tuple-element.16.dots_ref, f32[1536,128]{1,0:T(8,128)S(1)} %bitcast.7, s32[24,128]{1,0:T(8,128)S(1)} %bitcast.12, f32[8,128]{1,0:T(8,128)S(1)} %copy-done.3, ...), custom_call_target="tpu_custom_call" | custom-call | tf_op jit(solution)/shard_map/pallas_call | solution.py:669
  11.1 12.9 %all_to_all.10.got_ref = f32[32,4,128]{2,1,0:T(4,128)S(1)} all-to-all(f32[32,4,128]{2,1,0:T(4,128)S(1)} %shard_map.71), channel_id=1, replica_groups=mesh['row'=8,'col'=4] {'row','col'}, dimensions={0} | all-to-all | bytes 131072 | tf_op jit(solution)/shard_map/all_to_all | solution.py:680
  24.0 0.7 %shard_map.72 = (f32[32,8,128]{2,1,0:T(8,128)S(1)}, f32[72,128]{1,0:T(8,128)S(1)}, f32[40,128]{1,0:T(8,128)S(1)}, f32[8,128]{1,0:T(8,128)S(1)}, f32[64,128]{1,0:T(8,128)S(1)}) custom-call(f32[32,4,128]{2,1,0:T(4,128)S(1)} %all_to_all.10.got_ref, f32[1536,128]{1,0:T(8,128)S(1)} %bitcast.8, f32[24,128]{1,0:T(8,128)S(1)} %bitcast.17, s32[24,128]{1,0:T(8,128)S(1)} %bitcast.13, ...), custom_call_target="tpu_custom_call" | custom-call | tf_op jit(solution)/shard_map/pallas_call | solution.py:669
  24.7 9.9 %all_to_all.11.got_ref = f32[32,8,128]{2,1,0:T(8,128)S(1)} all-to-all(f32[32,8,128]{2,1,0:T(8,128)S(1)} %get-tuple-element.21), channel_id=1, replica_groups=mesh['row'=8,'col'=4] {'row','col'}, dimensions={0} | all-to-all | bytes 262144 | tf_op jit(solution)/shard_map/all_to_all | solution.py:680
  34.6 1.4 %shard_map.73 = (f32[24,128]{1,0:T(8,128)}, f32[24,128]{1,0:T(8,128)}) custom-call(f32[32,8,128]{2,1,0:T(8,128)S(1)} %all_to_all.11.got_ref, f32[1536,128]{1,0:T(8,128)S(1)} %bitcast.9, f32[24,128]{1,0:T(8,128)S(1)} %bitcast.18, s32[24,128]{1,0:T(8,128)S(1)} %bitcast.14, f32[200,128]{1,0:T(8,128)S(1)} %collective-permute-done.rowa_ref.refs_4_, ...), custom_call_target="tpu_custom_call" | custom-call | tf_op jit(solution)/shard_map/pallas_call | solution.py:669
Async XLA Ops:
  0.6 1.1 %copy-start = (f32[64,3,8,128]{3,2,1,0:T(8,128)S(1)}, f32[64,3,8,128]{3,2,1,0:T(8,128)}, u32[]{:S(2)}) copy-start(f32[64,3,8,128]{3,2,1,0:T(8,128)} %param.8) | copy-start | bytes 2359300
  0.6 0.8 %copy-start.4 = (f32[16,64]{1,0:T(8,128)S(1)}, f32[16,64]{1,0:T(8,128)}, u32[]{:S(2)}) copy-start(f32[16,64]{1,0:T(8,128)} %gram_ref.1) | copy-start | bytes 12292
  1.4 0.8 %copy-start.1 = (s32[3,8,128]{2,1,0:T(8,128)S(1)}, s32[3,8,128]{2,1,0:T(8,128)}, u32[]{:S(2)}) copy-start(s32[3,8,128]{2,1,0:T(8,128)} %param.7) | copy-start | bytes 36868
  1.4 0.8 %copy-start.2 = (f32[3,8,128]{2,1,0:T(8,128)S(1)}, f32[3,8,128]{2,1,0:T(8,128)}, u32[]{:S(2)}) copy-start(f32[3,8,128]{2,1,0:T(8,128)} %param.5) | copy-start | bytes 36868
  1.5 0.7 %copy-start.3 = (f32[8,128]{1,0:T(8,128)S(1)}, f32[8,128]{1,0:T(8,128)}, u32[]{:S(2)}) copy-start(f32[8,128]{1,0:T(8,128)} %refs_3_.1) | copy-start | bytes 12292
  2.7 7.8 %collective-permute-start = (f32[200,128]{1,0:T(8,128)S(1)}, f32[200,128]{1,0:T(8,128)S(1)}, u32[]{:S(2)}, u32[]{:S(2)}) collective-permute-start(f32[200,128]{1,0:T(8,128)S(1)} %get-tuple-element.17), channel_id=1, source_target_pairs={{0,4},{1,5},{2,6},{3,7},{4,0},{5,1},{6,2},{7,3},{8,12},{9,13},{10,... | collective-permute-start | bytes 307208 | tf_op jit(solution)/shard_map/ppermute | solution.py:695
  5.8 4.8 %collective-permute-start.1 = (f32[200,128]{1,0:T(8,128)S(1)}, f32[200,128]{1,0:T(8,128)S(1)}, u32[]{:S(2)}, u32[]{:S(2)}) collective-permute-start(f32[200,128]{1,0:T(8,128)S(1)} %get-tuple-element.18), channel_id=1, source_target_pairs={{0,1},{1,0},{2,3},{3,2},{4,8},{5,9},{6,10},{7,11},{8,4},{9,5},{10,... | collective-permute-start | bytes 307208 | tf_op jit(solution)/shard_map/ppermute | solution.py:695
  5.8 4.0 %collective-permute-start.2 = (f32[32,128]{1,0:T(8,128)S(1)}, f32[32,128]{1,0:T(8,128)S(1)}, u32[]{:S(2)}, u32[]{:S(2)}) collective-permute-start(f32[32,128]{1,0:T(8,128)S(1)} %get-tuple-element.19.owna_ref), channel_id=1, source_target_pairs={{0,1},{1,0},{2,3},{3,2},{4,5},{5,4},{6,7},{7,6},{8,9},{9,8},{10,11... | collective-permute-start | bytes 49160 | tf_op jit(solution)/shard_map/ppermute | solution.py:695
  6.3 4.2 %collective-permute-start.3 = (f32[32,128]{1,0:T(8,128)S(1)}, f32[32,128]{1,0:T(8,128)S(1)}, u32[]{:S(2)}, u32[]{:S(2)}) collective-permute-start(f32[32,128]{1,0:T(8,128)S(1)} %get-tuple-element.20.ownb_ref), channel_id=1, source_target_pairs={{0,4},{1,2},{2,1},{3,7},{4,0},{5,6},{6,5},{7,3},{8,12},{9,10},{10,... | collective-permute-start | bytes 49160 | tf_op jit(solution)/shard_map/ppermute | solution.py:695

commit v8 on v7

--- a/solution.py
+++ b/solution.py
@@ -101,14 +101,16 @@
     send_ref[...] = jnp.broadcast_to(both[None], send_ref.shape)
 
 
-def piece_kernel(gram_ref, piece_ref):
-    at = 2 * lax.axis_index("row")
-    rows = [gram_ref[pl.ds(at + t, 1), :] for t in range(2)]
-    piece_ref[...] = jnp.concatenate(rows, axis=1)
-
-
-def packets_kernel(sizes, basis_ref, rhs_ref, mask_ref, visc_ref, first_ref, *packet_refs):
-    packet_kernel(sizes, basis_ref, rhs_ref, mask_ref, visc_ref, *packet_refs)
+def open_kernel(out_ref):
+    out_ref[...] = jnp.zeros_like(out_ref)
+
+
+def rows_kernel(sizes, basis_ref, rhs_ref, mask_ref, visc_ref, first_ref, rowa_ref, rowb_ref):
+    packet_kernel(sizes, basis_ref, rhs_ref, mask_ref, visc_ref, rowa_ref, rowb_ref, None, None)
+
+
+def sides_kernel(sizes, basis_ref, rhs_ref, mask_ref, visc_ref, cola_ref, colb_ref):
+    packet_kernel(sizes, basis_ref, rhs_ref, mask_ref, visc_ref, None, None, cola_ref, colb_ref)
 
 
 def corners_of(visc):
@@ -127,25 +129,28 @@
     lane = iota((rows, cols), 1)
     top, low = rows - 1, cols - 1
 
-    for c in range(comps):
-        north = basis_ref[pl.ds(c * rows + top, columns, stride=comps * rows), :]
-        south = basis_ref[pl.ds(c * rows, columns, stride=comps * rows), :]
-        north = north * mask[c][top : top + 1, :]
-        south = south * mask[c][0:1, :]
-        rowa_ref[c * columns : (c + 1) * columns, :] = pick(even_row, north, south)
-        rowb_ref[c * columns : (c + 1) * columns, :] = pick(even_row, south, north)
-    north = [mask[c][top : top + 1, :] * rhs[c][top : top + 1, :] for c in range(comps)]
-    south = [mask[c][0:1, :] * rhs[c][0:1, :] for c in range(comps)]
-    north += [visc[top : top + 1, :], visc[top - 1 : top, :]]
-    south += [visc[0:1, :], visc[1:2, :]]
-    for i in range(comps + 2):
-        at = comps * columns + i
-        rowa_ref[at : at + 1, :] = pick(even_row, north[i], south[i])
-        rowb_ref[at : at + 1, :] = pick(even_row, south[i], north[i])
-    rest = comps * columns + comps + 2
-    blank = jnp.zeros((rowa_ref.shape[0] - rest, cols), F32)
-    rowa_ref[rest:, :] = blank
-    rowb_ref[rest:, :] = blank
+    if rowa_ref is not None:
+        for c in range(comps):
+            north = basis_ref[pl.ds(c * rows + top, columns, stride=comps * rows), :]
+            south = basis_ref[pl.ds(c * rows, columns, stride=comps * rows), :]
+            north = north * mask[c][top : top + 1, :]
+            south = south * mask[c][0:1, :]
+            rowa_ref[c * columns : (c + 1) * columns, :] = pick(even_row, north, south)
+            rowb_ref[c * columns : (c + 1) * columns, :] = pick(even_row, south, north)
+        north = [mask[c][top : top + 1, :] * rhs[c][top : top + 1, :] for c in range(comps)]
+        south = [mask[c][0:1, :] * rhs[c][0:1, :] for c in range(comps)]
+        north += [visc[top : top + 1, :], visc[top - 1 : top, :]]
+        south += [visc[0:1, :], visc[1:2, :]]
+        for i in range(comps + 2):
+            at = comps * columns + i
+            rowa_ref[at : at + 1, :] = pick(even_row, north[i], south[i])
+            rowb_ref[at : at + 1, :] = pick(even_row, south[i], north[i])
+        rest = comps * columns + comps + 2
+        blank = jnp.zeros((rowa_ref.shape[0] - rest, cols), F32)
+        rowa_ref[rest:, :] = blank
+        rowb_ref[rest:, :] = blank
+    if cola_ref is None:
+        return
 
     for c in range(comps):
         east, west = (jnp.zeros((rows, cols), F32), jnp.zeros((rows, cols), F32))
@@ -281,7 +286,9 @@
     corner_row = jnp.zeros((1, cols), F32)
     for i, corner in enumerate(corners_of(visc)):
         corner_row = jnp.where(lanes == i, corner, corner_row)
-    head = jnp.concatenate([jnp.where(lanes < half, dots, spine), gram_ref[...]], axis=0)
+    at = 2 * lax.axis_index("row")
+    piece = jnp.concatenate([gram_ref[pl.ds(at + t, 1), :] for t in range(2)], axis=1)
+    head = jnp.concatenate([jnp.where(lanes < half, dots, spine), piece], axis=0)
     for d in range(count):
         send_ref[d] = jnp.concatenate([head, chunk[d : d + 1, :], corner_row], axis=0)
 
@@ -702,7 +709,8 @@
     piece = -(-block // row_count)
     two = columns * columns == devices * cols and cols == 2 * columns and rows == 8 and comps == 3
     if two:
-        (own,) = call(piece_kernel, [(1, cols)], [], gram_inverse, flops=10**9)
+        (first,) = call(open_kernel, [(8, cols)], [], flops=10**9)
+        own = gram_inverse
     else:
         flat = jnp.pad(gram_inverse.reshape(-1), (0, piece * row_count - block))
         own = lax.dynamic_slice_in_dim(flat, lax.axis_index("row") * piece, piece)
@@ -712,11 +720,17 @@
     wide = (comps + 1) * rows
     field = comps * rows
     if two:
-        row_a, row_b, col_a, col_b = call(
-            functools.partial(packets_kernel, sizes),
-            [(tall, cols), (tall, cols), (wide, cols), (wide, cols)],
+        row_a, row_b = call(
+            functools.partial(rows_kernel, sizes),
+            [(tall, cols), (tall, cols)],
             [],
-            basis, rhs, mask, viscosity, own,
+            basis, rhs, mask, viscosity, first,
+        )
+        col_a, col_b = call(
+            functools.partial(sides_kernel, sizes),
+            [(wide, cols), (wide, cols)],
+            [],
+            basis, rhs, mask, viscosity,
         )
         packets = ((row_a, "row", 0), (row_b, "row", 1), (col_a, "col", 0), (col_b, "col", 1))
         halos = []

time: 36.3 us -> 35.3 us (0.972)
  blocking collectives: 22.8 us -> 22.2 us
  local copies, waits for them, and re-layouts: 1.51 us -> 1.1 us
    all_to_all x2, blocking collectives: 22.8 us -> 22.2 us  [share(): return lax.all_to_all(message, ('row', 'col'), 0, 0, tiled=True)]
    unnamed x10, local copies, waits for them, and re-layouts: 1.51 us -> 1.1 us
    pallas_call x6 -> x7, Pallas kernels: 4.14 us -> 4.11 us  [call(): pl.pallas_call(kernel, out_shape=[jax.ShapeDtypeStruct(s, F32) for s in o...]
  transfers between devices with their start and end apart: 4 -> 4, of which waited for: 1 -> 1; matrix products, arithmetic and copies ran while one was open for 0% -> 0% of each run, Pallas kernels for 3% -> 4%
where the time goes in v8:
time: 35.3 us; the launch traced here: 35.1 us
  blocking collectives  22.2 us (63%)
  starting transfers between devices  6.24 us (18%)
  Pallas kernels  4.11 us (12%)
  local copies, waits for them, and re-layouts  1.1 us (3%)
  waiting for transfers between devices  0.73 us (2%)
  between operations  0.71 us (2%)
    all_to_all x2, blocking collectives, share(): return lax.all_to_all(message, ('row', 'col'), 0, 0, tiled=True)  22.2 us
    ppermute x4, starting transfers between devices, swap(): return lax.ppermute(packet, ('row', 'col'), pairs)  6.24 us
    pallas_call x7, Pallas kernels, call(): pl.pallas_call(kernel, out_shape=[jax.ShapeDtypeStruct(s, F32) for s in o...  4.11 us
    unnamed x10, local copies, waits for them, and re-layouts  1.1 us
    ppermute x4, waiting for transfers between devices, swap(): return lax.ppermute(packet, ('row', 'col'), pairs)  0.73 us
  transfers between devices with their start and end apart: 4, of which 1 were waited for; matrix products, arithmetic and copies ran while one was open for 0% of the time, Pallas kernels for 4%

profile of v8, /device:TPU:0, one launch (start us, length us, event | category | flops | bytes accessed | tf_op | source)
XLA Modules:
  0.0 35.1 jit_solution(8309632138693968331)
XLA Ops:
  0.6 0.0 copy-start
  0.6 0.0 copy-start.1
  0.6 0.0 copy-start.2
  0.7 0.0 copy-start.3
  0.7 1.1 %copy-done = f32[64,3,8,128]{3,2,1,0:T(8,128)S(1)} copy-done((f32[64,3,8,128]{3,2,1,0:T(8,128)S(1)}, f32[64,3,8,128]{3,2,1,0:T(8,128)}, u32[]{:S(2)}) %copy-start) | copy-done | bytes 786456
  1.8 0.0 copy-done.1
  1.8 0.0 copy-done.2
  1.8 0.0 copy-done.3
  1.8 3.1 %collective-permute-start = (f32[200,128]{1,0:T(8,128)S(1)}, f32[200,128]{1,0:T(8,128)S(1)}, u32[]{:S(2)}, u32[]{:S(2)}) collective-permute-start(f32[200,128]{1,0:T(8,128)S(1)} %get-tuple-element.17), channel_id=1, source_target_pairs={{0,4},{1,5},{2,6},{3,7},{4,0},{5,1},{6,2},{7,3},{8,12},{9,13},{10,... | collective-permute-start | bytes 307208 | tf_op jit(solution)/shard_map/ppermute | solution.py:702
  4.9 0.0 collective-permute-start.1
  4.9 0.5 %shard_map.71 = (f32[32,128]{1,0:T(8,128)S(1)}, f32[32,128]{1,0:T(8,128)S(1)}) custom-call(f32[1536,128]{1,0:T(8,128)S(1)} %bitcast.6, f32[24,128]{1,0:T(8,128)S(1)} %bitcast.18, s32[24,128]{1,0:T(8,128)S(1)} %bitcast.12, f32[8,128]{1,0:T(8,128)S(1)} %copy-done.3), custom_call_target="tpu_custom_call" | custom-call | tf_op jit(solution)/shard_map/pallas_call | solution.py:676
  5.4 0.6 %collective-permute-start.2 = (f32[32,128]{1,0:T(8,128)S(1)}, f32[32,128]{1,0:T(8,128)S(1)}, u32[]{:S(2)}, u32[]{:S(2)}) collective-permute-start(f32[32,128]{1,0:T(8,128)S(1)} %get-tuple-element.19.owna_ref), channel_id=1, source_target_pairs={{0,1},{1,0},{2,3},{3,2},{4,5},{5,4},{6,7},{7,6},{8,9},{9,8},{10,11... | collective-permute-start | bytes 49160 | tf_op jit(solution)/shard_map/ppermute | solution.py:702
  5.9 2.6 %collective-permute-start.3 = (f32[32,128]{1,0:T(8,128)S(1)}, f32[32,128]{1,0:T(8,128)S(1)}, u32[]{:S(2)}, u32[]{:S(2)}) collective-permute-start(f32[32,128]{1,0:T(8,128)S(1)} %get-tuple-element.20.ownb_ref), channel_id=1, source_target_pairs={{0,4},{1,2},{2,1},{3,7},{4,0},{5,6},{6,5},{7,3},{8,12},{9,10},{10,... | collective-permute-start | bytes 49160 | tf_op jit(solution)/shard_map/ppermute | solution.py:702
  8.6 0.0 copy-start.4
  8.6 1.0 %shard_map.68 = (f32[64,128]{1,0:T(8,128)S(1)}, f32[8,128]{1,0:T(8,128)S(1)}) custom-call(f32[1536,128]{1,0:T(8,128)S(1)} %bitcast.7, f32[24,128]{1,0:T(8,128)S(1)} %bitcast.19, s32[24,128]{1,0:T(8,128)S(1)} %bitcast.13, f32[8,128]{1,0:T(8,128)S(1)} %copy-done.3), custom_call_target="tpu_custom_call" | custom-call | flops 100000000 | bytes 4096 | tf_op jit(solution)/shard_map/pallas_call | solution.py:676
  9.5 0.0 collective-permute-done.2.cola_ref.refs_6_
  9.5 0.7 %collective-permute-done.3.colb_ref.refs_7_ = f32[32,128]{1,0:T(8,128)S(1)} collective-permute-done((f32[32,128]{1,0:T(8,128)S(1)}, f32[32,128]{1,0:T(8,128)S(1)}, u32[]{:S(2)}, u32[]{:S(2)}) %collective-permute-start.3) | collective-permute-done | bytes 16416 | tf_op jit(solution)/shard_map/ppermute | solution.py:702
  10.3 0.0 collective-permute-done.rowa_ref.refs_4_
  10.3 0.0 collective-permute-done.1.rowb_ref.refs_5_
  10.3 0.0 copy-done.4
  10.3 0.6 %shard_map.72 = f32[32,4,128]{2,1,0:T(4,128)S(1)} custom-call(f32[64,128]{1,0:T(8,128)S(1)} %get-tuple-element.15.inner_ref, f32[8,128]{1,0:T(8,128)S(1)} %get-tuple-element.16.dots_ref, f32[1536,128]{1,0:T(8,128)S(1)} %bitcast.8, s32[24,128]{1,0:T(8,128)S(1)} %bitcast.14, f32[8,128]{1,0:T(8,128)S(1)} %copy-done.3, f32[16,64]{1,0:T(8,128)S(1)} %copy-done.4, ...), custom_call_target="tpu_custom_call" | custom-call | tf_op jit(solution)/shard_map/pallas_call | solution.py:676
  10.8 12.3 %all_to_all.10.got_ref = f32[32,4,128]{2,1,0:T(4,128)S(1)} all-to-all(f32[32,4,128]{2,1,0:T(4,128)S(1)} %shard_map.72), channel_id=1, replica_groups=mesh['row'=8,'col'=4] {'row','col'}, dimensions={0} | all-to-all | bytes 131072 | tf_op jit(solution)/shard_map/all_to_all | solution.py:687
  23.1 0.7 %shard_map.73 = (f32[32,8,128]{2,1,0:T(8,128)S(1)}, f32[72,128]{1,0:T(8,128)S(1)}, f32[40,128]{1,0:T(8,128)S(1)}, f32[8,128]{1,0:T(8,128)S(1)}, f32[64,128]{1,0:T(8,128)S(1)}) custom-call(f32[32,4,128]{2,1,0:T(4,128)S(1)} %all_to_all.10.got_ref, f32[1536,128]{1,0:T(8,128)S(1)} %bitcast.9, f32[24,128]{1,0:T(8,128)S(1)} %bitcast.20, s32[24,128]{1,0:T(8,128)S(1)} %bitcast.15, ...), custom_call_target="tpu_custom_call" | custom-call | tf_op jit(solution)/shard_map/pallas_call | solution.py:676
  23.8 9.9 %all_to_all.11.got_ref = f32[32,8,128]{2,1,0:T(8,128)S(1)} all-to-all(f32[32,8,128]{2,1,0:T(8,128)S(1)} %get-tuple-element.21), channel_id=1, replica_groups=mesh['row'=8,'col'=4] {'row','col'}, dimensions={0} | all-to-all | bytes 262144 | tf_op jit(solution)/shard_map/all_to_all | solution.py:687
  33.7 1.4 %shard_map.74 = (f32[24,128]{1,0:T(8,128)}, f32[24,128]{1,0:T(8,128)}) custom-call(f32[32,8,128]{2,1,0:T(8,128)S(1)} %all_to_all.11.got_ref, f32[1536,128]{1,0:T(8,128)S(1)} %bitcast.10, f32[24,128]{1,0:T(8,128)S(1)} %bitcast.21, s32[24,128]{1,0:T(8,128)S(1)} %bitcast.16, f32[200,128]{1,0:T(8,128)S(1)} %collective-permute-done.rowa_ref.refs_4_, ...), custom_call_target="tpu_custom_call" | custom-call | tf_op jit(solution)/shard_map/pallas_call | solution.py:676
  (2 shorter events, 0.0 us)
Async XLA Ops:
  0.6 1.1 %copy-start = (f32[64,3,8,128]{3,2,1,0:T(8,128)S(1)}, f32[64,3,8,128]{3,2,1,0:T(8,128)}, u32[]{:S(2)}) copy-start(f32[64,3,8,128]{3,2,1,0:T(8,128)} %param.8) | copy-start | bytes 2359300
  0.6 1.1 %copy-start.1 = (s32[3,8,128]{2,1,0:T(8,128)S(1)}, s32[3,8,128]{2,1,0:T(8,128)}, u32[]{:S(2)}) copy-start(s32[3,8,128]{2,1,0:T(8,128)} %param.7) | copy-start | bytes 36868
  0.6 1.1 %copy-start.2 = (f32[3,8,128]{2,1,0:T(8,128)S(1)}, f32[3,8,128]{2,1,0:T(8,128)}, u32[]{:S(2)}) copy-start(f32[3,8,128]{2,1,0:T(8,128)} %param.5) | copy-start | bytes 36868
  0.7 1.1 %copy-start.3 = (f32[8,128]{1,0:T(8,128)S(1)}, f32[8,128]{1,0:T(8,128)}, u32[]{:S(2)}) copy-start(f32[8,128]{1,0:T(8,128)} %refs_3_.1) | copy-start | bytes 12292
  1.8 8.5 %collective-permute-start = (f32[200,128]{1,0:T(8,128)S(1)}, f32[200,128]{1,0:T(8,128)S(1)}, u32[]{:S(2)}, u32[]{:S(2)}) collective-permute-start(f32[200,128]{1,0:T(8,128)S(1)} %get-tuple-element.17), channel_id=1, source_target_pairs={{0,4},{1,5},{2,6},{3,7},{4,0},{5,1},{6,2},{7,3},{8,12},{9,13},{10,... | collective-permute-start | bytes 307208 | tf_op jit(solution)/shard_map/ppermute | solution.py:702
  4.9 5.4 %collective-permute-start.1 = (f32[200,128]{1,0:T(8,128)S(1)}, f32[200,128]{1,0:T(8,128)S(1)}, u32[]{:S(2)}, u32[]{:S(2)}) collective-permute-start(f32[200,128]{1,0:T(8,128)S(1)} %get-tuple-element.18), channel_id=1, source_target_pairs={{0,1},{1,0},{2,3},{3,2},{4,8},{5,9},{6,10},{7,11},{8,4},{9,5},{10,... | collective-permute-start | bytes 307208 | tf_op jit(solution)/shard_map/ppermute | solution.py:702
  5.4 4.2 %collective-permute-start.2 = (f32[32,128]{1,0:T(8,128)S(1)}, f32[32,128]{1,0:T(8,128)S(1)}, u32[]{:S(2)}, u32[]{:S(2)}) collective-permute-start(f32[32,128]{1,0:T(8,128)S(1)} %get-tuple-element.19.owna_ref), channel_id=1, source_target_pairs={{0,1},{1,0},{2,3},{3,2},{4,5},{5,4},{6,7},{7,6},{8,9},{9,8},{10,11... | collective-permute-start | bytes 49160 | tf_op jit(solution)/shard_map/ppermute | solution.py:702
  5.9 4.3 %collective-permute-start.3 = (f32[32,128]{1,0:T(8,128)S(1)}, f32[32,128]{1,0:T(8,128)S(1)}, u32[]{:S(2)}, u32[]{:S(2)}) collective-permute-start(f32[32,128]{1,0:T(8,128)S(1)} %get-tuple-element.20.ownb_ref), channel_id=1, source_target_pairs={{0,4},{1,2},{2,1},{3,7},{4,0},{5,6},{6,5},{7,3},{8,12},{9,10},{10,... | collective-permute-start | bytes 49160 | tf_op jit(solution)/shard_map/ppermute | solution.py:702
  8.6 1.7 %copy-start.4 = (f32[16,64]{1,0:T(8,128)S(1)}, f32[16,64]{1,0:T(8,128)}, u32[]{:S(2)}) copy-start(f32[16,64]{1,0:T(8,128)} %gram_ref.1) | copy-start | bytes 12292

commit v9 on v8

--- a/solution.py
+++ b/solution.py
@@ -157,8 +157,10 @@
         for k in range(columns):
             base = (k * comps + c) * rows
             tile = basis_ref[base : base + rows, :]
-            east = jnp.where(lane == k, pltpu.roll(tile, (k - low) % cols, 1), east)
-            west = jnp.where(lane == k, tile if k == 0 else pltpu.roll(tile, k, 1), west)
+            tile = pltpu.roll(tile, k + 1, 1)
+            east = jnp.where(lane == k, tile, east)
+            west = jnp.where(lane == k + 1, tile, west)
+        west = pltpu.roll(west, low, 1)
         east = jnp.where(lane == columns, rhs[c][:, low : low + 1], east)
         west = jnp.where(lane == columns, rhs[c][:, 0:1], west)
         east = east * mask[c][:, low : low + 1]
@@ -609,9 +611,11 @@
         moved.append(value)
         moved_image.append(stencil(mask[c], faces, diagonal, value, (north, south, east, west)))
 
-    border = jnp.zeros((2 * comps + 2, cols), F32)
+    parts = [jnp.zeros((2 * comps + 2, cols), F32) for _ in range(4)]
     for d in range(devices - col_count):
-        border = border + got_ref[d] * pltpu.roll(got_ref[d + col_count], comps + 2, 0)
+        value = got_ref[d] * pltpu.roll(got_ref[d + col_count], comps + 2, 0)
+        parts[d % 4] = parts[d % 4] + value
+    border = (parts[0] + parts[1]) + (parts[2] + parts[3])
     border = jnp.where(iota(border.shape, 0) < comps, border, 0.0)
     lines = got_ref[:, 2 * comps, :]
     later = pltpu.roll(pltpu.roll(lines, devices - 1, 0), cols - (WEST2 - EAST2), 1)

time: 35.3 us -> 35.3 us (level)
  no operation moved by 1% of the time
where the time goes in v9:
time: 35.3 us; the launch traced here: 35.1 us
  blocking collectives  22.3 us (63%)
  starting transfers between devices  6.24 us (18%)
  Pallas kernels  4 us (11%)
  local copies, waits for them, and re-layouts  1.1 us (3%)
  waiting for transfers between devices  0.74 us (2%)
  between operations  0.72 us (2%)
    all_to_all x2, blocking collectives, share(): return lax.all_to_all(message, ('row', 'col'), 0, 0, tiled=True)  22.3 us
    ppermute x4, starting transfers between devices, swap(): return lax.ppermute(packet, ('row', 'col'), pairs)  6.24 us
    pallas_call x7, Pallas kernels, call(): pl.pallas_call(kernel, out_shape=[jax.ShapeDtypeStruct(s, F32) for s in o...  4 us
    unnamed x10, local copies, waits for them, and re-layouts  1.1 us
    ppermute x4, waiting for transfers between devices, swap(): return lax.ppermute(packet, ('row', 'col'), pairs)  0.74 us
  transfers between devices with their start and end apart: 4, of which 1 were waited for; matrix products, arithmetic and copies ran while one was open for 0% of the time, Pallas kernels for 4%

profile of v9, /device:TPU:0, one launch (start us, length us, event | category | flops | bytes accessed | tf_op | source)
XLA Modules:
  0.0 35.1 jit_solution(4549797566584091541)
XLA Ops:
  0.6 0.0 copy-start
  0.6 0.0 copy-start.1
  0.6 0.0 copy-start.2
  0.7 0.0 copy-start.3
  0.7 1.1 %copy-done = f32[64,3,8,128]{3,2,1,0:T(8,128)S(1)} copy-done((f32[64,3,8,128]{3,2,1,0:T(8,128)S(1)}, f32[64,3,8,128]{3,2,1,0:T(8,128)}, u32[]{:S(2)}) %copy-start) | copy-done | bytes 786456
  1.8 0.0 copy-done.1
  1.8 0.0 copy-done.2
  1.8 0.0 copy-done.3
  1.8 3.1 %collective-permute-start = (f32[200,128]{1,0:T(8,128)S(1)}, f32[200,128]{1,0:T(8,128)S(1)}, u32[]{:S(2)}, u32[]{:S(2)}) collective-permute-start(f32[200,128]{1,0:T(8,128)S(1)} %get-tuple-element.17), channel_id=1, source_target_pairs={{0,4},{1,5},{2,6},{3,7},{4,0},{5,1},{6,2},{7,3},{8,12},{9,13},{10,... | collective-permute-start | bytes 307208 | tf_op jit(solution)/shard_map/ppermute | solution.py:706
  4.9 0.0 collective-permute-start.1
  4.9 0.4 %shard_map.71 = (f32[32,128]{1,0:T(8,128)S(1)}, f32[32,128]{1,0:T(8,128)S(1)}) custom-call(f32[1536,128]{1,0:T(8,128)S(1)} %bitcast.6, f32[24,128]{1,0:T(8,128)S(1)} %bitcast.18, s32[24,128]{1,0:T(8,128)S(1)} %bitcast.12, f32[8,128]{1,0:T(8,128)S(1)} %copy-done.3), custom_call_target="tpu_custom_call" | custom-call | tf_op jit(solution)/shard_map/pallas_call | solution.py:680
  5.3 0.6 %collective-permute-start.2 = (f32[32,128]{1,0:T(8,128)S(1)}, f32[32,128]{1,0:T(8,128)S(1)}, u32[]{:S(2)}, u32[]{:S(2)}) collective-permute-start(f32[32,128]{1,0:T(8,128)S(1)} %get-tuple-element.19.owna_ref), channel_id=1, source_target_pairs={{0,1},{1,0},{2,3},{3,2},{4,5},{5,4},{6,7},{7,6},{8,9},{9,8},{10,11... | collective-permute-start | bytes 49160 | tf_op jit(solution)/shard_map/ppermute | solution.py:706
  5.8 2.6 %collective-permute-start.3 = (f32[32,128]{1,0:T(8,128)S(1)}, f32[32,128]{1,0:T(8,128)S(1)}, u32[]{:S(2)}, u32[]{:S(2)}) collective-permute-start(f32[32,128]{1,0:T(8,128)S(1)} %get-tuple-element.20.ownb_ref), channel_id=1, source_target_pairs={{0,4},{1,2},{2,1},{3,7},{4,0},{5,6},{6,5},{7,3},{8,12},{9,10},{10,... | collective-permute-start | bytes 49160 | tf_op jit(solution)/shard_map/ppermute | solution.py:706
  8.5 0.0 copy-start.4
  8.5 1.0 %shard_map.68 = (f32[64,128]{1,0:T(8,128)S(1)}, f32[8,128]{1,0:T(8,128)S(1)}) custom-call(f32[1536,128]{1,0:T(8,128)S(1)} %bitcast.7, f32[24,128]{1,0:T(8,128)S(1)} %bitcast.19, s32[24,128]{1,0:T(8,128)S(1)} %bitcast.13, f32[8,128]{1,0:T(8,128)S(1)} %copy-done.3), custom_call_target="tpu_custom_call" | custom-call | flops 100000000 | bytes 4096 | tf_op jit(solution)/shard_map/pallas_call | solution.py:680
  9.4 0.0 collective-permute-done.2.cola_ref.refs_6_
  9.4 0.7 %collective-permute-done.3.colb_ref.refs_7_ = f32[32,128]{1,0:T(8,128)S(1)} collective-permute-done((f32[32,128]{1,0:T(8,128)S(1)}, f32[32,128]{1,0:T(8,128)S(1)}, u32[]{:S(2)}, u32[]{:S(2)}) %collective-permute-start.3) | collective-permute-done | bytes 16416 | tf_op jit(solution)/shard_map/ppermute | solution.py:706
  10.2 0.0 collective-permute-done.rowa_ref.refs_4_
  10.2 0.0 collective-permute-done.1.rowb_ref.refs_5_
  10.2 0.0 copy-done.4
  10.2 0.6 %shard_map.72 = f32[32,4,128]{2,1,0:T(4,128)S(1)} custom-call(f32[64,128]{1,0:T(8,128)S(1)} %get-tuple-element.15.inner_ref, f32[8,128]{1,0:T(8,128)S(1)} %get-tuple-element.16.dots_ref, f32[1536,128]{1,0:T(8,128)S(1)} %bitcast.8, s32[24,128]{1,0:T(8,128)S(1)} %bitcast.14, f32[8,128]{1,0:T(8,128)S(1)} %copy-done.3, f32[16,64]{1,0:T(8,128)S(1)} %copy-done.4, ...), custom_call_target="tpu_custom_call" | custom-call | tf_op jit(solution)/shard_map/pallas_call | solution.py:680
  10.7 12.4 %all_to_all.10.got_ref = f32[32,4,128]{2,1,0:T(4,128)S(1)} all-to-all(f32[32,4,128]{2,1,0:T(4,128)S(1)} %shard_map.72), channel_id=1, replica_groups=mesh['row'=8,'col'=4] {'row','col'}, dimensions={0} | all-to-all | bytes 131072 | tf_op jit(solution)/shard_map/all_to_all | solution.py:691
  23.1 0.7 %shard_map.73 = (f32[32,8,128]{2,1,0:T(8,128)S(1)}, f32[72,128]{1,0:T(8,128)S(1)}, f32[40,128]{1,0:T(8,128)S(1)}, f32[8,128]{1,0:T(8,128)S(1)}, f32[64,128]{1,0:T(8,128)S(1)}) custom-call(f32[32,4,128]{2,1,0:T(4,128)S(1)} %all_to_all.10.got_ref, f32[1536,128]{1,0:T(8,128)S(1)} %bitcast.9, f32[24,128]{1,0:T(8,128)S(1)} %bitcast.20, s32[24,128]{1,0:T(8,128)S(1)} %bitcast.15, ...), custom_call_target="tpu_custom_call" | custom-call | tf_op jit(solution)/shard_map/pallas_call | solution.py:680
  23.8 9.9 %all_to_all.11.got_ref = f32[32,8,128]{2,1,0:T(8,128)S(1)} all-to-all(f32[32,8,128]{2,1,0:T(8,128)S(1)} %get-tuple-element.21), channel_id=1, replica_groups=mesh['row'=8,'col'=4] {'row','col'}, dimensions={0} | all-to-all | bytes 262144 | tf_op jit(solution)/shard_map/all_to_all | solution.py:691
  33.7 1.4 %shard_map.74 = (f32[24,128]{1,0:T(8,128)}, f32[24,128]{1,0:T(8,128)}) custom-call(f32[32,8,128]{2,1,0:T(8,128)S(1)} %all_to_all.11.got_ref, f32[1536,128]{1,0:T(8,128)S(1)} %bitcast.10, f32[24,128]{1,0:T(8,128)S(1)} %bitcast.21, s32[24,128]{1,0:T(8,128)S(1)} %bitcast.16, f32[200,128]{1,0:T(8,128)S(1)} %collective-permute-done.rowa_ref.refs_4_, ...), custom_call_target="tpu_custom_call" | custom-call | tf_op jit(solution)/shard_map/pallas_call | solution.py:680
  (2 shorter events, 0.0 us)
Async XLA Ops:
  0.6 1.1 %copy-start = (f32[64,3,8,128]{3,2,1,0:T(8,128)S(1)}, f32[64,3,8,128]{3,2,1,0:T(8,128)}, u32[]{:S(2)}) copy-start(f32[64,3,8,128]{3,2,1,0:T(8,128)} %param.8) | copy-start | bytes 2359300
  0.6 1.1 %copy-start.1 = (s32[3,8,128]{2,1,0:T(8,128)S(1)}, s32[3,8,128]{2,1,0:T(8,128)}, u32[]{:S(2)}) copy-start(s32[3,8,128]{2,1,0:T(8,128)} %param.7) | copy-start | bytes 36868
  0.6 1.1 %copy-start.2 = (f32[3,8,128]{2,1,0:T(8,128)S(1)}, f32[3,8,128]{2,1,0:T(8,128)}, u32[]{:S(2)}) copy-start(f32[3,8,128]{2,1,0:T(8,128)} %param.5) | copy-start | bytes 36868
  0.7 1.1 %copy-start.3 = (f32[8,128]{1,0:T(8,128)S(1)}, f32[8,128]{1,0:T(8,128)}, u32[]{:S(2)}) copy-start(f32[8,128]{1,0:T(8,128)} %refs_3_.1) | copy-start | bytes 12292
  1.8 8.4 %collective-permute-start = (f32[200,128]{1,0:T(8,128)S(1)}, f32[200,128]{1,0:T(8,128)S(1)}, u32[]{:S(2)}, u32[]{:S(2)}) collective-permute-start(f32[200,128]{1,0:T(8,128)S(1)} %get-tuple-element.17), channel_id=1, source_target_pairs={{0,4},{1,5},{2,6},{3,7},{4,0},{5,1},{6,2},{7,3},{8,12},{9,13},{10,... | collective-permute-start | bytes 307208 | tf_op jit(solution)/shard_map/ppermute | solution.py:706
  4.9 5.3 %collective-permute-start.1 = (f32[200,128]{1,0:T(8,128)S(1)}, f32[200,128]{1,0:T(8,128)S(1)}, u32[]{:S(2)}, u32[]{:S(2)}) collective-permute-start(f32[200,128]{1,0:T(8,128)S(1)} %get-tuple-element.18), channel_id=1, source_target_pairs={{0,1},{1,0},{2,3},{3,2},{4,8},{5,9},{6,10},{7,11},{8,4},{9,5},{10,... | collective-permute-start | bytes 307208 | tf_op jit(solution)/shard_map/ppermute | solution.py:706
  5.3 4.2 %collective-permute-start.2 = (f32[32,128]{1,0:T(8,128)S(1)}, f32[32,128]{1,0:T(8,128)S(1)}, u32[]{:S(2)}, u32[]{:S(2)}) collective-permute-start(f32[32,128]{1,0:T(8,128)S(1)} %get-tuple-element.19.owna_ref), channel_id=1, source_target_pairs={{0,1},{1,0},{2,3},{3,2},{4,5},{5,4},{6,7},{7,6},{8,9},{9,8},{10,11... | collective-permute-start | bytes 49160 | tf_op jit(solution)/shard_map/ppermute | solution.py:706
  5.8 4.3 %collective-permute-start.3 = (f32[32,128]{1,0:T(8,128)S(1)}, f32[32,128]{1,0:T(8,128)S(1)}, u32[]{:S(2)}, u32[]{:S(2)}) collective-permute-start(f32[32,128]{1,0:T(8,128)S(1)} %get-tuple-element.20.ownb_ref), channel_id=1, source_target_pairs={{0,4},{1,2},{2,1},{3,7},{4,0},{5,6},{6,5},{7,3},{8,12},{9,10},{10,... | collective-permute-start | bytes 49160 | tf_op jit(solution)/shard_map/ppermute | solution.py:706
  8.5 1.7 %copy-start.4 = (f32[16,64]{1,0:T(8,128)S(1)}, f32[16,64]{1,0:T(8,128)}, u32[]{:S(2)}) copy-start(f32[16,64]{1,0:T(8,128)} %gram_ref.1) | copy-start | bytes 12292

commit v10 on v8

--- a/solution.py
+++ b/solution.py
@@ -316,13 +316,14 @@
 
     if whole_rows:
         per = cols // columns
-        for r in range(row_count):
-            for c in range(col_count):
-                piece = got_ref[r * col_count + c, 1:2, :]
-                for t in range(per):
-                    at = (c * row_count + r) * per + t
-                    moved = pltpu.roll(piece, cols - t * columns, 1) if t else piece
-                    gram_ref[at : at + 1, :] = moved
+        pieces = got_ref[:, 1, :]
+        for c in range(col_count):
+            piece = jnp.concatenate(
+                [pieces[r * col_count + c : r * col_count + c + 1] for r in range(row_count)], axis=0
+            )
+            for t in range(per):
+                moved = pltpu.roll(piece, cols - t * columns, 1) if t else piece
+                gram_ref[pl.ds(c * row_count * per + t, row_count, stride=per), :] = moved
     else:
         gram_ref[:, :columns] = gram_in_ref[...]
     all_sums = jnp.sum(got_ref[...], axis=0)

time: 35.3 us -> 35.3 us (level)
  no operation moved by 1% of the time
where the time goes in v10:
time: 35.3 us; the launch traced here: 35.1 us
  blocking collectives  22.2 us (63%)
  starting transfers between devices  6.24 us (18%)
  Pallas kernels  4.12 us (12%)
  local copies, waits for them, and re-layouts  1.1 us (3%)
  waiting for transfers between devices  0.73 us (2%)
  between operations  0.71 us (2%)
    all_to_all x2, blocking collectives, share(): return lax.all_to_all(message, ('row', 'col'), 0, 0, tiled=True)  22.2 us
    ppermute x4, starting transfers between devices, swap(): return lax.ppermute(packet, ('row', 'col'), pairs)  6.24 us
    pallas_call x7, Pallas kernels, call(): pl.pallas_call(kernel, out_shape=[jax.ShapeDtypeStruct(s, F32) for s in o...  4.12 us
    unnamed x10, local copies, waits for them, and re-layouts  1.1 us
    ppermute x4, waiting for transfers between devices, swap(): return lax.ppermute(packet, ('row', 'col'), pairs)  0.73 us
  transfers between devices with their start and end apart: 4, of which 1 were waited for; matrix products, arithmetic and copies ran while one was open for 0% of the time, Pallas kernels for 4%

profile of v10, /device:TPU:0, one launch (start us, length us, event | category | flops | bytes accessed | tf_op | source)
XLA Modules:
  0.0 35.1 jit_solution(7143274839779414427)
XLA Ops:
  0.6 0.0 copy-start
  0.6 0.0 copy-start.1
  0.6 0.0 copy-start.2
  0.7 0.0 copy-start.3
  0.7 1.1 %copy-done = f32[64,3,8,128]{3,2,1,0:T(8,128)S(1)} copy-done((f32[64,3,8,128]{3,2,1,0:T(8,128)S(1)}, f32[64,3,8,128]{3,2,1,0:T(8,128)}, u32[]{:S(2)}) %copy-start) | copy-done | bytes 786456
  1.8 0.0 copy-done.1
  1.8 0.0 copy-done.2
  1.8 0.0 copy-done.3
  1.8 3.1 %collective-permute-start = (f32[200,128]{1,0:T(8,128)S(1)}, f32[200,128]{1,0:T(8,128)S(1)}, u32[]{:S(2)}, u32[]{:S(2)}) collective-permute-start(f32[200,128]{1,0:T(8,128)S(1)} %get-tuple-element.17), channel_id=1, source_target_pairs={{0,4},{1,5},{2,6},{3,7},{4,0},{5,1},{6,2},{7,3},{8,12},{9,13},{10,... | collective-permute-start | bytes 307208 | tf_op jit(solution)/shard_map/ppermute | solution.py:703
  4.9 0.0 collective-permute-start.1
  4.9 0.5 %shard_map.71 = (f32[32,128]{1,0:T(8,128)S(1)}, f32[32,128]{1,0:T(8,128)S(1)}) custom-call(f32[1536,128]{1,0:T(8,128)S(1)} %bitcast.6, f32[24,128]{1,0:T(8,128)S(1)} %bitcast.18, s32[24,128]{1,0:T(8,128)S(1)} %bitcast.12, f32[8,128]{1,0:T(8,128)S(1)} %copy-done.3), custom_call_target="tpu_custom_call" | custom-call | tf_op jit(solution)/shard_map/pallas_call | solution.py:677
  5.4 0.6 %collective-permute-start.2 = (f32[32,128]{1,0:T(8,128)S(1)}, f32[32,128]{1,0:T(8,128)S(1)}, u32[]{:S(2)}, u32[]{:S(2)}) collective-permute-start(f32[32,128]{1,0:T(8,128)S(1)} %get-tuple-element.19.owna_ref), channel_id=1, source_target_pairs={{0,1},{1,0},{2,3},{3,2},{4,5},{5,4},{6,7},{7,6},{8,9},{9,8},{10,11... | collective-permute-start | bytes 49160 | tf_op jit(solution)/shard_map/ppermute | solution.py:703
  5.9 2.6 %collective-permute-start.3 = (f32[32,128]{1,0:T(8,128)S(1)}, f32[32,128]{1,0:T(8,128)S(1)}, u32[]{:S(2)}, u32[]{:S(2)}) collective-permute-start(f32[32,128]{1,0:T(8,128)S(1)} %get-tuple-element.20.ownb_ref), channel_id=1, source_target_pairs={{0,4},{1,2},{2,1},{3,7},{4,0},{5,6},{6,5},{7,3},{8,12},{9,10},{10,... | collective-permute-start | bytes 49160 | tf_op jit(solution)/shard_map/ppermute | solution.py:703
  8.6 0.0 copy-start.4
  8.6 1.0 %shard_map.68 = (f32[64,128]{1,0:T(8,128)S(1)}, f32[8,128]{1,0:T(8,128)S(1)}) custom-call(f32[1536,128]{1,0:T(8,128)S(1)} %bitcast.7, f32[24,128]{1,0:T(8,128)S(1)} %bitcast.19, s32[24,128]{1,0:T(8,128)S(1)} %bitcast.13, f32[8,128]{1,0:T(8,128)S(1)} %copy-done.3), custom_call_target="tpu_custom_call" | custom-call | flops 100000000 | bytes 4096 | tf_op jit(solution)/shard_map/pallas_call | solution.py:677
  9.5 0.0 collective-permute-done.2.cola_ref.refs_6_
  9.5 0.7 %collective-permute-done.3.colb_ref.refs_7_ = f32[32,128]{1,0:T(8,128)S(1)} collective-permute-done((f32[32,128]{1,0:T(8,128)S(1)}, f32[32,128]{1,0:T(8,128)S(1)}, u32[]{:S(2)}, u32[]{:S(2)}) %collective-permute-start.3) | collective-permute-done | bytes 16416 | tf_op jit(solution)/shard_map/ppermute | solution.py:703
  10.3 0.0 collective-permute-done.rowa_ref.refs_4_
  10.3 0.0 collective-permute-done.1.rowb_ref.refs_5_
  10.3 0.0 copy-done.4
  10.3 0.6 %shard_map.72 = f32[32,4,128]{2,1,0:T(4,128)S(1)} custom-call(f32[64,128]{1,0:T(8,128)S(1)} %get-tuple-element.15.inner_ref, f32[8,128]{1,0:T(8,128)S(1)} %get-tuple-element.16.dots_ref, f32[1536,128]{1,0:T(8,128)S(1)} %bitcast.8, s32[24,128]{1,0:T(8,128)S(1)} %bitcast.14, f32[8,128]{1,0:T(8,128)S(1)} %copy-done.3, f32[16,64]{1,0:T(8,128)S(1)} %copy-done.4, ...), custom_call_target="tpu_custom_call" | custom-call | tf_op jit(solution)/shard_map/pallas_call | solution.py:677
  10.8 12.3 %all_to_all.10.got_ref = f32[32,4,128]{2,1,0:T(4,128)S(1)} all-to-all(f32[32,4,128]{2,1,0:T(4,128)S(1)} %shard_map.72), channel_id=1, replica_groups=mesh['row'=8,'col'=4] {'row','col'}, dimensions={0} | all-to-all | bytes 131072 | tf_op jit(solution)/shard_map/all_to_all | solution.py:688
  23.1 0.7 %shard_map.73 = (f32[32,8,128]{2,1,0:T(8,128)S(1)}, f32[72,128]{1,0:T(8,128)S(1)}, f32[40,128]{1,0:T(8,128)S(1)}, f32[8,128]{1,0:T(8,128)S(1)}, f32[64,128]{1,0:T(8,128)S(1)}) custom-call(f32[32,4,128]{2,1,0:T(4,128)S(1)} %all_to_all.10.got_ref, f32[1536,128]{1,0:T(8,128)S(1)} %bitcast.9, f32[24,128]{1,0:T(8,128)S(1)} %bitcast.20, s32[24,128]{1,0:T(8,128)S(1)} %bitcast.15, ...), custom_call_target="tpu_custom_call" | custom-call | tf_op jit(solution)/shard_map/pallas_call | solution.py:677
  23.8 9.9 %all_to_all.11.got_ref = f32[32,8,128]{2,1,0:T(8,128)S(1)} all-to-all(f32[32,8,128]{2,1,0:T(8,128)S(1)} %get-tuple-element.21), channel_id=1, replica_groups=mesh['row'=8,'col'=4] {'row','col'}, dimensions={0} | all-to-all | bytes 262144 | tf_op jit(solution)/shard_map/all_to_all | solution.py:688
  33.7 1.4 %shard_map.74 = (f32[24,128]{1,0:T(8,128)}, f32[24,128]{1,0:T(8,128)}) custom-call(f32[32,8,128]{2,1,0:T(8,128)S(1)} %all_to_all.11.got_ref, f32[1536,128]{1,0:T(8,128)S(1)} %bitcast.10, f32[24,128]{1,0:T(8,128)S(1)} %bitcast.21, s32[24,128]{1,0:T(8,128)S(1)} %bitcast.16, f32[200,128]{1,0:T(8,128)S(1)} %collective-permute-done.rowa_ref.refs_4_, ...), custom_call_target="tpu_custom_call" | custom-call | tf_op jit(solution)/shard_map/pallas_call | solution.py:677
  (2 shorter events, 0.0 us)
Async XLA Ops:
  0.6 1.1 %copy-start = (f32[64,3,8,128]{3,2,1,0:T(8,128)S(1)}, f32[64,3,8,128]{3,2,1,0:T(8,128)}, u32[]{:S(2)}) copy-start(f32[64,3,8,128]{3,2,1,0:T(8,128)} %param.8) | copy-start | bytes 2359300
  0.6 1.1 %copy-start.1 = (s32[3,8,128]{2,1,0:T(8,128)S(1)}, s32[3,8,128]{2,1,0:T(8,128)}, u32[]{:S(2)}) copy-start(s32[3,8,128]{2,1,0:T(8,128)} %param.7) | copy-start | bytes 36868
  0.6 1.1 %copy-start.2 = (f32[3,8,128]{2,1,0:T(8,128)S(1)}, f32[3,8,128]{2,1,0:T(8,128)}, u32[]{:S(2)}) copy-start(f32[3,8,128]{2,1,0:T(8,128)} %param.5) | copy-start | bytes 36868
  0.7 1.1 %copy-start.3 = (f32[8,128]{1,0:T(8,128)S(1)}, f32[8,128]{1,0:T(8,128)}, u32[]{:S(2)}) copy-start(f32[8,128]{1,0:T(8,128)} %refs_3_.1) | copy-start | bytes 12292
  1.8 8.5 %collective-permute-start = (f32[200,128]{1,0:T(8,128)S(1)}, f32[200,128]{1,0:T(8,128)S(1)}, u32[]{:S(2)}, u32[]{:S(2)}) collective-permute-start(f32[200,128]{1,0:T(8,128)S(1)} %get-tuple-element.17), channel_id=1, source_target_pairs={{0,4},{1,5},{2,6},{3,7},{4,0},{5,1},{6,2},{7,3},{8,12},{9,13},{10,... | collective-permute-start | bytes 307208 | tf_op jit(solution)/shard_map/ppermute | solution.py:703
  4.9 5.4 %collective-permute-start.1 = (f32[200,128]{1,0:T(8,128)S(1)}, f32[200,128]{1,0:T(8,128)S(1)}, u32[]{:S(2)}, u32[]{:S(2)}) collective-permute-start(f32[200,128]{1,0:T(8,128)S(1)} %get-tuple-element.18), channel_id=1, source_target_pairs={{0,1},{1,0},{2,3},{3,2},{4,8},{5,9},{6,10},{7,11},{8,4},{9,5},{10,... | collective-permute-start | bytes 307208 | tf_op jit(solution)/shard_map/ppermute | solution.py:703
  5.4 4.2 %collective-permute-start.2 = (f32[32,128]{1,0:T(8,128)S(1)}, f32[32,128]{1,0:T(8,128)S(1)}, u32[]{:S(2)}, u32[]{:S(2)}) collective-permute-start(f32[32,128]{1,0:T(8,128)S(1)} %get-tuple-element.19.owna_ref), channel_id=1, source_target_pairs={{0,1},{1,0},{2,3},{3,2},{4,5},{5,4},{6,7},{7,6},{8,9},{9,8},{10,11... | collective-permute-start | bytes 49160 | tf_op jit(solution)/shard_map/ppermute | solution.py:703
  5.9 4.3 %collective-permute-start.3 = (f32[32,128]{1,0:T(8,128)S(1)}, f32[32,128]{1,0:T(8,128)S(1)}, u32[]{:S(2)}, u32[]{:S(2)}) collective-permute-start(f32[32,128]{1,0:T(8,128)S(1)} %get-tuple-element.20.ownb_ref), channel_id=1, source_target_pairs={{0,4},{1,2},{2,1},{3,7},{4,0},{5,6},{6,5},{7,3},{8,12},{9,10},{10,... | collective-permute-start | bytes 49160 | tf_op jit(solution)/shard_map/ppermute | solution.py:703
  8.6 1.7 %copy-start.4 = (f32[16,64]{1,0:T(8,128)S(1)}, f32[16,64]{1,0:T(8,128)}, u32[]{:S(2)}) copy-start(f32[16,64]{1,0:T(8,128)} %gram_ref.1) | copy-start | bytes 12292
